TPU v7x, 128 devices: a whole 4x4x4 slice. The times are simulated.
128 devices in a mesh: expert: 16 (over y, z), width: 8 (over x, core).
Axes of the slice: x: 4, y: 4, z: 4, core: 2. Of those that a mesh axis runs over, the one named last changes fastest.
Arguments:
- tokens_in: bfloat16 [6144, 7168], P('expert', 'width'), may hold values from -6 to 6
- out_grad: bfloat16 [6144, 7168], P('expert', 'width'), may hold values from -0.08984375 to 0.08984375
- router_weight: bfloat16 [7168, 256], P('width'), may hold values from -0.0625 to 0.0625
- expert_out: bfloat16 [49152, 7168], P('expert', 'width'), may hold values from -6 to 6
- expert_ids: int32 [6144, 8], P('expert'), may hold values from 0 to 255, as said below
- slot_ids: int32 [6144, 8], P('expert'), may hold values from 0 to 191, as said below
Outputs:
- expert_grad: bfloat16 [49152, 7168], P('expert', 'width')
- router_grad: float32 [7168, 256], P('width', 'expert')
- input_grad: bfloat16 [6144, 7168], P('expert', 'width')
Inputs may be any that keep to these rules, and one draw needn't show every extreme that they name: `expert_ids`: expert e lies on device e // 16 of the expert axis; a token's 8 experts lie on 8 different devices. The tokens of each device choose experts of each device of the expert axis exactly 192 times. slot_ids[t, k] is the row, within the block of 192 rows that token t's device sends to the device of expert expert_ids[t, k], of that pair. The pairs of one block fill all its rows, grouped by expert in rising order and by token in rising order within an expert. The values of expert_ids and slot_ids fit in 8 bits each, and both may be sent packed several to a 32-bit word.
All inputs are finite; a program needn't handle non-finite values.
Results may differ from a plain program's by a relative error of at most 0.015.
Values may be sent and summed in bfloat16 or wider, within the bound.
No kernel may reach another device: no remote copies, remote signals or barrier semaphores. Data moves between devices by JAX's collectives and lax.ppermute only.
A program may use at most 128 MiB of HBM per device.

v0:
```python
import functools

import jax
import jax.numpy as jnp
from jax import lax
from jax.experimental import pallas as pl
from jax.experimental.pallas import tpu as pltpu
from jax.sharding import PartitionSpec as P


route_scale = 2.5
AXES = ("expert", "width")
f32, bf16, i32 = jnp.float32, jnp.bfloat16, jnp.int32
VMEM = pl.BlockSpec(memory_space=pltpu.VMEM)
SMEM = pl.BlockSpec(memory_space=pltpu.SMEM)
ANY = pl.BlockSpec(memory_space=pl.ANY)
HBM = pl.BlockSpec(memory_space=pltpu.HBM)


def params(mib):
    return pltpu.CompilerParams(vmem_limit_bytes=mib * 1024 * 1024)


def cost(flops, moved):
    return pl.CostEstimate(flops=flops, bytes_accessed=moved, transcendentals=0)


def line_shift(n_expert, n_width, shift, second):
    side = int(round(n_expert**0.5))
    pairs = []
    for e in range(n_expert):
        y, z = e // side, e % side
        for w in range(n_width):
            if (w % 2 == 0) != second:
                to = ((y + shift) % side) * side + z
            else:
                to = y * side + (z + shift) % side
            pairs.append((e * n_width + w, to * n_width + w))
    return pairs


def here():
    n_expert = lax.axis_size("expert")
    side = int(round(n_expert**0.5))
    me = lax.axis_index("expert")
    return side, lax.div(me, side), lax.rem(me, side), lax.rem(lax.axis_index("width"), 2)


def cell(place, along, across):
    side, y, z, core = place
    along, across = along % side, across % side
    first = lax.rem(y + along, side) * side + lax.rem(z + across, side)
    second = lax.rem(y + across, side) * side + lax.rem(z + along, side)
    return jnp.where(core == 0, first, second)


def in_hbm(x):
    return pltpu.with_memory_space_constraint(x, pltpu.HBM)


def pack_kernel(per_device, x_ref, ids_ref, slots_ref, out_ref):
    tok, width = x_ref.shape
    top = ids_ref.shape[0]
    out_ref[:tok, :] = x_ref[...]
    dev = (ids_ref[...] // per_device).astype(f32)
    slots = slots_ref[...].astype(f32)
    rest = jnp.zeros((top, width - 2 * tok), f32)
    out_ref[tok:, :] = jnp.concatenate([dev, slots, rest], axis=1).astype(bf16)


def compact_kernel(n_src, tok, cap, n_dest, *refs):
    x_refs, (stage, sem), out_refs = refs[:n_src], refs[-2:], refs[-2 - n_dest : -2]
    place = here()
    copies = []
    for d in list(range(1, n_dest)) + [0]:
        for j in range(n_src):
            info = x_refs[j][tok:, :].astype(f32)
            dev, slots = info[:, :tok], info[:, tok : 2 * tok]
            mine = dev == cell(place, 0, d).astype(f32)
            slot = jnp.sum(jnp.where(mine, slots + 1.0, 0.0), axis=0, keepdims=True)
            rows = lax.broadcasted_iota(i32, (cap, tok), 0)
            table = jnp.where(rows == slot.astype(i32) - 1, 1.0, 0.0).astype(bf16)
            got = jnp.dot(table, x_refs[j][:tok, :], preferred_element_type=f32)
            stage[d, j * cap : (j + 1) * cap, :] = got.astype(bf16)
        copies.append(pltpu.make_async_copy(stage.at[d], out_refs[d], sem.at[d]))
        copies[-1].start()
    for copy in copies:
        copy.wait()


def compact(xs, after, tok, cap, n_dest):
    n_src, width = len(xs), xs[0].shape[1]
    return pl.pallas_call(
        functools.partial(compact_kernel, n_src, tok, cap, n_dest),
        out_shape=[pltpu.HBM((n_src * cap, width), bf16)] * n_dest,
        in_specs=[VMEM] * n_src + [ANY] * len(after),
        out_specs=[HBM] * n_dest,
        scratch_shapes=[
            pltpu.VMEM((n_dest, n_src * cap, width), bf16),
            pltpu.SemaphoreType.DMA((n_dest,)),
        ],
        compiler_params=params(8),
        cost_estimate=cost(2 * n_src * n_dest * cap * tok * width, n_src * tok * width * 6),
        name="compact",
    )(*xs, *map(in_hbm, after))


def picked_kernel(ids_ref, tok_ref, w_ref, after_ref, out_ref):
    logits = lax.dot_general(
        w_ref[...], tok_ref[...], (((0,), (1,)), ((), ())), preferred_element_type=f32
    )
    experts = lax.broadcasted_iota(i32, logits.shape, 0)
    rows = []
    for k in range(ids_ref.shape[0]):
        hit = experts == ids_ref[k : k + 1, :]
        rows.append(jnp.sum(jnp.where(hit, logits, 0.0), axis=0, keepdims=True))
    picked = jnp.concatenate(rows, axis=0)
    for w in range(out_ref.shape[0]):
        out_ref[w] = picked


def front(ids, tokens_in, router_weight, after, n_width):
    (top, tok), width, experts = ids.shape, tokens_in.shape[1], router_weight.shape[1]
    return pl.pallas_call(
        picked_kernel,
        out_shape=jax.ShapeDtypeStruct((n_width, top, tok), f32),
        in_specs=[VMEM] * 3 + [HBM],
        out_specs=VMEM,
        compiler_params=params(4),
        cost_estimate=cost(2 * tok * width * experts, 2 * tok * width),
        name="picked",
    )(ids, tokens_in, router_weight, in_hbm(after))


def gates_of(parts):
    logits = jnp.sum(parts, axis=0)
    picked = 1.0 / (1.0 + jnp.exp(-logits))
    totals = jnp.sum(picked, axis=0, keepdims=True)
    return picked, totals


def gate_kernel(per_device, parts_ref, ids_ref, slots_ref, out_ref):
    picked, totals = gates_of(parts_ref[...])
    gates = (route_scale * picked / totals).astype(bf16).astype(f32)
    top, tok = ids_ref.shape
    n_expert, cap = out_ref.shape
    dev, slots = ids_ref[...] // per_device, slots_ref[...]
    dev_rows = lax.broadcasted_iota(i32, (n_expert, tok), 0)
    slot_rows = lax.broadcasted_iota(i32, (cap, tok), 0)
    total = jnp.zeros((n_expert, cap), f32)
    for k in range(top):
        left = jnp.where(dev_rows == dev[k : k + 1], gates[k : k + 1], 0.0).astype(bf16)
        right = jnp.where(slot_rows == slots[k : k + 1], 1.0, 0.0).astype(bf16)
        total = total + lax.dot_general(left, right, (((1,), (1,)), ((), ())), preferred_element_type=f32)
    out_ref[...] = total


def row_dots(chunk, other):
    total = None
    for at in range(0, chunk.shape[1], 128):
        term = chunk[:, at : at + 128].astype(f32) * other[:, at : at + 128].astype(f32)
        total = term if total is None else total + term
    return jnp.sum(total.T, axis=0, keepdims=True)


def fetch(eo_ref, stage, sem, cells, cap):
    copies = []
    for at, src in enumerate(cells):
        rows = eo_ref.at[pl.ds(pl.multiple_of(src * cap, cap), cap), :]
        copies.append(pltpu.make_async_copy(rows, stage.at[at], sem.at[at]))
        copies[-1].start()
    return copies


def fetch_chunks(chunk_refs, stage, sem, cap, first=0):
    copies, at = [], first
    for chunk_ref in chunk_refs:
        for j in range(chunk_ref.shape[0] // cap):
            copies.append(pltpu.make_async_copy(chunk_ref.at[pl.ds(j * cap, cap), :], stage.at[at], sem.at[at]))
            copies[-1].start()
            at += 1
    return copies


def cells_of(batch, side, place):
    return [cell(place, -s, -d) for d in range(side) for s in batch]


def dots_kernel(batch, side, cap, next_batch, eo_ref, *refs):
    chunk_refs = refs[:side]
    out_refs, (held, stage, sem, next_sem) = refs[side:-4], refs[-4:]
    place = here()
    rows = fetch_chunks(chunk_refs, held, sem.at[0], cap)
    others = fetch(eo_ref, stage, sem.at[1], cells_of(batch, side, place), cap)
    ahead = fetch(eo_ref, out_refs[1], next_sem, cells_of(next_batch, side, place), cap) if next_batch else []
    for at in range(len(rows)):
        rows[at].wait()
        others[at].wait()
        out_refs[0][at : at + 1, :] = row_dots(held.at[at], stage.at[at])
    for copy in ahead:
        copy.wait()


def row_dots_call(batch, next_batch, eo, chunks, cap):
    n, width, side = len(batch) * len(chunks), chunks[0].shape[1], len(chunks)
    n_next = len(next_batch) * side
    outs = [jax.ShapeDtypeStruct((n, cap), f32)]
    if n_next:
        outs.append(pltpu.VMEM((n_next, cap, width), bf16))
    return pl.pallas_call(
        functools.partial(dots_kernel, batch, side, cap, next_batch),
        out_shape=outs,
        in_specs=[HBM] * (1 + side),
        out_specs=[VMEM] * len(outs),
        scratch_shapes=[
            pltpu.VMEM((n, cap, width), bf16),
            pltpu.VMEM((n, cap, width), bf16),
            pltpu.SemaphoreType.DMA((2, n)),
            pltpu.SemaphoreType.DMA((max(n_next, 1),)),
        ],
        compiler_params=params(8),
        cost_estimate=cost(2 * n * cap * width, 4 * n * cap * width),
        name="dots",
    )(in_hbm(eo), *map(in_hbm, chunks))


def last_dots_kernel(n_width, batches, cap, side, gate_ref, eo_ref, *refs):
    chunk_refs, early_refs, (out_ref, held, sem) = refs[:side], refs[side:-3], refs[-3:]
    n_expert = gate_ref.shape[0]
    place = here()
    copies = fetch_chunks(chunk_refs, held, sem, cap)
    for e in range(n_expert):
        for w in range(n_width):
            out_ref[2 * (e * n_width + w) + 1] = gate_ref[e : e + 1, :]

    def put(src, row):
        base = src * (2 * n_width)
        for w in range(n_width):
            out_ref[base + 2 * w] = row

    for batch, early in zip(batches[:-1], early_refs):
        for at, src in enumerate(cells_of(batch, side, place)):
            put(src, early[at : at + 1, :])
    for at, src in enumerate(cells_of(batches[-1], side, place)):
        copies[at].wait()
        put(src, row_dots(held.at[at], eo_ref.at[at]))


def tail_kernel(n_expert, n_width, per_device, got_ref, parts_ref, ids_ref, slots_ref, tok_ref, lg_ref, router_ref):
    top, tok = ids_ref.shape
    rows = []
    for e in range(n_expert):
        row = got_ref[2 * e * n_width]
        for w in range(1, n_width):
            row = row + got_ref[2 * (e * n_width + w)]
        rows.append(row)
    dots = jnp.concatenate(rows, axis=0)
    cap = dots.shape[1]
    high = dots.astype(bf16)
    low = (dots - high.astype(f32)).astype(bf16)
    both = jnp.concatenate([high, low], axis=0)
    ids, slots = ids_ref[...], slots_ref[...]
    dev = ids // per_device
    slot_rows = lax.broadcasted_iota(i32, (cap, tok), 0)
    dev_rows = lax.broadcasted_iota(i32, (n_expert, tok), 0)
    out = []
    for k in range(top):
        table = jnp.where(slot_rows == slots[k : k + 1], 1.0, 0.0).astype(bf16)
        found = jnp.dot(both, table, preferred_element_type=f32)
        found = found[:n_expert] + found[n_expert:]
        out.append(jnp.sum(jnp.where(dev_rows == dev[k : k + 1], found, 0.0), axis=0, keepdims=True))
    gate_grads = jnp.concatenate(out, axis=0)
    picked, totals = gates_of(parts_ref[...])
    weighted = jnp.sum(gate_grads * picked, axis=0, keepdims=True) / totals
    local = route_scale / totals * (gate_grads - weighted) * picked * (1.0 - picked)
    experts = lax.broadcasted_iota(i32, (lg_ref.shape[0], tok), 0)
    grads = jnp.zeros(lg_ref.shape, f32)
    for k in range(top):
        grads = grads + jnp.where(experts == ids[k : k + 1], local[k : k + 1], 0.0)
    grads = grads.astype(bf16)
    lg_ref[...] = grads
    router_ref[...] = jnp.dot(grads, tok_ref[...], preferred_element_type=f32).astype(bf16)


def scale_kernel(n_width, batches, cap, side, got_ref, lg_ref, w_ref, *refs):
    chunk_refs, (out_ref, input_ref, held, stage, in_sem, sem) = refs[:-6], refs[-6:]
    place = here()
    rows = fetch_chunks(chunk_refs, held, in_sem, cap)
    copies = []
    cells = sum([cells_of(batch, side, place) for batch in batches], [])
    for at, src in enumerate(cells):
        gate = jnp.broadcast_to(got_ref[src * (2 * n_width) + 1], (128, cap)).T
        rows[at].wait()
        for lane in range(0, held.shape[2], 128):
            part = held[at, :, lane : lane + 128].astype(f32)
            stage[at, :, lane : lane + 128] = (part * gate).astype(bf16)
        to = out_ref.at[pl.ds(pl.multiple_of(src * cap, cap), cap), :]
        copies.append(pltpu.make_async_copy(stage.at[at], to, sem.at[at]))
        copies[-1].start()
    input_ref[...] = lax.dot_general(
        lg_ref[...], w_ref[...], (((0,), (1,)), ((), ())), preferred_element_type=f32
    ).astype(bf16)
    for copy in copies:
        copy.wait()


def body(tokens_in, out_grad, router_weight, expert_out, expert_ids, slot_ids):
    n_expert, n_width = lax.axis_size("expert"), lax.axis_size("width")
    side = int(round(n_expert**0.5))
    tok, width = out_grad.shape
    top = expert_ids.shape[1]
    experts = router_weight.shape[1]
    per_device = experts // n_expert
    cap = tok * top // n_expert

    def send(x, shift, second):
        return lax.ppermute(x, AXES, line_shift(n_expert, n_width, shift, second))

    ids, slots = expert_ids.T, slot_ids.T
    packed = pl.pallas_call(
        functools.partial(pack_kernel, per_device),
        out_shape=jax.ShapeDtypeStruct((tok + top, width), bf16),
        in_specs=[VMEM] * 3,
        out_specs=VMEM,
        compiler_params=params(4),
        cost_estimate=cost(0, 4 * tok * width),
        name="pack",
    )(out_grad, ids, slots)
    batches = [[0], [1, side - 1]] + [[s] for s in range(2, side - 1)]
    xs = {0: packed}
    for batch in batches[1:]:
        for s in batch:
            xs[s] = send(packed, s, False)

    landed, after = [], []
    for batch in batches:
        chunks = compact([xs[s] for s in batch], after, tok, cap, side)
        after = [chunks[0]]
        group = [chunks[0]]
        for d in range(1, side):
            group.append(send(chunks[d], d, True))
        landed.append(group)

    sent_parts = front(ids, tokens_in, router_weight, after[0], n_width)
    parts = lax.all_to_all(sent_parts, "width", 0, 0, tiled=True)
    gates = pl.pallas_call(
        functools.partial(gate_kernel, per_device),
        out_shape=jax.ShapeDtypeStruct((n_expert, cap), f32),
        in_specs=[VMEM] * 3,
        out_specs=VMEM,
        compiler_params=params(4),
        cost_estimate=cost(2 * top * n_expert * cap * tok, 4 * n_width * top * tok),
        name="gates",
    )(parts, ids, slots)

    early = []
    for b, batch in enumerate(batches[:-1]):
        next_batch = batches[-1] if b == len(batches) - 2 else []
        outs = row_dots_call(batch, next_batch, expert_out, landed[b], cap)
        early.append(outs[0])
    sent = pl.pallas_call(
        functools.partial(last_dots_kernel, n_width, batches, cap, side),
        out_shape=jax.ShapeDtypeStruct((2 * n_expert * n_width, 1, cap), f32),
        in_specs=[VMEM] * 2 + [HBM] * side + [VMEM] * len(early),
        out_specs=VMEM,
        scratch_shapes=[
            pltpu.VMEM((side, cap, width), bf16),
            pltpu.SemaphoreType.DMA((side,)),
        ],
        compiler_params=params(6),
        cost_estimate=cost(2 * side * cap * width, 4 * side * cap * width),
        name="last_dots",
    )(gates, outs[1], *map(in_hbm, landed[-1]), *early)
    got = lax.all_to_all(sent, AXES, 0, 0, tiled=True)

    logit_grads, router_part = pl.pallas_call(
        functools.partial(tail_kernel, n_expert, n_width, per_device),
        out_shape=[
            jax.ShapeDtypeStruct((experts, tok), bf16),
            jax.ShapeDtypeStruct((experts, width), bf16),
        ],
        in_specs=[VMEM] * 5,
        out_specs=[VMEM] * 2,
        compiler_params=params(8),
        cost_estimate=cost(2 * tok * width * experts, 2 * tok * width),
        name="tail",
    )(got, parts, ids, slots, tokens_in)
    blocks = lax.all_to_all(router_part.reshape(n_expert, per_device, width), "expert", 0, 0, tiled=True)
    flat = sum(landed, [])
    expert_grad, input_grad = pl.pallas_call(
        functools.partial(scale_kernel, n_width, batches, cap, side),
        out_shape=[
            jax.ShapeDtypeStruct(expert_out.shape, bf16),
            jax.ShapeDtypeStruct((tok, width), bf16),
        ],
        in_specs=[VMEM] * 3 + [HBM] * len(flat),
        out_specs=[HBM, VMEM],
        scratch_shapes=[
            pltpu.VMEM((n_expert, cap, width), bf16),
            pltpu.VMEM((n_expert, cap, width), bf16),
            pltpu.SemaphoreType.DMA((n_expert,)),
            pltpu.SemaphoreType.DMA((n_expert,)),
        ],
        compiler_params=params(16),
        cost_estimate=cost(2 * tok * width * experts, 4 * n_expert * cap * width),
        name="scale",
    )(got, logit_grads, router_weight, *map(in_hbm, flat))
    router_grad = jnp.sum(blocks.astype(f32), axis=0).T
    return (expert_grad, router_grad, input_grad)


def solution(mesh):
    return jax.shard_map(
        body,
        mesh=mesh,
        in_specs=(
            P("expert", "width"),
            P("expert", "width"),
            P("width", None),
            P("expert", "width"),
            P("expert", None),
            P("expert", None),
        ),
        out_specs=(P("expert", "width"), P("width", "expert"), P("expert", "width")),
        check_vma=False,
    )
```

profile of v0, /device:TPU:0, one launch (start us, length us, event | category | flops | bytes accessed | tf_op | source)
XLA Modules:
  0.0 120.3 jit_solution(5736027454196899907)
XLA Ops:
  3.3 3.2 %collective-permute-start.2 = (bf16[392,896]{1,0:T(8,128)(2,1)S(1)}, bf16[392,896]{1,0:T(8,128)(2,1)S(1)}, u32[]{:S(2)}, u32[]{:S(2)}) collective-permute-start(bf16[392,896]{1,0:T(8,128)(2,1)S(1)} %pack.1.refs_0_), channel_id=1, source_target_pairs={{0,96},{1,25},{2,98},{3,27},{4,100},{5,29},{6,102},{7,31},{8,104},... | collective-permute-start | bytes 2107400 | tf_op jit(solution)/shard_map/ppermute | solution.py:317
  6.5 2.2 %collective-permute-start = (bf16[392,896]{1,0:T(8,128)(2,1)S(1)}, bf16[392,896]{1,0:T(8,128)(2,1)S(1)}, u32[]{:S(2)}, u32[]{:S(2)}) collective-permute-start(bf16[392,896]{1,0:T(8,128)(2,1)S(1)} %pack.1.refs_0_), channel_id=1, source_target_pairs={{0,64},{1,17},{2,66},{3,19},{4,68},{5,21},{6,70},{7,23},{8,72},{9,... | collective-permute-start | bytes 2107400 | tf_op jit(solution)/shard_map/ppermute | solution.py:317
  10.5 2.0 %collective-permute-start.9 = (bf16[192,896]{1,0:T(8,128)(2,1)}, bf16[192,896]{1,0:T(8,128)(2,1)S(1)}, u32[]{:S(2)}, u32[]{:S(2)}) collective-permute-start(bf16[192,896]{1,0:T(8,128)(2,1)} %get-tuple-element.31), channel_id=1, source_target_pairs={{0,8},{1,33},{2,10},{3,35},{4,12},{5,37},{6,14},{7,39},{8,16},{9,4... | collective-permute-start | bytes 1032200 | tf_op jit(solution)/shard_map/ppermute | solution.py:317
  12.4 10.2 %collective-permute-done.2.refs_1_ = bf16[392,896]{1,0:T(8,128)(2,1)S(1)} collective-permute-done((bf16[392,896]{1,0:T(8,128)(2,1)S(1)}, bf16[392,896]{1,0:T(8,128)(2,1)S(1)}, u32[]{:S(2)}, u32[]{:S(2)}) %collective-permute-start.2) | collective-permute-done | bytes 702496 | tf_op jit(solution)/shard_map/ppermute | solution.py:317
  22.7 7.4 %collective-permute-done.1.refs_0_ = bf16[392,896]{1,0:T(8,128)(2,1)S(1)} collective-permute-done((bf16[392,896]{1,0:T(8,128)(2,1)S(1)}, bf16[392,896]{1,0:T(8,128)(2,1)S(1)}, u32[]{:S(2)}, u32[]{:S(2)}) %collective-permute-start.1) | collective-permute-done | bytes 702496 | tf_op jit(solution)/shard_map/ppermute | solution.py:317
  30.0 2.6 %compact.4 = (bf16[384,896]{1,0:T(8,128)(2,1)}, bf16[384,896]{1,0:T(8,128)(2,1)}, bf16[384,896]{1,0:T(8,128)(2,1)}, bf16[384,896]{1,0:T(8,128)(2,1)}) custom-call(bf16[392,896]{1,0:T(8,128)(2,1)S(1)} %collective-permute-done.1.refs_0_, bf16[392,896]{1,0:T(8,128)(2,1)S(1)} %collective-permute-done.2.refs_1_, bf16[192,896]{1,0:T(8,128)(2,1)} %get-tuple-element.21.refs_2_.refs_0_), custom_call_target="tpu_custom_call" | custom-call | flops 1056964608 | bytes 4128768 | tf_op jit(solution)/shard_map/compact/pallas_call | solution.py:93
  32.7 1.9 %collective-permute-start.3 = (bf16[384,896]{1,0:T(8,128)(2,1)}, bf16[384,896]{1,0:T(8,128)(2,1)S(1)}, u32[]{:S(2)}, u32[]{:S(2)}) collective-permute-start(bf16[384,896]{1,0:T(8,128)(2,1)} %get-tuple-element.24), channel_id=1, source_target_pairs={{0,8},{1,33},{2,10},{3,35},{4,12},{5,37},{6,14},{7,39},{8,16},{9,4... | collective-permute-start | bytes 2064392 | tf_op jit(solution)/shard_map/ppermute | solution.py:317
  34.6 3.6 %collective-permute-start.4 = (bf16[384,896]{1,0:T(8,128)(2,1)}, bf16[384,896]{1,0:T(8,128)(2,1)S(1)}, u32[]{:S(2)}, u32[]{:S(2)}) collective-permute-start(bf16[384,896]{1,0:T(8,128)(2,1)} %get-tuple-element.25), channel_id=1, source_target_pairs={{0,16},{1,65},{2,18},{3,67},{4,20},{5,69},{6,22},{7,71},{8,24},{9,... | collective-permute-start | bytes 2064392 | tf_op jit(solution)/shard_map/ppermute | solution.py:317
  38.2 2.4 %collective-permute-start.5 = (bf16[384,896]{1,0:T(8,128)(2,1)}, bf16[384,896]{1,0:T(8,128)(2,1)}, u32[]{:S(2)}, u32[]{:S(2)}) collective-permute-start(bf16[384,896]{1,0:T(8,128)(2,1)} %get-tuple-element.26), channel_id=1, source_target_pairs={{0,24},{1,97},{2,26},{3,99},{4,28},{5,101},{6,30},{7,103},{8,0},{9... | collective-permute-start | bytes 2064392 | tf_op jit(solution)/shard_map/ppermute | solution.py:317
  40.6 2.3 %collective-permute-start.11 = (bf16[192,896]{1,0:T(8,128)(2,1)}, bf16[192,896]{1,0:T(8,128)(2,1)S(1)}, u32[]{:S(2)}, u32[]{:S(2)}) collective-permute-start(bf16[192,896]{1,0:T(8,128)(2,1)} %get-tuple-element.33), channel_id=1, source_target_pairs={{0,24},{1,97},{2,26},{3,99},{4,28},{5,101},{6,30},{7,103},{8,0},{9... | collective-permute-start | bytes 1032200 | tf_op jit(solution)/shard_map/ppermute | solution.py:317
  43.0 1.7 %compact.5 = (bf16[192,896]{1,0:T(8,128)(2,1)}, bf16[192,896]{1,0:T(8,128)(2,1)}, bf16[192,896]{1,0:T(8,128)(2,1)}, bf16[192,896]{1,0:T(8,128)(2,1)}) custom-call(bf16[392,896]{1,0:T(8,128)(2,1)S(1)} %collective-permute-done.refs_0_, bf16[384,896]{1,0:T(8,128)(2,1)} %get-tuple-element.22.refs_1_.refs_0_.refs_4_), custom_call_target="tpu_custom_call" | custom-call | flops 528482304 | bytes 2064384 | tf_op jit(solution)/shard_map/compact/pallas_call | solution.py:93
  44.7 13.7 %collective-permute-done.10.refs_2_ = bf16[192,896]{1,0:T(8,128)(2,1)S(1)} collective-permute-done((bf16[192,896]{1,0:T(8,128)(2,1)}, bf16[192,896]{1,0:T(8,128)(2,1)S(1)}, u32[]{:S(2)}, u32[]{:S(2)}) %collective-permute-start.10) | collective-permute-done | bytes 344096 | tf_op jit(solution)/shard_map/ppermute | solution.py:317
  58.4 3.4 %collective-permute-start.6 = (bf16[192,896]{1,0:T(8,128)(2,1)}, bf16[192,896]{1,0:T(8,128)(2,1)S(1)}, u32[]{:S(2)}, u32[]{:S(2)}) collective-permute-start(bf16[192,896]{1,0:T(8,128)(2,1)} %get-tuple-element.28), channel_id=1, source_target_pairs={{0,8},{1,33},{2,10},{3,35},{4,12},{5,37},{6,14},{7,39},{8,16},{9,4... | collective-permute-start | bytes 1032200 | tf_op jit(solution)/shard_map/ppermute | solution.py:317
  61.9 4.1 %collective-permute-start.7 = (bf16[192,896]{1,0:T(8,128)(2,1)}, bf16[192,896]{1,0:T(8,128)(2,1)}, u32[]{:S(2)}, u32[]{:S(2)}) collective-permute-start(bf16[192,896]{1,0:T(8,128)(2,1)} %get-tuple-element.29), channel_id=1, source_target_pairs={{0,16},{1,65},{2,18},{3,67},{4,20},{5,69},{6,22},{7,71},{8,24},{9,... | collective-permute-start | bytes 1032200 | tf_op jit(solution)/shard_map/ppermute | solution.py:317
  68.2 4.3 %all-to-all-start = ((f32[8,8,384]{2,1,0:T(8,128)}), f32[8,8,384]{2,1,0:T(8,128)S(1)}, u32[]{:S(2)}, u32[]{:S(2)}) async-start(f32[8,8,384]{2,1,0:T(8,128)} %picked.1), calls=%async_computation | async-start | bytes 196608 | tf_op jit(solution)/shard_map/all_to_all | solution.py:345
  72.5 2.2 %dots.3.refs_4_ = f32[4,192]{1,0:T(4,128)S(1)} custom-call(bf16[3072,896]{1,0:T(8,128)(2,1)} %eo_ref.3, bf16[192,896]{1,0:T(8,128)(2,1)} %get-tuple-element.21.refs_2_.refs_0_, bf16[192,896]{1,0:T(8,128)(2,1)} %copy-done.10, bf16[192,896]{1,0:T(8,128)(2,1)} %copy-done.11, bf16[192,896]{1,0:T(8,128)(2,1)} %copy-done.12), custom_call_target="tpu_custom_call" | custom-call | flops 1376256 | bytes 2752512 | tf_op jit(solution)/shard_map/dots/pallas_call | solution.py:210
  74.6 3.6 %all-to-all-done.parts_ref = f32[8,8,384]{2,1,0:T(8,128)S(1)} async-done(((f32[8,8,384]{2,1,0:T(8,128)}), f32[8,8,384]{2,1,0:T(8,128)S(1)}, u32[]{:S(2)}, u32[]{:S(2)}) %all-to-all-start) | async-done | bytes 98336 | tf_op jit(solution)/shard_map/all_to_all | solution.py:345
  79.6 3.4 %dots.2 = (f32[8,192]{1,0:T(8,128)S(1)}, bf16[4,192,896]{2,1,0:T(8,128)(2,1)S(1)}) custom-call(bf16[3072,896]{1,0:T(8,128)(2,1)} %eo_ref.3, bf16[384,896]{1,0:T(8,128)(2,1)} %get-tuple-element.22.refs_1_.refs_0_.refs_4_, bf16[384,896]{1,0:T(8,128)(2,1)} %copy-done.7, bf16[384,896]{1,0:T(8,128)(2,1)} %copy-done.8, ...), custom_call_target="tpu_custom_call" | custom-call | flops 2752512 | bytes 5505024 | tf_op jit(solution)/shard_map/dots/pallas_call | solution.py:210
  83.7 1.8 %last_dots.1 = f32[256,1,192]{2,1,0:T(1,128)S(1)} custom-call(f32[16,192]{1,0:T(8,128)S(1)} %gates.1.gate_ref, bf16[4,192,896]{2,1,0:T(8,128)(2,1)S(1)} %get-tuple-element.27.eo_ref, bf16[192,896]{1,0:T(8,128)(2,1)} %get-tuple-element.23.after_ref.refs_0_.refs_8_, bf16[192,896]{1,0:T(8,128)(2,1)} %copy-done.9, ...), custom_call_target="tpu_custom_call" | custom-call | flops 1376256 | bytes 2752512 | tf_op jit(solution)/shard_map/last_dots/pallas_call | solution.py:361
  85.5 17.7 %all_to_all.15.got_ref = f32[256,1,192]{2,1,0:T(1,128)S(1)} all-to-all(f32[256,1,192]{2,1,0:T(1,128)S(1)} %last_dots.1), channel_id=1, replica_groups=mesh['expert'=16,'width'=8] {'expert','width'}, dimensions={0} | all-to-all | bytes 393216 | tf_op jit(solution)/shard_map/all_to_all | solution.py:374
  103.2 1.9 %tail.1 = (bf16[256,384]{1,0:T(8,128)(2,1)S(1)}, bf16[256,896]{1,0:T(8,128)(2,1)}) custom-call(f32[256,1,192]{2,1,0:T(1,128)S(1)} %all_to_all.15.got_ref, f32[8,8,384]{2,1,0:T(8,128)S(1)} %all-to-all-done.parts_ref, s32[8,384]{1,0:T(8,128)S(1)} %bitcast.7, s32[8,384]{1,0:T(8,128)S(1)} %bitcast.10, bf16[384,896]{1,0:T(8,128)(2,1)S(1)} %copy-done), custom_call_target="tpu_custom_call" | custom-call | flops 176160768 | bytes 688128 | tf_op jit(solution)/shard_map/tail/pallas_call | solution.py:376
  105.2 3.6 %all-to-all-start.2 = ((bf16[16,16,896]{2,1,0:T(8,128)(2,1)}), bf16[16,16,896]{2,1,0:T(8,128)(2,1)S(1)}, u32[]{:S(2)}, u32[]{:S(2)}) async-start(bf16[16,16,896]{2,1,0:T(8,128)(2,1)} %bitcast.2), calls=%async_computation.2 | async-start | bytes 917504 | tf_op jit(solution)/shard_map/all_to_all | solution.py:388
  108.8 6.3 %scale.1 = (bf16[3072,896]{1,0:T(8,128)(2,1)}, bf16[384,896]{1,0:T(8,128)(2,1)}) custom-call(f32[256,1,192]{2,1,0:T(1,128)S(1)} %all_to_all.15.got_ref, bf16[256,384]{1,0:T(8,128)(2,1)S(1)} %get-tuple-element.35.lg_ref, bf16[896,256]{1,0:T(8,128)(2,1)S(1)} %copy-done.1, bf16[192,896]{1,0:T(8,128)(2,1)} %get-tuple-element.21.refs_2_.refs_0_, ...), custom_call_target="tpu_custom_call" | custom-call | flops 176160768 | bytes 11010048 | tf_op jit(solution)/shard_map/scale/pallas_call | solution.py:390
  115.0 4.5 %all-to-all-done.2 = bf16[16,16,896]{2,1,0:T(8,128)(2,1)S(1)} async-done(((bf16[16,16,896]{2,1,0:T(8,128)(2,1)}), bf16[16,16,896]{2,1,0:T(8,128)(2,1)S(1)}, u32[]{:S(2)}, u32[]{:S(2)}) %all-to-all-start.2) | async-done | bytes 458784 | tf_op jit(solution)/shard_map/all_to_all | solution.py:388
  (43 shorter events, 9.4 us)
Async XLA Ops:
  0.6 66.0 %copy-start.1 = (bf16[896,256]{1,0:T(8,128)(2,1)S(1)}, bf16[896,256]{1,0:T(8,128)(2,1)}, u32[]{:S(2)}) copy-start(bf16[896,256]{1,0:T(8,128)(2,1)} %w_ref.3) | copy-start | bytes 1376260
  0.6 66.0 %copy-start = (bf16[384,896]{1,0:T(8,128)(2,1)S(1)}, bf16[384,896]{1,0:T(8,128)(2,1)}, u32[]{:S(2)}) copy-start(bf16[384,896]{1,0:T(8,128)(2,1)} %tok_ref.3) | copy-start | bytes 2064388
  0.7 1.2 copy-start.2
  3.3 63.3 %copy-start.4 = (s32[384,8]{0,1:T(8,128)S(1)}, s32[384,8]{0,1:T(8,128)}, u32[]{:S(2)}) copy-start(s32[384,8]{0,1:T(8,128)} %param.10) | copy-start | bytes 36868
  3.3 19.3 %collective-permute-start.2 = (bf16[392,896]{1,0:T(8,128)(2,1)S(1)}, bf16[392,896]{1,0:T(8,128)(2,1)S(1)}, u32[]{:S(2)}, u32[]{:S(2)}) collective-permute-start(bf16[392,896]{1,0:T(8,128)(2,1)S(1)} %pack.1.refs_0_), channel_id=1, source_target_pairs={{0,96},{1,25},{2,98},{3,27},{4,100},{5,29},{6,102},{7,31},{8,104},... | collective-permute-start | bytes 2107400 | tf_op jit(solution)/shard_map/ppermute | solution.py:317
  6.5 23.5 %collective-permute-start.1 = (bf16[392,896]{1,0:T(8,128)(2,1)S(1)}, bf16[392,896]{1,0:T(8,128)(2,1)S(1)}, u32[]{:S(2)}, u32[]{:S(2)}) collective-permute-start(bf16[392,896]{1,0:T(8,128)(2,1)S(1)} %pack.1.refs_0_), channel_id=1, source_target_pairs={{0,32},{1,9},{2,34},{3,11},{4,36},{5,13},{6,38},{7,15},{8,40},{9,1... | collective-permute-start | bytes 2107400 | tf_op jit(solution)/shard_map/ppermute | solution.py:317
  6.5 34.1 %collective-permute-start = (bf16[392,896]{1,0:T(8,128)(2,1)S(1)}, bf16[392,896]{1,0:T(8,128)(2,1)S(1)}, u32[]{:S(2)}, u32[]{:S(2)}) collective-permute-start(bf16[392,896]{1,0:T(8,128)(2,1)S(1)} %pack.1.refs_0_), channel_id=1, source_target_pairs={{0,64},{1,17},{2,66},{3,19},{4,68},{5,21},{6,70},{7,23},{8,72},{9,... | collective-permute-start | bytes 2107400 | tf_op jit(solution)/shard_map/ppermute | solution.py:317
  10.5 30.2 %collective-permute-start.9 = (bf16[192,896]{1,0:T(8,128)(2,1)}, bf16[192,896]{1,0:T(8,128)(2,1)S(1)}, u32[]{:S(2)}, u32[]{:S(2)}) collective-permute-start(bf16[192,896]{1,0:T(8,128)(2,1)} %get-tuple-element.31), channel_id=1, source_target_pairs={{0,8},{1,33},{2,10},{3,35},{4,12},{5,37},{6,14},{7,39},{8,16},{9,4... | collective-permute-start | bytes 1032200 | tf_op jit(solution)/shard_map/ppermute | solution.py:317
  32.7 45.6 %copy-start.6 = (s32[384,8]{0,1:T(8,128)S(1)}, s32[384,8]{0,1:T(8,128)}, u32[]{:S(2)}) copy-start(s32[384,8]{0,1:T(8,128)} %param.11) | copy-start | bytes 36868
  32.7 33.4 %collective-permute-start.3 = (bf16[384,896]{1,0:T(8,128)(2,1)}, bf16[384,896]{1,0:T(8,128)(2,1)S(1)}, u32[]{:S(2)}, u32[]{:S(2)}) collective-permute-start(bf16[384,896]{1,0:T(8,128)(2,1)} %get-tuple-element.24), channel_id=1, source_target_pairs={{0,8},{1,33},{2,10},{3,35},{4,12},{5,37},{6,14},{7,39},{8,16},{9,4... | collective-permute-start | bytes 2064392 | tf_op jit(solution)/shard_map/ppermute | solution.py:317
  34.6 44.2 %collective-permute-start.4 = (bf16[384,896]{1,0:T(8,128)(2,1)}, bf16[384,896]{1,0:T(8,128)(2,1)S(1)}, u32[]{:S(2)}, u32[]{:S(2)}) collective-permute-start(bf16[384,896]{1,0:T(8,128)(2,1)} %get-tuple-element.25), channel_id=1, source_target_pairs={{0,16},{1,65},{2,18},{3,67},{4,20},{5,69},{6,22},{7,71},{8,24},{9,... | collective-permute-start | bytes 2064392 | tf_op jit(solution)/shard_map/ppermute | solution.py:317
  38.2 40.5 %collective-permute-start.5 = (bf16[384,896]{1,0:T(8,128)(2,1)}, bf16[384,896]{1,0:T(8,128)(2,1)}, u32[]{:S(2)}, u32[]{:S(2)}) collective-permute-start(bf16[384,896]{1,0:T(8,128)(2,1)} %get-tuple-element.26), channel_id=1, source_target_pairs={{0,24},{1,97},{2,26},{3,99},{4,28},{5,101},{6,30},{7,103},{8,0},{9... | collective-permute-start | bytes 2064392 | tf_op jit(solution)/shard_map/ppermute | solution.py:317
  40.6 25.4 %copy-start.10 = (bf16[192,896]{1,0:T(8,128)(2,1)}, bf16[192,896]{1,0:T(8,128)(2,1)S(1)}, u32[]{:S(2)}) copy-start(bf16[192,896]{1,0:T(8,128)(2,1)S(1)} %collective-permute-done.9.refs_1_) | copy-start | bytes 1032196
  40.6 17.8 %collective-permute-start.10 = (bf16[192,896]{1,0:T(8,128)(2,1)}, bf16[192,896]{1,0:T(8,128)(2,1)S(1)}, u32[]{:S(2)}, u32[]{:S(2)}) collective-permute-start(bf16[192,896]{1,0:T(8,128)(2,1)} %get-tuple-element.32), channel_id=1, source_target_pairs={{0,16},{1,65},{2,18},{3,67},{4,20},{5,69},{6,22},{7,71},{8,24},{9,... | collective-permute-start | bytes 1032200 | tf_op jit(solution)/shard_map/ppermute | solution.py:317
  40.6 21.3 %collective-permute-start.11 = (bf16[192,896]{1,0:T(8,128)(2,1)}, bf16[192,896]{1,0:T(8,128)(2,1)S(1)}, u32[]{:S(2)}, u32[]{:S(2)}) collective-permute-start(bf16[192,896]{1,0:T(8,128)(2,1)} %get-tuple-element.33), channel_id=1, source_target_pairs={{0,24},{1,97},{2,26},{3,99},{4,28},{5,101},{6,30},{7,103},{8,0},{9... | collective-permute-start | bytes 1032200 | tf_op jit(solution)/shard_map/ppermute | solution.py:317
  58.4 7.6 %copy-start.11 = (bf16[192,896]{1,0:T(8,128)(2,1)}, bf16[192,896]{1,0:T(8,128)(2,1)S(1)}, u32[]{:S(2)}) copy-start(bf16[192,896]{1,0:T(8,128)(2,1)S(1)} %collective-permute-done.10.refs_2_) | copy-start | bytes 1032196
  58.4 24.6 %collective-permute-start.6 = (bf16[192,896]{1,0:T(8,128)(2,1)}, bf16[192,896]{1,0:T(8,128)(2,1)S(1)}, u32[]{:S(2)}, u32[]{:S(2)}) collective-permute-start(bf16[192,896]{1,0:T(8,128)(2,1)} %get-tuple-element.28), channel_id=1, source_target_pairs={{0,8},{1,33},{2,10},{3,35},{4,12},{5,37},{6,14},{7,39},{8,16},{9,4... | collective-permute-start | bytes 1032200 | tf_op jit(solution)/shard_map/ppermute | solution.py:317
  61.9 4.7 %copy-start.12 = (bf16[192,896]{1,0:T(8,128)(2,1)}, bf16[192,896]{1,0:T(8,128)(2,1)S(1)}, u32[]{:S(2)}) copy-start(bf16[192,896]{1,0:T(8,128)(2,1)S(1)} %collective-permute-done.11.refs_3_) | copy-start | bytes 1032196
  61.9 21.1 %collective-permute-start.7 = (bf16[192,896]{1,0:T(8,128)(2,1)}, bf16[192,896]{1,0:T(8,128)(2,1)}, u32[]{:S(2)}, u32[]{:S(2)}) collective-permute-start(bf16[192,896]{1,0:T(8,128)(2,1)} %get-tuple-element.29), channel_id=1, source_target_pairs={{0,16},{1,65},{2,18},{3,67},{4,20},{5,69},{6,22},{7,71},{8,24},{9,... | collective-permute-start | bytes 1032200 | tf_op jit(solution)/shard_map/ppermute | solution.py:317
  66.0 12.8 %copy-start.7 = (bf16[384,896]{1,0:T(8,128)(2,1)}, bf16[384,896]{1,0:T(8,128)(2,1)S(1)}, u32[]{:S(2)}) copy-start(bf16[384,896]{1,0:T(8,128)(2,1)S(1)} %collective-permute-done.3.refs_1_.refs_5_) | copy-start | bytes 2064388
  66.0 17.0 %collective-permute-start.8 = (bf16[192,896]{1,0:T(8,128)(2,1)}, bf16[192,896]{1,0:T(8,128)(2,1)}, u32[]{:S(2)}, u32[]{:S(2)}) collective-permute-start(bf16[192,896]{1,0:T(8,128)(2,1)} %get-tuple-element.30), channel_id=1, source_target_pairs={{0,24},{1,97},{2,26},{3,99},{4,28},{5,101},{6,30},{7,103},{8,0},{9... | collective-permute-start | bytes 1032200 | tf_op jit(solution)/shard_map/ppermute | solution.py:317
  68.2 10.1 %all-to-all-start = ((f32[8,8,384]{2,1,0:T(8,128)}), f32[8,8,384]{2,1,0:T(8,128)S(1)}, u32[]{:S(2)}, u32[]{:S(2)}) async-start(f32[8,8,384]{2,1,0:T(8,128)} %picked.1), calls=%async_computation | async-start | bytes 196608 | tf_op jit(solution)/shard_map/all_to_all | solution.py:345
  78.8 0.9 copy-start.8
  105.2 14.4 %all-to-all-start.2 = ((bf16[16,16,896]{2,1,0:T(8,128)(2,1)}), bf16[16,16,896]{2,1,0:T(8,128)(2,1)S(1)}, u32[]{:S(2)}, u32[]{:S(2)}) async-start(bf16[16,16,896]{2,1,0:T(8,128)(2,1)} %bitcast.2), calls=%async_computation.2 | async-start | bytes 917504 | tf_op jit(solution)/shard_map/all_to_all | solution.py:388
  (3 other events, 2.1 us)
where the time goes:
time: 121 us; the launch traced here: 120 us
  waiting for transfers between devices  39.6 us (33%)
  starting transfers between devices  33.5 us (28%)
  Pallas kernels  23.7 us (20%)
  blocking collectives  17.7 us (15%)
  local copies, waits for them, and re-layouts  4.16 us (3%)
    ppermute x12, waiting for transfers between devices, send(): return lax.ppermute(x, AXES, line_shift(n_expert, n_width, shift, second))  31.5 us
    ppermute x12, starting transfers between devices, send(): return lax.ppermute(x, AXES, line_shift(n_expert, n_width, shift, second))  25.7 us
    all_to_all x1, blocking collectives, body(): got = lax.all_to_all(sent, AXES, 0, 0, tiled=True)  17.7 us
    pallas_call x1, Pallas kernels, body(): pl.pallas_call(functools.partial(scale_kernel, n_width, batches, cap, sid...  6.26 us
    pallas_call x3, Pallas kernels, compact(): pl.pallas_call(functools.partial(compact_kernel, n_src, tok, cap, n_dest)...  6.06 us
    pallas_call x2, Pallas kernels, row_dots_call(): pl.pallas_call(functools.partial(dots_kernel, batch, side, cap, next_batc...  5.51 us
    all_to_all x1, waiting for transfers between devices, body(): lax.all_to_all(router_part.reshape(n_expert, per_device, width), 'expert'...  4.55 us
    all_to_all x1, starting transfers between devices, body(): parts = lax.all_to_all(sent_parts, 'width', 0, 0, tiled=True)  4.3 us
  transfers between devices with their start and end apart: 14, of which 6 were waited for; matrix products, arithmetic and copies ran while one was open for 0% of the time, Pallas kernels for 17%

commit v1 on v0

--- a/solution.py
+++ b/solution.py
@@ -58,29 +58,54 @@
     return pltpu.with_memory_space_constraint(x, pltpu.HBM)
 
 
-def pack_kernel(per_device, x_ref, ids_ref, slots_ref, out_ref):
+def pack_kernel(per_device, x_ref, ids_ref, slots_ref, out_ref, held_ids, held_slots, sem):
     tok, width = x_ref.shape
     top = ids_ref.shape[0]
-    out_ref[:tok, :] = x_ref[...]
-    dev = (ids_ref[...] // per_device).astype(f32)
-    slots = slots_ref[...].astype(f32)
+    copies = [
+        pltpu.make_async_copy(ids_ref, held_ids, sem.at[0]),
+        pltpu.make_async_copy(slots_ref, held_slots, sem.at[1]),
+        pltpu.make_async_copy(x_ref, out_ref.at[pl.ds(0, tok), :], sem.at[2]),
+    ]
+    for copy in copies:
+        copy.start()
+    copies[0].wait()
+    copies[1].wait()
+    dev = (held_ids[...] // per_device).astype(f32)
+    slots = held_slots[...].astype(f32)
     rest = jnp.zeros((top, width - 2 * tok), f32)
     out_ref[tok:, :] = jnp.concatenate([dev, slots, rest], axis=1).astype(bf16)
-
-
-def compact_kernel(n_src, tok, cap, n_dest, *refs):
-    x_refs, (stage, sem), out_refs = refs[:n_src], refs[-2:], refs[-2 - n_dest : -2]
+    copies[2].wait()
+
+
+def compact_kernel(parts, tok, cap, n_dest, halves, *refs):
+    n_in, n_half = sum(parts), len(halves)
+    x_refs, (stage, sem) = refs[:n_in], refs[-2:]
+    out_refs, half_refs = refs[-2 - n_half - n_dest : -2 - n_half], refs[-2 - n_half : -2]
     place = here()
     copies = []
+    for at, (j, rows, first) in enumerate(halves):
+        part = x_refs[j].at[pl.ds(first, rows), :]
+        copies.append(pltpu.make_async_copy(part, half_refs[at], sem.at[n_dest + at]))
+        copies[-1].start()
     for d in list(range(1, n_dest)) + [0]:
-        for j in range(n_src):
-            info = x_refs[j][tok:, :].astype(f32)
+        at = 0
+        for j, count in enumerate(parts):
+            mine_refs = x_refs[at : at + count]
+            at += count
+            last = mine_refs[-1].shape[0]
+            top = sum(ref.shape[0] for ref in mine_refs) - tok
+            info = mine_refs[-1][last - top :, :].astype(f32)
             dev, slots = info[:, :tok], info[:, tok : 2 * tok]
             mine = dev == cell(place, 0, d).astype(f32)
-            slot = jnp.sum(jnp.where(mine, slots + 1.0, 0.0), axis=0, keepdims=True)
-            rows = lax.broadcasted_iota(i32, (cap, tok), 0)
-            table = jnp.where(rows == slot.astype(i32) - 1, 1.0, 0.0).astype(bf16)
-            got = jnp.dot(table, x_refs[j][:tok, :], preferred_element_type=f32)
+            slot = jnp.sum(jnp.where(mine, slots + 1.0, 0.0), axis=0, keepdims=True).astype(i32) - 1
+            got, first = None, 0
+            for ref in mine_refs:
+                rows = min(ref.shape[0], tok - first)
+                want = lax.broadcasted_iota(i32, (cap, rows), 0)
+                table = jnp.where(want == slot[:, first : first + rows], 1.0, 0.0).astype(bf16)
+                term = jnp.dot(table, ref[:rows, :], preferred_element_type=f32)
+                got = term if got is None else got + term
+                first += rows
             stage[d, j * cap : (j + 1) * cap, :] = got.astype(bf16)
         copies.append(pltpu.make_async_copy(stage.at[d], out_refs[d], sem.at[d]))
         copies[-1].start()
@@ -88,48 +113,66 @@
         copy.wait()
 
 
-def compact(xs, after, tok, cap, n_dest):
-    n_src, width = len(xs), xs[0].shape[1]
+def compact(sources, after, tok, cap, n_dest, halves=()):
+    n_src, width = len(sources), sources[0][0].shape[1]
+    xs = sum(sources, [])
+    outs = [pltpu.HBM((n_src * cap, width), bf16)] * n_dest
+    outs += [pltpu.HBM((rows, width), bf16) for _, rows, _ in halves]
     return pl.pallas_call(
-        functools.partial(compact_kernel, n_src, tok, cap, n_dest),
-        out_shape=[pltpu.HBM((n_src * cap, width), bf16)] * n_dest,
-        in_specs=[VMEM] * n_src + [ANY] * len(after),
-        out_specs=[HBM] * n_dest,
+        functools.partial(compact_kernel, [len(x) for x in sources], tok, cap, n_dest, halves),
+        out_shape=outs,
+        in_specs=[VMEM] * len(xs) + [HBM] * len(after),
+        out_specs=[HBM] * len(outs),
         scratch_shapes=[
             pltpu.VMEM((n_dest, n_src * cap, width), bf16),
-            pltpu.SemaphoreType.DMA((n_dest,)),
-        ],
-        compiler_params=params(8),
+            pltpu.SemaphoreType.DMA((n_dest + len(halves),)),
+        ],
+        compiler_params=params(12),
         cost_estimate=cost(2 * n_src * n_dest * cap * tok * width, n_src * tok * width * 6),
         name="compact",
     )(*xs, *map(in_hbm, after))
 
 
-def picked_kernel(ids_ref, tok_ref, w_ref, after_ref, out_ref):
+def picked_kernel(ids_ref, tok_ref, w_ref, out_ref, ids, toks, weights, sem):
+    copies = [
+        pltpu.make_async_copy(w_ref, weights, sem.at[0]),
+        pltpu.make_async_copy(tok_ref, toks, sem.at[1]),
+        pltpu.make_async_copy(ids_ref, ids, sem.at[2]),
+    ]
+    for copy in copies:
+        copy.start()
+    for copy in copies:
+        copy.wait()
     logits = lax.dot_general(
-        w_ref[...], tok_ref[...], (((0,), (1,)), ((), ())), preferred_element_type=f32
+        weights[...], toks[...], (((0,), (1,)), ((), ())), preferred_element_type=f32
     )
     experts = lax.broadcasted_iota(i32, logits.shape, 0)
     rows = []
-    for k in range(ids_ref.shape[0]):
-        hit = experts == ids_ref[k : k + 1, :]
+    for k in range(ids.shape[0]):
+        hit = experts == ids[k : k + 1, :]
         rows.append(jnp.sum(jnp.where(hit, logits, 0.0), axis=0, keepdims=True))
     picked = jnp.concatenate(rows, axis=0)
     for w in range(out_ref.shape[0]):
         out_ref[w] = picked
 
 
-def front(ids, tokens_in, router_weight, after, n_width):
+def front(ids, tokens_in, router_weight, n_width):
     (top, tok), width, experts = ids.shape, tokens_in.shape[1], router_weight.shape[1]
     return pl.pallas_call(
         picked_kernel,
         out_shape=jax.ShapeDtypeStruct((n_width, top, tok), f32),
-        in_specs=[VMEM] * 3 + [HBM],
+        in_specs=[HBM] * 3,
         out_specs=VMEM,
-        compiler_params=params(4),
+        scratch_shapes=[
+            pltpu.VMEM((top, tok), i32),
+            pltpu.VMEM((tok, width), bf16),
+            pltpu.VMEM((width, experts), bf16),
+            pltpu.SemaphoreType.DMA((3,)),
+        ],
+        compiler_params=params(6),
         cost_estimate=cost(2 * tok * width * experts, 2 * tok * width),
         name="picked",
-    )(ids, tokens_in, router_weight, in_hbm(after))
+    )(in_hbm(ids), in_hbm(tokens_in), in_hbm(router_weight))
 
 
 def gates_of(parts):
@@ -218,7 +261,7 @@
             pltpu.SemaphoreType.DMA((2, n)),
             pltpu.SemaphoreType.DMA((max(n_next, 1),)),
         ],
-        compiler_params=params(8),
+        compiler_params=params(12),
         cost_estimate=cost(2 * n * cap * width, 4 * n * cap * width),
         name="dots",
     )(in_hbm(eo), *map(in_hbm, chunks))
@@ -320,29 +363,34 @@
     packed = pl.pallas_call(
         functools.partial(pack_kernel, per_device),
         out_shape=jax.ShapeDtypeStruct((tok + top, width), bf16),
-        in_specs=[VMEM] * 3,
+        in_specs=[HBM] * 3,
         out_specs=VMEM,
+        scratch_shapes=[
+            pltpu.VMEM((top, tok), i32),
+            pltpu.VMEM((top, tok), i32),
+            pltpu.SemaphoreType.DMA((3,)),
+        ],
         compiler_params=params(4),
         cost_estimate=cost(0, 4 * tok * width),
         name="pack",
-    )(out_grad, ids, slots)
-    batches = [[0], [1, side - 1]] + [[s] for s in range(2, side - 1)]
+    )(in_hbm(out_grad), in_hbm(ids), in_hbm(slots))
     xs = {0: packed}
-    for batch in batches[1:]:
-        for s in batch:
-            xs[s] = send(packed, s, False)
+    for s in [1, side - 1] + list(range(2, side - 1)):
+        xs[s] = send(packed, s, False)
+    batches = [[0, 1, side - 1], list(range(2, side - 1))]
+
+    sent_parts = front(ids, tokens_in, router_weight, n_width)
+    parts = lax.all_to_all(sent_parts, "width", 0, 0, tiled=True)
 
     landed, after = [], []
     for batch in batches:
-        chunks = compact([xs[s] for s in batch], after, tok, cap, side)
+        chunks = compact([[xs[s]] for s in batch], after, tok, cap, side)
         after = [chunks[0]]
         group = [chunks[0]]
         for d in range(1, side):
             group.append(send(chunks[d], d, True))
         landed.append(group)
 
-    sent_parts = front(ids, tokens_in, router_weight, after[0], n_width)
-    parts = lax.all_to_all(sent_parts, "width", 0, 0, tiled=True)
     gates = pl.pallas_call(
         functools.partial(gate_kernel, per_device),
         out_shape=jax.ShapeDtypeStruct((n_expert, cap), f32),

time: 121 us -> 110 us (0.909)
  starting transfers between devices: 33.5 us -> 19.7 us
  blocking collectives: 17.7 us -> 29.7 us
  waiting for transfers between devices: 39.6 us -> 32.4 us
  local copies, waits for them, and re-layouts: 4.16 us -> 2.91 us
    all_to_all x0 -> x1, blocking collectives: none -> 9.88 us  [body(): parts = lax.all_to_all(sent_parts, 'width', 0, 0, tiled=True)]
    ppermute x12 -> x9, starting transfers between devices: 25.7 us -> 16.1 us  [send(): return lax.ppermute(x, AXES, line_shift(n_expert, n_width, shift, second))]
    all_to_all x1 -> x0, starting transfers between devices: 4.3 us -> none  [body(): parts = lax.all_to_all(sent_parts, 'width', 0, 0, tiled=True)]
    all_to_all x1 -> x0, waiting for transfers between devices: 3.63 us -> none  [body(): parts = lax.all_to_all(sent_parts, 'width', 0, 0, tiled=True)]
    ppermute x12 -> x9, waiting for transfers between devices: 31.5 us -> 27.9 us  [send(): return lax.ppermute(x, AXES, line_shift(n_expert, n_width, shift, second))]
    all_to_all x1, blocking collectives: 17.7 us -> 19.9 us  [body(): got = lax.all_to_all(sent, AXES, 0, 0, tiled=True)]
    unnamed x26 -> x20, local copies, waits for them, and re-layouts: 4.16 us -> 2.91 us
    pallas_call x2 -> x1, Pallas kernels: 5.51 us -> 4.52 us  [row_dots_call(): pl.pallas_call(functools.partial(dots_kernel, batch, side, cap, next_batc...]
  transfers between devices with their start and end apart: 14 -> 10, of which waited for: 6 -> 4; matrix products, arithmetic and copies ran while one was open for 0% -> 0% of each run, Pallas kernels for 17% -> 14%
where the time goes in v1:
time: 110 us
  waiting for transfers between devices  32.4 us (29%)
  blocking collectives  29.7 us (27%)
  Pallas kernels  23.6 us (21%)
  starting transfers between devices  19.7 us (18%)
  local copies, waits for them, and re-layouts  2.91 us (3%)
    ppermute x9, waiting for transfers between devices, send(): return lax.ppermute(x, AXES, line_shift(n_expert, n_width, shift, second))  27.9 us
    all_to_all x1, blocking collectives, body(): got = lax.all_to_all(sent, AXES, 0, 0, tiled=True)  19.9 us
    ppermute x9, starting transfers between devices, send(): return lax.ppermute(x, AXES, line_shift(n_expert, n_width, shift, second))  16.1 us
    all_to_all x1, blocking collectives, body(): parts = lax.all_to_all(sent_parts, 'width', 0, 0, tiled=True)  9.88 us
    pallas_call x1, Pallas kernels, body(): pl.pallas_call(functools.partial(scale_kernel, n_width, batches, cap, sid...  6.25 us
    pallas_call x2, Pallas kernels, compact(): pl.pallas_call(functools.partial(compact_kernel, [len(x) for x in sources...  5.29 us
    all_to_all x1, waiting for transfers between devices, body(): lax.all_to_all(router_part.reshape(n_expert, per_device, width), 'expert'...  4.55 us
    pallas_call x1, Pallas kernels, row_dots_call(): pl.pallas_call(functools.partial(dots_kernel, batch, side, cap, next_batc...  4.52 us
  transfers between devices with their start and end apart: 10, of which 4 were waited for; matrix products, arithmetic and copies ran while one was open for 0% of the time, Pallas kernels for 14%

profile of v1, /device:TPU:0, one launch (start us, length us, event | category | flops | bytes accessed | tf_op | source)
XLA Modules:
  0.0 109.8 jit_solution(8600891239561420675)
XLA Ops:
  0.7 1.2 %pack.1.refs_0_ = bf16[392,896]{1,0:T(8,128)(2,1)S(1)} custom-call(bf16[384,896]{1,0:T(8,128)(2,1)} %x_ref.1, s32[8,384]{1,0:T(8,128)} %bitcast.4, s32[8,384]{1,0:T(8,128)} %bitcast.8), custom_call_target="tpu_custom_call" | custom-call | bytes 1376256 | tf_op jit(solution)/shard_map/pack/pallas_call | solution.py:363
  1.8 3.2 %collective-permute-start.1 = (bf16[392,896]{1,0:T(8,128)(2,1)S(1)}, bf16[392,896]{1,0:T(8,128)(2,1)S(1)}, u32[]{:S(2)}, u32[]{:S(2)}) collective-permute-start(bf16[392,896]{1,0:T(8,128)(2,1)S(1)} %pack.1.refs_0_), channel_id=1, source_target_pairs={{0,96},{1,25},{2,98},{3,27},{4,100},{5,29},{6,102},{7,31},{8,104},... | collective-permute-start | bytes 2107400 | tf_op jit(solution)/shard_map/ppermute | solution.py:360
  5.0 8.6 %collective-permute-done.1.refs_2_ = bf16[392,896]{1,0:T(8,128)(2,1)S(1)} collective-permute-done((bf16[392,896]{1,0:T(8,128)(2,1)S(1)}, bf16[392,896]{1,0:T(8,128)(2,1)S(1)}, u32[]{:S(2)}, u32[]{:S(2)}) %collective-permute-start.1) | collective-permute-done | bytes 702496 | tf_op jit(solution)/shard_map/ppermute | solution.py:360
  13.6 3.7 %collective-permute-done.refs_1_ = bf16[392,896]{1,0:T(8,128)(2,1)S(1)} collective-permute-done((bf16[392,896]{1,0:T(8,128)(2,1)S(1)}, bf16[392,896]{1,0:T(8,128)(2,1)S(1)}, u32[]{:S(2)}, u32[]{:S(2)}) %collective-permute-start) | collective-permute-done | bytes 702496 | tf_op jit(solution)/shard_map/ppermute | solution.py:360
  17.3 3.6 %compact.2 = (bf16[576,896]{1,0:T(8,128)(2,1)}, bf16[576,896]{1,0:T(8,128)(2,1)}, bf16[576,896]{1,0:T(8,128)(2,1)}, bf16[576,896]{1,0:T(8,128)(2,1)}) custom-call(bf16[392,896]{1,0:T(8,128)(2,1)S(1)} %pack.1.refs_0_, bf16[392,896]{1,0:T(8,128)(2,1)S(1)} %collective-permute-done.refs_1_, bf16[392,896]{1,0:T(8,128)(2,1)S(1)} %collective-permute-done.1.refs_2_), custom_call_target="tpu_custom_call" | custom-call | flops 1585446912 | bytes 6193152 | tf_op jit(solution)/shard_map/compact/pallas_call | solution.py:121
  20.9 2.0 %collective-permute-start.2 = (bf16[576,896]{1,0:T(8,128)(2,1)}, bf16[576,896]{1,0:T(8,128)(2,1)S(1)}, u32[]{:S(2)}, u32[]{:S(2)}) collective-permute-start(bf16[576,896]{1,0:T(8,128)(2,1)} %get-tuple-element.18), channel_id=1, source_target_pairs={{0,8},{1,33},{2,10},{3,35},{4,12},{5,37},{6,14},{7,39},{8,16},{9,4... | collective-permute-start | bytes 3096584 | tf_op jit(solution)/shard_map/ppermute | solution.py:360
  22.9 3.6 %collective-permute-start.3 = (bf16[576,896]{1,0:T(8,128)(2,1)}, bf16[576,896]{1,0:T(8,128)(2,1)S(1)}, u32[]{:S(2)}, u32[]{:S(2)}) collective-permute-start(bf16[576,896]{1,0:T(8,128)(2,1)} %get-tuple-element.19), channel_id=1, source_target_pairs={{0,16},{1,65},{2,18},{3,67},{4,20},{5,69},{6,22},{7,71},{8,24},{9,... | collective-permute-start | bytes 3096584 | tf_op jit(solution)/shard_map/ppermute | solution.py:360
  26.5 1.0 collective-permute-start.4
  27.5 15.5 %collective-permute-done.5.refs_0_ = bf16[392,896]{1,0:T(8,128)(2,1)S(1)} collective-permute-done((bf16[392,896]{1,0:T(8,128)(2,1)S(1)}, bf16[392,896]{1,0:T(8,128)(2,1)S(1)}, u32[]{:S(2)}, u32[]{:S(2)}) %collective-permute-start.5) | collective-permute-done | bytes 702496 | tf_op jit(solution)/shard_map/ppermute | solution.py:360
  43.0 1.7 %compact.3 = (bf16[192,896]{1,0:T(8,128)(2,1)}, bf16[192,896]{1,0:T(8,128)(2,1)}, bf16[192,896]{1,0:T(8,128)(2,1)}, bf16[192,896]{1,0:T(8,128)(2,1)}) custom-call(bf16[392,896]{1,0:T(8,128)(2,1)S(1)} %collective-permute-done.5.refs_0_, bf16[576,896]{1,0:T(8,128)(2,1)} %get-tuple-element.17.refs_0_.refs_1_), custom_call_target="tpu_custom_call" | custom-call | flops 528482304 | bytes 2064384 | tf_op jit(solution)/shard_map/compact/pallas_call | solution.py:121
  44.7 2.1 %collective-permute-start.6 = (bf16[192,896]{1,0:T(8,128)(2,1)}, bf16[192,896]{1,0:T(8,128)(2,1)S(1)}, u32[]{:S(2)}, u32[]{:S(2)}) collective-permute-start(bf16[192,896]{1,0:T(8,128)(2,1)} %get-tuple-element.23), channel_id=1, source_target_pairs={{0,8},{1,33},{2,10},{3,35},{4,12},{5,37},{6,14},{7,39},{8,16},{9,4... | collective-permute-start | bytes 1032200 | tf_op jit(solution)/shard_map/ppermute | solution.py:360
  46.8 1.8 %collective-permute-start.7 = (bf16[192,896]{1,0:T(8,128)(2,1)}, bf16[192,896]{1,0:T(8,128)(2,1)S(1)}, u32[]{:S(2)}, u32[]{:S(2)}) collective-permute-start(bf16[192,896]{1,0:T(8,128)(2,1)} %get-tuple-element.24), channel_id=1, source_target_pairs={{0,16},{1,65},{2,18},{3,67},{4,20},{5,69},{6,22},{7,71},{8,24},{9,... | collective-permute-start | bytes 1032200 | tf_op jit(solution)/shard_map/ppermute | solution.py:360
  48.6 2.5 %collective-permute-start.8 = (bf16[192,896]{1,0:T(8,128)(2,1)}, bf16[192,896]{1,0:T(8,128)(2,1)S(1)}, u32[]{:S(2)}, u32[]{:S(2)}) collective-permute-start(bf16[192,896]{1,0:T(8,128)(2,1)} %get-tuple-element.25), channel_id=1, source_target_pairs={{0,24},{1,97},{2,26},{3,99},{4,28},{5,101},{6,30},{7,103},{8,0},{9... | collective-permute-start | bytes 1032200 | tf_op jit(solution)/shard_map/ppermute | solution.py:360
  51.1 2.2 %picked.1 = f32[8,8,384]{2,1,0:T(8,128)S(1)} custom-call(s32[8,384]{1,0:T(8,128)} %bitcast.5, bf16[384,896]{1,0:T(8,128)(2,1)} %tok_ref.3, bf16[896,256]{1,0:T(8,128)(2,1)} %w_ref.3), custom_call_target="tpu_custom_call" | custom-call | flops 176160768 | bytes 688128 | tf_op jit(solution)/shard_map/picked/pallas_call | solution.py:161
  53.3 9.9 %all_to_all.15.parts_ref = f32[8,8,384]{2,1,0:T(8,128)S(1)} all-to-all(f32[8,8,384]{2,1,0:T(8,128)S(1)} %picked.1), channel_id=1, replica_groups=mesh['expert'=16,'width'=8] {'width'}, dimensions={0} | all-to-all | bytes 196608 | tf_op jit(solution)/shard_map/all_to_all | solution.py:383
  63.8 0.9 copy-done.5
  64.7 1.0 copy-done.6
  65.7 4.5 %dots.1 = (f32[12,192]{1,0:T(8,128)S(1)}, bf16[4,192,896]{2,1,0:T(8,128)(2,1)S(1)}) custom-call(bf16[3072,896]{1,0:T(8,128)(2,1)} %eo_ref.1, bf16[576,896]{1,0:T(8,128)(2,1)} %get-tuple-element.17.refs_0_.refs_1_, bf16[576,896]{1,0:T(8,128)(2,1)} %copy-done.4, bf16[576,896]{1,0:T(8,128)(2,1)} %copy-done.5, bf16[576,896]{1,0:T(8,128)(2,1)} %copy-done.6), custom_call_target="tpu_custom_call" | custom-call | flops 4128768 | bytes 8257536 | tf_op jit(solution)/shard_map/dots/pallas_call | solution.py:253
  71.2 1.8 %last_dots.1 = f32[256,1,192]{2,1,0:T(1,128)S(1)} custom-call(f32[16,192]{1,0:T(8,128)S(1)} %gates.1.gate_ref, bf16[4,192,896]{2,1,0:T(8,128)(2,1)S(1)} %get-tuple-element.21.eo_ref, bf16[192,896]{1,0:T(8,128)(2,1)} %get-tuple-element.22.refs_0_.refs_4_, bf16[192,896]{1,0:T(8,128)(2,1)} %copy-done.7, bf16[192,896]{1,0:T(8,128)(2,1)} %copy-done.8, ...), custom_call_target="tpu_custom_call" | custom-call | flops 1376256 | bytes 2752512 | tf_op jit(solution)/shard_map/last_dots/pallas_call | solution.py:409
  73.0 19.9 %all_to_all.16.got_ref = f32[256,1,192]{2,1,0:T(1,128)S(1)} all-to-all(f32[256,1,192]{2,1,0:T(1,128)S(1)} %last_dots.1), channel_id=1, replica_groups=mesh['expert'=16,'width'=8] {'expert','width'}, dimensions={0} | all-to-all | bytes 393216 | tf_op jit(solution)/shard_map/all_to_all | solution.py:422
  92.9 1.9 %tail.1 = (bf16[256,384]{1,0:T(8,128)(2,1)S(1)}, bf16[256,896]{1,0:T(8,128)(2,1)}) custom-call(f32[256,1,192]{2,1,0:T(1,128)S(1)} %all_to_all.16.got_ref, f32[8,8,384]{2,1,0:T(8,128)S(1)} %all_to_all.15.parts_ref, s32[8,384]{1,0:T(8,128)S(1)} %bitcast.7, s32[8,384]{1,0:T(8,128)S(1)} %bitcast.10, bf16[384,896]{1,0:T(8,128)(2,1)S(1)} %copy-done), custom_call_target="tpu_custom_call" | custom-call | flops 176160768 | bytes 688128 | tf_op jit(solution)/shard_map/tail/pallas_call | solution.py:424
  94.8 3.6 %all-to-all-start.2 = ((bf16[16,16,896]{2,1,0:T(8,128)(2,1)}), bf16[16,16,896]{2,1,0:T(8,128)(2,1)S(1)}, u32[]{:S(2)}, u32[]{:S(2)}) async-start(bf16[16,16,896]{2,1,0:T(8,128)(2,1)} %bitcast.2), calls=%async_computation.2 | async-start | bytes 917504 | tf_op jit(solution)/shard_map/all_to_all | solution.py:436
  98.4 6.3 %scale.1 = (bf16[3072,896]{1,0:T(8,128)(2,1)}, bf16[384,896]{1,0:T(8,128)(2,1)}) custom-call(f32[256,1,192]{2,1,0:T(1,128)S(1)} %all_to_all.16.got_ref, bf16[256,384]{1,0:T(8,128)(2,1)S(1)} %get-tuple-element.27.lg_ref, bf16[896,256]{1,0:T(8,128)(2,1)S(1)} %copy-done.1, bf16[576,896]{1,0:T(8,128)(2,1)} %get-tuple-element.17.refs_0_.refs_1_, ...), custom_call_target="tpu_custom_call" | custom-call | flops 176160768 | bytes 11010048 | tf_op jit(solution)/shard_map/scale/pallas_call | solution.py:438
  104.6 4.6 %all-to-all-done.2 = bf16[16,16,896]{2,1,0:T(8,128)(2,1)S(1)} async-done(((bf16[16,16,896]{2,1,0:T(8,128)(2,1)}), bf16[16,16,896]{2,1,0:T(8,128)(2,1)S(1)}, u32[]{:S(2)}, u32[]{:S(2)}) %all-to-all-start.2) | async-done | bytes 458784 | tf_op jit(solution)/shard_map/all_to_all | solution.py:436
  (28 shorter events, 2.2 us)
Async XLA Ops:
  0.6 62.5 %copy-start.3 = (s32[384,8]{0,1:T(8,128)S(1)}, s32[384,8]{0,1:T(8,128)}, u32[]{:S(2)}) copy-start(s32[384,8]{0,1:T(8,128)} %param.11) | copy-start | bytes 36868
  0.6 62.5 %copy-start.2 = (s32[384,8]{0,1:T(8,128)S(1)}, s32[384,8]{0,1:T(8,128)}, u32[]{:S(2)}) copy-start(s32[384,8]{0,1:T(8,128)} %param.10) | copy-start | bytes 36868
  1.8 11.8 %collective-permute-start.1 = (bf16[392,896]{1,0:T(8,128)(2,1)S(1)}, bf16[392,896]{1,0:T(8,128)(2,1)S(1)}, u32[]{:S(2)}, u32[]{:S(2)}) collective-permute-start(bf16[392,896]{1,0:T(8,128)(2,1)S(1)} %pack.1.refs_0_), channel_id=1, source_target_pairs={{0,96},{1,25},{2,98},{3,27},{4,100},{5,29},{6,102},{7,31},{8,104},... | collective-permute-start | bytes 2107400 | tf_op jit(solution)/shard_map/ppermute | solution.py:360
  5.0 12.3 %collective-permute-start = (bf16[392,896]{1,0:T(8,128)(2,1)S(1)}, bf16[392,896]{1,0:T(8,128)(2,1)S(1)}, u32[]{:S(2)}, u32[]{:S(2)}) collective-permute-start(bf16[392,896]{1,0:T(8,128)(2,1)S(1)} %pack.1.refs_0_), channel_id=1, source_target_pairs={{0,32},{1,9},{2,34},{3,11},{4,36},{5,13},{6,38},{7,15},{8,40},{9,1... | collective-permute-start | bytes 2107400 | tf_op jit(solution)/shard_map/ppermute | solution.py:360
  20.9 27.7 %collective-permute-start.2 = (bf16[576,896]{1,0:T(8,128)(2,1)}, bf16[576,896]{1,0:T(8,128)(2,1)S(1)}, u32[]{:S(2)}, u32[]{:S(2)}) collective-permute-start(bf16[576,896]{1,0:T(8,128)(2,1)} %get-tuple-element.18), channel_id=1, source_target_pairs={{0,8},{1,33},{2,10},{3,35},{4,12},{5,37},{6,14},{7,39},{8,16},{9,4... | collective-permute-start | bytes 3096584 | tf_op jit(solution)/shard_map/ppermute | solution.py:360
  22.9 20.1 %collective-permute-start.5 = (bf16[392,896]{1,0:T(8,128)(2,1)S(1)}, bf16[392,896]{1,0:T(8,128)(2,1)S(1)}, u32[]{:S(2)}, u32[]{:S(2)}) collective-permute-start(bf16[392,896]{1,0:T(8,128)(2,1)S(1)} %pack.1.refs_0_), channel_id=1, source_target_pairs={{0,64},{1,17},{2,66},{3,19},{4,68},{5,21},{6,70},{7,23},{8,72},{9,... | collective-permute-start | bytes 2107400 | tf_op jit(solution)/shard_map/ppermute | solution.py:360
  22.9 40.8 %collective-permute-start.3 = (bf16[576,896]{1,0:T(8,128)(2,1)}, bf16[576,896]{1,0:T(8,128)(2,1)S(1)}, u32[]{:S(2)}, u32[]{:S(2)}) collective-permute-start(bf16[576,896]{1,0:T(8,128)(2,1)} %get-tuple-element.19), channel_id=1, source_target_pairs={{0,16},{1,65},{2,18},{3,67},{4,20},{5,69},{6,22},{7,71},{8,24},{9,... | collective-permute-start | bytes 3096584 | tf_op jit(solution)/shard_map/ppermute | solution.py:360
  26.5 37.3 %collective-permute-start.4 = (bf16[576,896]{1,0:T(8,128)(2,1)}, bf16[576,896]{1,0:T(8,128)(2,1)S(1)}, u32[]{:S(2)}, u32[]{:S(2)}) collective-permute-start(bf16[576,896]{1,0:T(8,128)(2,1)} %get-tuple-element.20), channel_id=1, source_target_pairs={{0,24},{1,97},{2,26},{3,99},{4,28},{5,101},{6,30},{7,103},{8,0},{9... | collective-permute-start | bytes 3096584 | tf_op jit(solution)/shard_map/ppermute | solution.py:360
  44.7 25.5 %collective-permute-start.6 = (bf16[192,896]{1,0:T(8,128)(2,1)}, bf16[192,896]{1,0:T(8,128)(2,1)S(1)}, u32[]{:S(2)}, u32[]{:S(2)}) collective-permute-start(bf16[192,896]{1,0:T(8,128)(2,1)} %get-tuple-element.23), channel_id=1, source_target_pairs={{0,8},{1,33},{2,10},{3,35},{4,12},{5,37},{6,14},{7,39},{8,16},{9,4... | collective-permute-start | bytes 1032200 | tf_op jit(solution)/shard_map/ppermute | solution.py:360
  46.8 23.4 %collective-permute-start.7 = (bf16[192,896]{1,0:T(8,128)(2,1)}, bf16[192,896]{1,0:T(8,128)(2,1)S(1)}, u32[]{:S(2)}, u32[]{:S(2)}) collective-permute-start(bf16[192,896]{1,0:T(8,128)(2,1)} %get-tuple-element.24), channel_id=1, source_target_pairs={{0,16},{1,65},{2,18},{3,67},{4,20},{5,69},{6,22},{7,71},{8,24},{9,... | collective-permute-start | bytes 1032200 | tf_op jit(solution)/shard_map/ppermute | solution.py:360
  48.6 15.2 %copy-start.4 = (bf16[576,896]{1,0:T(8,128)(2,1)}, bf16[576,896]{1,0:T(8,128)(2,1)S(1)}, u32[]{:S(2)}) copy-start(bf16[576,896]{1,0:T(8,128)(2,1)S(1)} %collective-permute-done.2.refs_1_) | copy-start | bytes 3096580
  48.6 21.7 %collective-permute-start.8 = (bf16[192,896]{1,0:T(8,128)(2,1)}, bf16[192,896]{1,0:T(8,128)(2,1)S(1)}, u32[]{:S(2)}, u32[]{:S(2)}) collective-permute-start(bf16[192,896]{1,0:T(8,128)(2,1)} %get-tuple-element.25), channel_id=1, source_target_pairs={{0,24},{1,97},{2,26},{3,99},{4,28},{5,101},{6,30},{7,103},{8,0},{9... | collective-permute-start | bytes 1032200 | tf_op jit(solution)/shard_map/ppermute | solution.py:360
  63.7 29.2 %copy-start = (bf16[384,896]{1,0:T(8,128)(2,1)S(1)}, bf16[384,896]{1,0:T(8,128)(2,1)}, u32[]{:S(2)}) copy-start(bf16[384,896]{1,0:T(8,128)(2,1)} %tok_ref.3) | copy-start | bytes 2064388
  63.7 34.7 %copy-start.1 = (bf16[896,256]{1,0:T(8,128)(2,1)S(1)}, bf16[896,256]{1,0:T(8,128)(2,1)}, u32[]{:S(2)}) copy-start(bf16[896,256]{1,0:T(8,128)(2,1)} %w_ref.3) | copy-start | bytes 1376260
  63.7 1.0 copy-start.5
  64.7 1.0 copy-start.6
  70.2 0.7 copy-start.7
  70.3 0.9 copy-start.8
  70.3 1.0 copy-start.9
  94.8 14.4 %all-to-all-start.2 = ((bf16[16,16,896]{2,1,0:T(8,128)(2,1)}), bf16[16,16,896]{2,1,0:T(8,128)(2,1)S(1)}, u32[]{:S(2)}, u32[]{:S(2)}) async-start(bf16[16,16,896]{2,1,0:T(8,128)(2,1)} %bitcast.2), calls=%async_computation.2 | async-start | bytes 917504 | tf_op jit(solution)/shard_map/all_to_all | solution.py:436

commit v2 on v1

--- a/solution.py
+++ b/solution.py
@@ -267,11 +267,10 @@
     )(in_hbm(eo), *map(in_hbm, chunks))
 
 
-def last_dots_kernel(n_width, batches, cap, side, gate_ref, eo_ref, *refs):
-    chunk_refs, early_refs, (out_ref, held, sem) = refs[:side], refs[side:-3], refs[-3:]
+def last_dots_kernel(n_width, batches, side, gate_ref, eo_ref, *refs):
+    chunk_refs, early_refs, out_ref = refs[:side], refs[side:-1], refs[-1]
     n_expert = gate_ref.shape[0]
     place = here()
-    copies = fetch_chunks(chunk_refs, held, sem, cap)
     for e in range(n_expert):
         for w in range(n_width):
             out_ref[2 * (e * n_width + w) + 1] = gate_ref[e : e + 1, :]
@@ -285,8 +284,7 @@
         for at, src in enumerate(cells_of(batch, side, place)):
             put(src, early[at : at + 1, :])
     for at, src in enumerate(cells_of(batches[-1], side, place)):
-        copies[at].wait()
-        put(src, row_dots(held.at[at], eo_ref.at[at]))
+        put(src, row_dots(chunk_refs[at], eo_ref.at[at]))
 
 
 def tail_kernel(n_expert, n_width, per_device, got_ref, parts_ref, ids_ref, slots_ref, tok_ref, lg_ref, router_ref):
@@ -407,18 +405,14 @@
         outs = row_dots_call(batch, next_batch, expert_out, landed[b], cap)
         early.append(outs[0])
     sent = pl.pallas_call(
-        functools.partial(last_dots_kernel, n_width, batches, cap, side),
+        functools.partial(last_dots_kernel, n_width, batches, side),
         out_shape=jax.ShapeDtypeStruct((2 * n_expert * n_width, 1, cap), f32),
-        in_specs=[VMEM] * 2 + [HBM] * side + [VMEM] * len(early),
+        in_specs=[VMEM] * (2 + side + len(early)),
         out_specs=VMEM,
-        scratch_shapes=[
-            pltpu.VMEM((side, cap, width), bf16),
-            pltpu.SemaphoreType.DMA((side,)),
-        ],
         compiler_params=params(6),
         cost_estimate=cost(2 * side * cap * width, 4 * side * cap * width),
         name="last_dots",
-    )(gates, outs[1], *map(in_hbm, landed[-1]), *early)
+    )(gates, outs[1], *landed[-1], *early)
     got = lax.all_to_all(sent, AXES, 0, 0, tiled=True)
 
     logit_grads, router_part = pl.pallas_call(

time: 110 us -> 108 us (0.982)
  Pallas kernels: 23.6 us -> 22.3 us
    pallas_call x1, Pallas kernels: 1.77 us -> 0.49 us  [body(): pl.pallas_call(functools.partial(last_dots_kernel, n_width, batches, side...]
    unnamed x20 -> x22, local copies, waits for them, and re-layouts: 2.91 us -> 1.96 us
where the time goes in v2:
time: 108 us
  waiting for transfers between devices  32.4 us (30%)
  blocking collectives  29.7 us (28%)
  Pallas kernels  22.3 us (21%)
  starting transfers between devices  19.7 us (18%)
  local copies, waits for them, and re-layouts  1.96 us (2%)
    ppermute x9, waiting for transfers between devices, send(): return lax.ppermute(x, AXES, line_shift(n_expert, n_width, shift, second))  27.9 us
    all_to_all x1, blocking collectives, body(): got = lax.all_to_all(sent, AXES, 0, 0, tiled=True)  19.8 us
    ppermute x9, starting transfers between devices, send(): return lax.ppermute(x, AXES, line_shift(n_expert, n_width, shift, second))  16.1 us
    all_to_all x1, blocking collectives, body(): parts = lax.all_to_all(sent_parts, 'width', 0, 0, tiled=True)  9.88 us
    pallas_call x1, Pallas kernels, body(): pl.pallas_call(functools.partial(scale_kernel, n_width, batches, cap, sid...  6.25 us
    pallas_call x2, Pallas kernels, compact(): pl.pallas_call(functools.partial(compact_kernel, [len(x) for x in sources...  5.29 us
    pallas_call x1, Pallas kernels, row_dots_call(): pl.pallas_call(functools.partial(dots_kernel, batch, side, cap, next_batc...  4.52 us
    all_to_all x1, waiting for transfers between devices, body(): lax.all_to_all(router_part.reshape(n_expert, per_device, width), 'expert'...  4.52 us
  transfers between devices with their start and end apart: 10, of which 4 were waited for; matrix products, arithmetic and copies ran while one was open for 0% of the time, Pallas kernels for 14%

profile of v2, /device:TPU:0, one launch (start us, length us, event | category | flops | bytes accessed | tf_op | source)
XLA Modules:
  0.0 107.6 jit_solution(1108561720761225932)
XLA Ops:
  0.7 1.2 %pack.1.refs_0_ = bf16[392,896]{1,0:T(8,128)(2,1)S(1)} custom-call(bf16[384,896]{1,0:T(8,128)(2,1)} %x_ref.1, s32[8,384]{1,0:T(8,128)} %bitcast.4, s32[8,384]{1,0:T(8,128)} %bitcast.8), custom_call_target="tpu_custom_call" | custom-call | bytes 1376256 | tf_op jit(solution)/shard_map/pack/pallas_call | solution.py:361
  1.8 3.2 %collective-permute-start.1 = (bf16[392,896]{1,0:T(8,128)(2,1)S(1)}, bf16[392,896]{1,0:T(8,128)(2,1)S(1)}, u32[]{:S(2)}, u32[]{:S(2)}) collective-permute-start(bf16[392,896]{1,0:T(8,128)(2,1)S(1)} %pack.1.refs_0_), channel_id=1, source_target_pairs={{0,96},{1,25},{2,98},{3,27},{4,100},{5,29},{6,102},{7,31},{8,104},... | collective-permute-start | bytes 2107400 | tf_op jit(solution)/shard_map/ppermute | solution.py:358
  5.0 8.6 %collective-permute-done.1.refs_2_ = bf16[392,896]{1,0:T(8,128)(2,1)S(1)} collective-permute-done((bf16[392,896]{1,0:T(8,128)(2,1)S(1)}, bf16[392,896]{1,0:T(8,128)(2,1)S(1)}, u32[]{:S(2)}, u32[]{:S(2)}) %collective-permute-start.1) | collective-permute-done | bytes 702496 | tf_op jit(solution)/shard_map/ppermute | solution.py:358
  13.6 3.7 %collective-permute-done.refs_1_ = bf16[392,896]{1,0:T(8,128)(2,1)S(1)} collective-permute-done((bf16[392,896]{1,0:T(8,128)(2,1)S(1)}, bf16[392,896]{1,0:T(8,128)(2,1)S(1)}, u32[]{:S(2)}, u32[]{:S(2)}) %collective-permute-start) | collective-permute-done | bytes 702496 | tf_op jit(solution)/shard_map/ppermute | solution.py:358
  17.3 3.6 %compact.2 = (bf16[576,896]{1,0:T(8,128)(2,1)}, bf16[576,896]{1,0:T(8,128)(2,1)}, bf16[576,896]{1,0:T(8,128)(2,1)}, bf16[576,896]{1,0:T(8,128)(2,1)}) custom-call(bf16[392,896]{1,0:T(8,128)(2,1)S(1)} %pack.1.refs_0_, bf16[392,896]{1,0:T(8,128)(2,1)S(1)} %collective-permute-done.refs_1_, bf16[392,896]{1,0:T(8,128)(2,1)S(1)} %collective-permute-done.1.refs_2_), custom_call_target="tpu_custom_call" | custom-call | flops 1585446912 | bytes 6193152 | tf_op jit(solution)/shard_map/compact/pallas_call | solution.py:121
  20.9 2.0 %collective-permute-start.2 = (bf16[576,896]{1,0:T(8,128)(2,1)}, bf16[576,896]{1,0:T(8,128)(2,1)S(1)}, u32[]{:S(2)}, u32[]{:S(2)}) collective-permute-start(bf16[576,896]{1,0:T(8,128)(2,1)} %get-tuple-element.18), channel_id=1, source_target_pairs={{0,8},{1,33},{2,10},{3,35},{4,12},{5,37},{6,14},{7,39},{8,16},{9,4... | collective-permute-start | bytes 3096584 | tf_op jit(solution)/shard_map/ppermute | solution.py:358
  22.9 3.6 %collective-permute-start.3 = (bf16[576,896]{1,0:T(8,128)(2,1)}, bf16[576,896]{1,0:T(8,128)(2,1)S(1)}, u32[]{:S(2)}, u32[]{:S(2)}) collective-permute-start(bf16[576,896]{1,0:T(8,128)(2,1)} %get-tuple-element.19), channel_id=1, source_target_pairs={{0,16},{1,65},{2,18},{3,67},{4,20},{5,69},{6,22},{7,71},{8,24},{9,... | collective-permute-start | bytes 3096584 | tf_op jit(solution)/shard_map/ppermute | solution.py:358
  26.5 1.0 collective-permute-start.4
  27.5 15.5 %collective-permute-done.5.refs_0_ = bf16[392,896]{1,0:T(8,128)(2,1)S(1)} collective-permute-done((bf16[392,896]{1,0:T(8,128)(2,1)S(1)}, bf16[392,896]{1,0:T(8,128)(2,1)S(1)}, u32[]{:S(2)}, u32[]{:S(2)}) %collective-permute-start.5) | collective-permute-done | bytes 702496 | tf_op jit(solution)/shard_map/ppermute | solution.py:358
  43.0 1.7 %compact.3 = (bf16[192,896]{1,0:T(8,128)(2,1)}, bf16[192,896]{1,0:T(8,128)(2,1)}, bf16[192,896]{1,0:T(8,128)(2,1)}, bf16[192,896]{1,0:T(8,128)(2,1)}) custom-call(bf16[392,896]{1,0:T(8,128)(2,1)S(1)} %collective-permute-done.5.refs_0_, bf16[576,896]{1,0:T(8,128)(2,1)} %get-tuple-element.17.refs_0_.refs_1_), custom_call_target="tpu_custom_call" | custom-call | flops 528482304 | bytes 2064384 | tf_op jit(solution)/shard_map/compact/pallas_call | solution.py:121
  44.7 2.1 %collective-permute-start.6 = (bf16[192,896]{1,0:T(8,128)(2,1)}, bf16[192,896]{1,0:T(8,128)(2,1)S(1)}, u32[]{:S(2)}, u32[]{:S(2)}) collective-permute-start(bf16[192,896]{1,0:T(8,128)(2,1)} %get-tuple-element.23), channel_id=1, source_target_pairs={{0,8},{1,33},{2,10},{3,35},{4,12},{5,37},{6,14},{7,39},{8,16},{9,4... | collective-permute-start | bytes 1032200 | tf_op jit(solution)/shard_map/ppermute | solution.py:358
  46.8 1.8 %collective-permute-start.7 = (bf16[192,896]{1,0:T(8,128)(2,1)}, bf16[192,896]{1,0:T(8,128)(2,1)S(1)}, u32[]{:S(2)}, u32[]{:S(2)}) collective-permute-start(bf16[192,896]{1,0:T(8,128)(2,1)} %get-tuple-element.24), channel_id=1, source_target_pairs={{0,16},{1,65},{2,18},{3,67},{4,20},{5,69},{6,22},{7,71},{8,24},{9,... | collective-permute-start | bytes 1032200 | tf_op jit(solution)/shard_map/ppermute | solution.py:358
  48.6 2.5 %collective-permute-start.8 = (bf16[192,896]{1,0:T(8,128)(2,1)}, bf16[192,896]{1,0:T(8,128)(2,1)S(1)}, u32[]{:S(2)}, u32[]{:S(2)}) collective-permute-start(bf16[192,896]{1,0:T(8,128)(2,1)} %get-tuple-element.25), channel_id=1, source_target_pairs={{0,24},{1,97},{2,26},{3,99},{4,28},{5,101},{6,30},{7,103},{8,0},{9... | collective-permute-start | bytes 1032200 | tf_op jit(solution)/shard_map/ppermute | solution.py:358
  51.1 2.2 %picked.1 = f32[8,8,384]{2,1,0:T(8,128)S(1)} custom-call(s32[8,384]{1,0:T(8,128)} %bitcast.5, bf16[384,896]{1,0:T(8,128)(2,1)} %tok_ref.3, bf16[896,256]{1,0:T(8,128)(2,1)} %w_ref.3), custom_call_target="tpu_custom_call" | custom-call | flops 176160768 | bytes 688128 | tf_op jit(solution)/shard_map/picked/pallas_call | solution.py:161
  53.3 9.9 %all_to_all.15.parts_ref = f32[8,8,384]{2,1,0:T(8,128)S(1)} all-to-all(f32[8,8,384]{2,1,0:T(8,128)S(1)} %picked.1), channel_id=1, replica_groups=mesh['expert'=16,'width'=8] {'width'}, dimensions={0} | all-to-all | bytes 196608 | tf_op jit(solution)/shard_map/all_to_all | solution.py:381
  63.8 0.9 copy-done.9
  64.7 1.0 copy-done.10
  65.7 4.5 %dots.1 = (f32[12,192]{1,0:T(8,128)S(1)}, bf16[4,192,896]{2,1,0:T(8,128)(2,1)S(1)}) custom-call(bf16[3072,896]{1,0:T(8,128)(2,1)} %eo_ref.1, bf16[576,896]{1,0:T(8,128)(2,1)} %get-tuple-element.17.refs_0_.refs_1_, bf16[576,896]{1,0:T(8,128)(2,1)} %copy-done.8, bf16[576,896]{1,0:T(8,128)(2,1)} %copy-done.9, bf16[576,896]{1,0:T(8,128)(2,1)} %copy-done.10), custom_call_target="tpu_custom_call" | custom-call | flops 4128768 | bytes 8257536 | tf_op jit(solution)/shard_map/dots/pallas_call | solution.py:253
  70.8 19.8 %all_to_all.16.got_ref = f32[256,1,192]{2,1,0:T(1,128)S(1)} all-to-all(f32[256,1,192]{2,1,0:T(1,128)S(1)} %last_dots.1), channel_id=1, replica_groups=mesh['expert'=16,'width'=8] {'expert','width'}, dimensions={0} | all-to-all | bytes 393216 | tf_op jit(solution)/shard_map/all_to_all | solution.py:416
  90.6 1.9 %tail.1 = (bf16[256,384]{1,0:T(8,128)(2,1)S(1)}, bf16[256,896]{1,0:T(8,128)(2,1)}) custom-call(f32[256,1,192]{2,1,0:T(1,128)S(1)} %all_to_all.16.got_ref, f32[8,8,384]{2,1,0:T(8,128)S(1)} %all_to_all.15.parts_ref, s32[8,384]{1,0:T(8,128)S(1)} %bitcast.7, s32[8,384]{1,0:T(8,128)S(1)} %bitcast.10, bf16[384,896]{1,0:T(8,128)(2,1)S(1)} %copy-done), custom_call_target="tpu_custom_call" | custom-call | flops 176160768 | bytes 688128 | tf_op jit(solution)/shard_map/tail/pallas_call | solution.py:418
  92.5 3.6 %all-to-all-start.2 = ((bf16[16,16,896]{2,1,0:T(8,128)(2,1)}), bf16[16,16,896]{2,1,0:T(8,128)(2,1)S(1)}, u32[]{:S(2)}, u32[]{:S(2)}) async-start(bf16[16,16,896]{2,1,0:T(8,128)(2,1)} %bitcast.2), calls=%async_computation.2 | async-start | bytes 917504 | tf_op jit(solution)/shard_map/all_to_all | solution.py:430
  96.1 6.3 %scale.1 = (bf16[3072,896]{1,0:T(8,128)(2,1)}, bf16[384,896]{1,0:T(8,128)(2,1)}) custom-call(f32[256,1,192]{2,1,0:T(1,128)S(1)} %all_to_all.16.got_ref, bf16[256,384]{1,0:T(8,128)(2,1)S(1)} %get-tuple-element.27.lg_ref, bf16[896,256]{1,0:T(8,128)(2,1)S(1)} %copy-done.1, bf16[576,896]{1,0:T(8,128)(2,1)} %get-tuple-element.17.refs_0_.refs_1_, ...), custom_call_target="tpu_custom_call" | custom-call | flops 176160768 | bytes 11010048 | tf_op jit(solution)/shard_map/scale/pallas_call | solution.py:432
  102.4 4.5 %all-to-all-done.2 = bf16[16,16,896]{2,1,0:T(8,128)(2,1)S(1)} async-done(((bf16[16,16,896]{2,1,0:T(8,128)(2,1)}), bf16[16,16,896]{2,1,0:T(8,128)(2,1)S(1)}, u32[]{:S(2)}, u32[]{:S(2)}) %all-to-all-start.2) | async-done | bytes 458784 | tf_op jit(solution)/shard_map/all_to_all | solution.py:430
  106.9 0.7 convert_reduce_fusion
  (30 shorter events, 1.1 us)
Async XLA Ops:
  0.6 62.6 %copy-start.7 = (s32[384,8]{0,1:T(8,128)S(1)}, s32[384,8]{0,1:T(8,128)}, u32[]{:S(2)}) copy-start(s32[384,8]{0,1:T(8,128)} %param.11) | copy-start | bytes 36868
  0.6 62.5 %copy-start.6 = (s32[384,8]{0,1:T(8,128)S(1)}, s32[384,8]{0,1:T(8,128)}, u32[]{:S(2)}) copy-start(s32[384,8]{0,1:T(8,128)} %param.10) | copy-start | bytes 36868
  1.8 11.8 %collective-permute-start.1 = (bf16[392,896]{1,0:T(8,128)(2,1)S(1)}, bf16[392,896]{1,0:T(8,128)(2,1)S(1)}, u32[]{:S(2)}, u32[]{:S(2)}) collective-permute-start(bf16[392,896]{1,0:T(8,128)(2,1)S(1)} %pack.1.refs_0_), channel_id=1, source_target_pairs={{0,96},{1,25},{2,98},{3,27},{4,100},{5,29},{6,102},{7,31},{8,104},... | collective-permute-start | bytes 2107400 | tf_op jit(solution)/shard_map/ppermute | solution.py:358
  5.0 12.3 %collective-permute-start = (bf16[392,896]{1,0:T(8,128)(2,1)S(1)}, bf16[392,896]{1,0:T(8,128)(2,1)S(1)}, u32[]{:S(2)}, u32[]{:S(2)}) collective-permute-start(bf16[392,896]{1,0:T(8,128)(2,1)S(1)} %pack.1.refs_0_), channel_id=1, source_target_pairs={{0,32},{1,9},{2,34},{3,11},{4,36},{5,13},{6,38},{7,15},{8,40},{9,1... | collective-permute-start | bytes 2107400 | tf_op jit(solution)/shard_map/ppermute | solution.py:358
  20.9 27.7 %collective-permute-start.2 = (bf16[576,896]{1,0:T(8,128)(2,1)}, bf16[576,896]{1,0:T(8,128)(2,1)S(1)}, u32[]{:S(2)}, u32[]{:S(2)}) collective-permute-start(bf16[576,896]{1,0:T(8,128)(2,1)} %get-tuple-element.18), channel_id=1, source_target_pairs={{0,8},{1,33},{2,10},{3,35},{4,12},{5,37},{6,14},{7,39},{8,16},{9,4... | collective-permute-start | bytes 3096584 | tf_op jit(solution)/shard_map/ppermute | solution.py:358
  22.9 20.1 %collective-permute-start.5 = (bf16[392,896]{1,0:T(8,128)(2,1)S(1)}, bf16[392,896]{1,0:T(8,128)(2,1)S(1)}, u32[]{:S(2)}, u32[]{:S(2)}) collective-permute-start(bf16[392,896]{1,0:T(8,128)(2,1)S(1)} %pack.1.refs_0_), channel_id=1, source_target_pairs={{0,64},{1,17},{2,66},{3,19},{4,68},{5,21},{6,70},{7,23},{8,72},{9,... | collective-permute-start | bytes 2107400 | tf_op jit(solution)/shard_map/ppermute | solution.py:358
  22.9 40.8 %collective-permute-start.3 = (bf16[576,896]{1,0:T(8,128)(2,1)}, bf16[576,896]{1,0:T(8,128)(2,1)S(1)}, u32[]{:S(2)}, u32[]{:S(2)}) collective-permute-start(bf16[576,896]{1,0:T(8,128)(2,1)} %get-tuple-element.19), channel_id=1, source_target_pairs={{0,16},{1,65},{2,18},{3,67},{4,20},{5,69},{6,22},{7,71},{8,24},{9,... | collective-permute-start | bytes 3096584 | tf_op jit(solution)/shard_map/ppermute | solution.py:358
  26.5 37.3 %collective-permute-start.4 = (bf16[576,896]{1,0:T(8,128)(2,1)}, bf16[576,896]{1,0:T(8,128)(2,1)S(1)}, u32[]{:S(2)}, u32[]{:S(2)}) collective-permute-start(bf16[576,896]{1,0:T(8,128)(2,1)} %get-tuple-element.20), channel_id=1, source_target_pairs={{0,24},{1,97},{2,26},{3,99},{4,28},{5,101},{6,30},{7,103},{8,0},{9... | collective-permute-start | bytes 3096584 | tf_op jit(solution)/shard_map/ppermute | solution.py:358
  44.7 25.5 %collective-permute-start.6 = (bf16[192,896]{1,0:T(8,128)(2,1)}, bf16[192,896]{1,0:T(8,128)(2,1)S(1)}, u32[]{:S(2)}, u32[]{:S(2)}) collective-permute-start(bf16[192,896]{1,0:T(8,128)(2,1)} %get-tuple-element.23), channel_id=1, source_target_pairs={{0,8},{1,33},{2,10},{3,35},{4,12},{5,37},{6,14},{7,39},{8,16},{9,4... | collective-permute-start | bytes 1032200 | tf_op jit(solution)/shard_map/ppermute | solution.py:358
  46.8 23.4 %collective-permute-start.7 = (bf16[192,896]{1,0:T(8,128)(2,1)}, bf16[192,896]{1,0:T(8,128)(2,1)S(1)}, u32[]{:S(2)}, u32[]{:S(2)}) collective-permute-start(bf16[192,896]{1,0:T(8,128)(2,1)} %get-tuple-element.24), channel_id=1, source_target_pairs={{0,16},{1,65},{2,18},{3,67},{4,20},{5,69},{6,22},{7,71},{8,24},{9,... | collective-permute-start | bytes 1032200 | tf_op jit(solution)/shard_map/ppermute | solution.py:358
  48.6 15.2 %copy-start.8 = (bf16[576,896]{1,0:T(8,128)(2,1)}, bf16[576,896]{1,0:T(8,128)(2,1)S(1)}, u32[]{:S(2)}) copy-start(bf16[576,896]{1,0:T(8,128)(2,1)S(1)} %collective-permute-done.2.refs_1_) | copy-start | bytes 3096580
  48.6 21.7 %copy-start.2 = (bf16[192,896]{1,0:T(8,128)(2,1)S(1)}, bf16[192,896]{1,0:T(8,128)(2,1)}, u32[]{:S(2)}) copy-start(bf16[192,896]{1,0:T(8,128)(2,1)} %get-tuple-element.22.refs_0_.refs_4_) | copy-start | bytes 1032196
  48.6 21.7 %collective-permute-start.8 = (bf16[192,896]{1,0:T(8,128)(2,1)}, bf16[192,896]{1,0:T(8,128)(2,1)S(1)}, u32[]{:S(2)}, u32[]{:S(2)}) collective-permute-start(bf16[192,896]{1,0:T(8,128)(2,1)} %get-tuple-element.25), channel_id=1, source_target_pairs={{0,24},{1,97},{2,26},{3,99},{4,28},{5,101},{6,30},{7,103},{8,0},{9... | collective-permute-start | bytes 1032200 | tf_op jit(solution)/shard_map/ppermute | solution.py:358
  63.7 26.9 %copy-start = (bf16[384,896]{1,0:T(8,128)(2,1)S(1)}, bf16[384,896]{1,0:T(8,128)(2,1)}, u32[]{:S(2)}) copy-start(bf16[384,896]{1,0:T(8,128)(2,1)} %tok_ref.3) | copy-start | bytes 2064388
  63.7 32.4 %copy-start.1 = (bf16[896,256]{1,0:T(8,128)(2,1)S(1)}, bf16[896,256]{1,0:T(8,128)(2,1)}, u32[]{:S(2)}) copy-start(bf16[896,256]{1,0:T(8,128)(2,1)} %w_ref.3) | copy-start | bytes 1376260
  63.7 1.0 copy-start.9
  64.7 1.0 copy-start.10
  70.2 25.9 %copy-start.3 = (bf16[192,896]{1,0:T(8,128)(2,1)}, bf16[192,896]{1,0:T(8,128)(2,1)S(1)}, u32[]{:S(2)}) copy-start(bf16[192,896]{1,0:T(8,128)(2,1)S(1)} %collective-permute-done.6.refs_1_.refs_5_) | copy-start | bytes 1032196
  70.2 25.9 %copy-start.4 = (bf16[192,896]{1,0:T(8,128)(2,1)}, bf16[192,896]{1,0:T(8,128)(2,1)S(1)}, u32[]{:S(2)}) copy-start(bf16[192,896]{1,0:T(8,128)(2,1)S(1)} %collective-permute-done.7.refs_2_.refs_6_) | copy-start | bytes 1032196
  70.3 25.9 %copy-start.5 = (bf16[192,896]{1,0:T(8,128)(2,1)}, bf16[192,896]{1,0:T(8,128)(2,1)S(1)}, u32[]{:S(2)}) copy-start(bf16[192,896]{1,0:T(8,128)(2,1)S(1)} %collective-permute-done.8.refs_3_.refs_7_) | copy-start | bytes 1032196
  92.5 14.4 %all-to-all-start.2 = ((bf16[16,16,896]{2,1,0:T(8,128)(2,1)}), bf16[16,16,896]{2,1,0:T(8,128)(2,1)S(1)}, u32[]{:S(2)}, u32[]{:S(2)}) async-start(bf16[16,16,896]{2,1,0:T(8,128)(2,1)} %bitcast.2), calls=%async_computation.2 | async-start | bytes 917504 | tf_op jit(solution)/shard_map/all_to_all | solution.py:430

commit v3 on v2

--- a/solution.py
+++ b/solution.py
@@ -58,13 +58,14 @@
     return pltpu.with_memory_space_constraint(x, pltpu.HBM)
 
 
-def pack_kernel(per_device, x_ref, ids_ref, slots_ref, out_ref, held_ids, held_slots, sem):
+def pack_kernel(per_device, x_ref, ids_ref, slots_ref, first_ref, last_ref, held_ids, held_slots, sem):
     tok, width = x_ref.shape
-    top = ids_ref.shape[0]
+    top, half = ids_ref.shape[0], first_ref.shape[0]
     copies = [
         pltpu.make_async_copy(ids_ref, held_ids, sem.at[0]),
         pltpu.make_async_copy(slots_ref, held_slots, sem.at[1]),
-        pltpu.make_async_copy(x_ref, out_ref.at[pl.ds(0, tok), :], sem.at[2]),
+        pltpu.make_async_copy(x_ref.at[pl.ds(0, half), :], first_ref, sem.at[2]),
+        pltpu.make_async_copy(x_ref.at[pl.ds(half, tok - half), :], last_ref.at[pl.ds(0, tok - half), :], sem.at[3]),
     ]
     for copy in copies:
         copy.start()
@@ -73,8 +74,9 @@
     dev = (held_ids[...] // per_device).astype(f32)
     slots = held_slots[...].astype(f32)
     rest = jnp.zeros((top, width - 2 * tok), f32)
-    out_ref[tok:, :] = jnp.concatenate([dev, slots, rest], axis=1).astype(bf16)
+    last_ref[tok - half :, :] = jnp.concatenate([dev, slots, rest], axis=1).astype(bf16)
     copies[2].wait()
+    copies[3].wait()
 
 
 def compact_kernel(parts, tok, cap, n_dest, halves, *refs):
@@ -358,31 +360,38 @@
         return lax.ppermute(x, AXES, line_shift(n_expert, n_width, shift, second))
 
     ids, slots = expert_ids.T, slot_ids.T
-    packed = pl.pallas_call(
+    half = tok // 2
+    first, last = pl.pallas_call(
         functools.partial(pack_kernel, per_device),
-        out_shape=jax.ShapeDtypeStruct((tok + top, width), bf16),
+        out_shape=[
+            jax.ShapeDtypeStruct((half, width), bf16),
+            jax.ShapeDtypeStruct((tok - half + top, width), bf16),
+        ],
         in_specs=[HBM] * 3,
-        out_specs=VMEM,
+        out_specs=[VMEM] * 2,
         scratch_shapes=[
             pltpu.VMEM((top, tok), i32),
             pltpu.VMEM((top, tok), i32),
-            pltpu.SemaphoreType.DMA((3,)),
+            pltpu.SemaphoreType.DMA((4,)),
         ],
         compiler_params=params(4),
         cost_estimate=cost(0, 4 * tok * width),
         name="pack",
     )(in_hbm(out_grad), in_hbm(ids), in_hbm(slots))
-    xs = {0: packed}
-    for s in [1, side - 1] + list(range(2, side - 1)):
-        xs[s] = send(packed, s, False)
-    batches = [[0, 1, side - 1], list(range(2, side - 1))]
+    up_first = send(first, 1, False)
+    down_last = send(last, side - 1, False)
+    up_last = send(last, 1, False)
+    down_first = send(first, side - 1, False)
+    far = [send(up_first, 1, False), send(down_last, side - 1, False)]
+    sources = {0: [first, last], 1: [up_first, up_last], side - 1: [down_first, down_last], 2: far}
+    batches = [[0, 1, side - 1], [2]]
 
     sent_parts = front(ids, tokens_in, router_weight, n_width)
     parts = lax.all_to_all(sent_parts, "width", 0, 0, tiled=True)
 
     landed, after = [], []
     for batch in batches:
-        chunks = compact([[xs[s]] for s in batch], after, tok, cap, side)
+        chunks = compact([sources[s] for s in batch], after, tok, cap, side)
         after = [chunks[0]]
         group = [chunks[0]]
         for d in range(1, side):

time: 108 us -> 106 us (0.981)
  waiting for transfers between devices: 32.4 us -> 27.2 us
  starting transfers between devices: 19.7 us -> 22 us
    ppermute x9 -> x12, waiting for transfers between devices: 27.9 us -> 22.7 us  [send(): return lax.ppermute(x, AXES, line_shift(n_expert, n_width, shift, second))]
    ppermute x9 -> x12, starting transfers between devices: 16.1 us -> 18.4 us  [send(): return lax.ppermute(x, AXES, line_shift(n_expert, n_width, shift, second))]
  transfers between devices with their start and end apart: 10 -> 13, of which waited for: 4 -> 5; matrix products, arithmetic and copies ran while one was open for 0% -> 0% of each run, Pallas kernels for 14% -> 14%
where the time goes in v3:
time: 106 us
  blocking collectives  30.4 us (29%)
  waiting for transfers between devices  27.2 us (26%)
  Pallas kernels  22.6 us (21%)
  starting transfers between devices  22 us (21%)
  local copies, waits for them, and re-layouts  1.96 us (2%)
    ppermute x12, waiting for transfers between devices, send(): return lax.ppermute(x, AXES, line_shift(n_expert, n_width, shift, second))  22.7 us
    all_to_all x1, blocking collectives, body(): got = lax.all_to_all(sent, AXES, 0, 0, tiled=True)  20.5 us
    ppermute x12, starting transfers between devices, send(): return lax.ppermute(x, AXES, line_shift(n_expert, n_width, shift, second))  18.4 us
    all_to_all x1, blocking collectives, body(): parts = lax.all_to_all(sent_parts, 'width', 0, 0, tiled=True)  9.88 us
    pallas_call x1, Pallas kernels, body(): pl.pallas_call(functools.partial(scale_kernel, n_width, batches, cap, sid...  6.25 us
    pallas_call x2, Pallas kernels, compact(): pl.pallas_call(functools.partial(compact_kernel, [len(x) for x in sources...  5.54 us
    all_to_all x1, waiting for transfers between devices, body(): lax.all_to_all(router_part.reshape(n_expert, per_device, width), 'expert'...  4.53 us
    pallas_call x1, Pallas kernels, row_dots_call(): pl.pallas_call(functools.partial(dots_kernel, batch, side, cap, next_batc...  4.52 us
  transfers between devices with their start and end apart: 13, of which 5 were waited for; matrix products, arithmetic and copies ran while one was open for 0% of the time, Pallas kernels for 14%

profile of v3, /device:TPU:0, one launch (start us, length us, event | category | flops | bytes accessed | tf_op | source)
XLA Modules:
  0.0 105.7 jit_solution(13384299516134517292)
XLA Ops:
  0.7 1.2 %pack.1 = (bf16[192,896]{1,0:T(8,128)(2,1)S(1)}, bf16[200,896]{1,0:T(8,128)(2,1)S(1)}) custom-call(bf16[384,896]{1,0:T(8,128)(2,1)} %x_ref.1, s32[8,384]{1,0:T(8,128)} %bitcast.4, s32[8,384]{1,0:T(8,128)} %bitcast.8), custom_call_target="tpu_custom_call" | custom-call | bytes 1376256 | tf_op jit(solution)/shard_map/pack/pallas_call | solution.py:364
  1.8 3.2 %collective-permute-start.3 = (bf16[200,896]{1,0:T(8,128)(2,1)S(1)}, bf16[200,896]{1,0:T(8,128)(2,1)S(1)}, u32[]{:S(2)}, u32[]{:S(2)}) collective-permute-start(bf16[200,896]{1,0:T(8,128)(2,1)S(1)} %get-tuple-element.20.refs_1_), channel_id=1, source_target_pairs={{0,96},{1,25},{2,98},{3,27},{4,100},{5,29},{6,102},{7,31},{8,104},... | collective-permute-start | bytes 1075208 | tf_op jit(solution)/shard_map/ppermute | solution.py:360
  5.0 3.2 %collective-permute-start.2 = (bf16[192,896]{1,0:T(8,128)(2,1)S(1)}, bf16[192,896]{1,0:T(8,128)(2,1)S(1)}, u32[]{:S(2)}, u32[]{:S(2)}) collective-permute-start(bf16[192,896]{1,0:T(8,128)(2,1)S(1)} %get-tuple-element.19.refs_0_), channel_id=1, source_target_pairs={{0,96},{1,25},{2,98},{3,27},{4,100},{5,29},{6,102},{7,31},{8,104},... | collective-permute-start | bytes 1032200 | tf_op jit(solution)/shard_map/ppermute | solution.py:360
  8.3 5.4 %collective-permute-done.2.refs_4_ = bf16[192,896]{1,0:T(8,128)(2,1)S(1)} collective-permute-done((bf16[192,896]{1,0:T(8,128)(2,1)S(1)}, bf16[192,896]{1,0:T(8,128)(2,1)S(1)}, u32[]{:S(2)}, u32[]{:S(2)}) %collective-permute-start.2) | collective-permute-done | bytes 344096 | tf_op jit(solution)/shard_map/ppermute | solution.py:360
  13.6 3.7 %collective-permute-done.refs_2_ = bf16[192,896]{1,0:T(8,128)(2,1)S(1)} collective-permute-done((bf16[192,896]{1,0:T(8,128)(2,1)S(1)}, bf16[192,896]{1,0:T(8,128)(2,1)S(1)}, u32[]{:S(2)}, u32[]{:S(2)}) %collective-permute-start) | collective-permute-done | bytes 344096 | tf_op jit(solution)/shard_map/ppermute | solution.py:360
  17.3 3.7 %compact.2 = (bf16[576,896]{1,0:T(8,128)(2,1)}, bf16[576,896]{1,0:T(8,128)(2,1)}, bf16[576,896]{1,0:T(8,128)(2,1)}, bf16[576,896]{1,0:T(8,128)(2,1)}) custom-call(bf16[192,896]{1,0:T(8,128)(2,1)S(1)} %get-tuple-element.19.refs_0_, bf16[200,896]{1,0:T(8,128)(2,1)S(1)} %get-tuple-element.20.refs_1_, bf16[192,896]{1,0:T(8,128)(2,1)S(1)} %collective-permute-done.refs_2_, ...), custom_call_target="tpu_custom_call" | custom-call | flops 1585446912 | bytes 6193152 | tf_op jit(solution)/shard_map/compact/pallas_call | solution.py:123
  21.1 2.0 %collective-permute-start.4 = (bf16[576,896]{1,0:T(8,128)(2,1)}, bf16[576,896]{1,0:T(8,128)(2,1)S(1)}, u32[]{:S(2)}, u32[]{:S(2)}) collective-permute-start(bf16[576,896]{1,0:T(8,128)(2,1)} %get-tuple-element.22), channel_id=1, source_target_pairs={{0,8},{1,33},{2,10},{3,35},{4,12},{5,37},{6,14},{7,39},{8,16},{9,4... | collective-permute-start | bytes 3096584 | tf_op jit(solution)/shard_map/ppermute | solution.py:360
  23.0 3.6 %collective-permute-start.5 = (bf16[576,896]{1,0:T(8,128)(2,1)}, bf16[576,896]{1,0:T(8,128)(2,1)S(1)}, u32[]{:S(2)}, u32[]{:S(2)}) collective-permute-start(bf16[576,896]{1,0:T(8,128)(2,1)} %get-tuple-element.23), channel_id=1, source_target_pairs={{0,16},{1,65},{2,18},{3,67},{4,20},{5,69},{6,22},{7,71},{8,24},{9,... | collective-permute-start | bytes 3096584 | tf_op jit(solution)/shard_map/ppermute | solution.py:360
  26.6 1.0 collective-permute-start.6
  27.7 2.0 %collective-permute-start.7 = (bf16[192,896]{1,0:T(8,128)(2,1)S(1)}, bf16[192,896]{1,0:T(8,128)(2,1)S(1)}, u32[]{:S(2)}, u32[]{:S(2)}) collective-permute-start(bf16[192,896]{1,0:T(8,128)(2,1)S(1)} %collective-permute-done.refs_2_), channel_id=1, source_target_pairs={{0,32},{1,9},{2,34},{3,11},{4,36},{5,13},{6,38},{7,15},{8,40},{9,1... | collective-permute-start | bytes 1032200 | tf_op jit(solution)/shard_map/ppermute | solution.py:360
  29.7 9.9 %collective-permute-done.7.refs_0_ = bf16[192,896]{1,0:T(8,128)(2,1)S(1)} collective-permute-done((bf16[192,896]{1,0:T(8,128)(2,1)S(1)}, bf16[192,896]{1,0:T(8,128)(2,1)S(1)}, u32[]{:S(2)}, u32[]{:S(2)}) %collective-permute-start.7) | collective-permute-done | bytes 344096 | tf_op jit(solution)/shard_map/ppermute | solution.py:360
  39.6 3.6 %collective-permute-done.8.refs_1_ = bf16[200,896]{1,0:T(8,128)(2,1)S(1)} collective-permute-done((bf16[200,896]{1,0:T(8,128)(2,1)S(1)}, bf16[200,896]{1,0:T(8,128)(2,1)S(1)}, u32[]{:S(2)}, u32[]{:S(2)}) %collective-permute-start.8) | collective-permute-done | bytes 358432 | tf_op jit(solution)/shard_map/ppermute | solution.py:360
  43.3 1.8 %compact.3 = (bf16[192,896]{1,0:T(8,128)(2,1)}, bf16[192,896]{1,0:T(8,128)(2,1)}, bf16[192,896]{1,0:T(8,128)(2,1)}, bf16[192,896]{1,0:T(8,128)(2,1)}) custom-call(bf16[192,896]{1,0:T(8,128)(2,1)S(1)} %collective-permute-done.7.refs_0_, bf16[200,896]{1,0:T(8,128)(2,1)S(1)} %collective-permute-done.8.refs_1_, bf16[576,896]{1,0:T(8,128)(2,1)} %get-tuple-element.21.refs_0_.refs_2_), custom_call_target="tpu_custom_call" | custom-call | flops 528482304 | bytes 2064384 | tf_op jit(solution)/shard_map/compact/pallas_call | solution.py:123
  45.2 1.9 %collective-permute-start.10 = (bf16[192,896]{1,0:T(8,128)(2,1)}, bf16[192,896]{1,0:T(8,128)(2,1)S(1)}, u32[]{:S(2)}, u32[]{:S(2)}) collective-permute-start(bf16[192,896]{1,0:T(8,128)(2,1)} %get-tuple-element.28), channel_id=1, source_target_pairs={{0,16},{1,65},{2,18},{3,67},{4,20},{5,69},{6,22},{7,71},{8,24},{9,... | collective-permute-start | bytes 1032200 | tf_op jit(solution)/shard_map/ppermute | solution.py:360
  47.0 1.4 %collective-permute-start.11 = (bf16[192,896]{1,0:T(8,128)(2,1)}, bf16[192,896]{1,0:T(8,128)(2,1)S(1)}, u32[]{:S(2)}, u32[]{:S(2)}) collective-permute-start(bf16[192,896]{1,0:T(8,128)(2,1)} %get-tuple-element.29), channel_id=1, source_target_pairs={{0,24},{1,97},{2,26},{3,99},{4,28},{5,101},{6,30},{7,103},{8,0},{9... | collective-permute-start | bytes 1032200 | tf_op jit(solution)/shard_map/ppermute | solution.py:360
  48.5 2.2 %picked.1 = f32[8,8,384]{2,1,0:T(8,128)S(1)} custom-call(s32[8,384]{1,0:T(8,128)} %bitcast.5, bf16[384,896]{1,0:T(8,128)(2,1)} %tok_ref.3, bf16[896,256]{1,0:T(8,128)(2,1)} %w_ref.3), custom_call_target="tpu_custom_call" | custom-call | flops 176160768 | bytes 688128 | tf_op jit(solution)/shard_map/picked/pallas_call | solution.py:163
  50.7 9.9 %all_to_all.15.parts_ref = f32[8,8,384]{2,1,0:T(8,128)S(1)} all-to-all(f32[8,8,384]{2,1,0:T(8,128)S(1)} %picked.1), channel_id=1, replica_groups=mesh['expert'=16,'width'=8] {'width'}, dimensions={0} | all-to-all | bytes 196608 | tf_op jit(solution)/shard_map/all_to_all | solution.py:390
  62.1 1.0 copy-done.10
  63.1 4.5 %dots.1 = (f32[12,192]{1,0:T(8,128)S(1)}, bf16[4,192,896]{2,1,0:T(8,128)(2,1)S(1)}) custom-call(bf16[3072,896]{1,0:T(8,128)(2,1)} %eo_ref.1, bf16[576,896]{1,0:T(8,128)(2,1)} %get-tuple-element.21.refs_0_.refs_2_, bf16[576,896]{1,0:T(8,128)(2,1)} %copy-done.8, bf16[576,896]{1,0:T(8,128)(2,1)} %copy-done.9, bf16[576,896]{1,0:T(8,128)(2,1)} %copy-done.10), custom_call_target="tpu_custom_call" | custom-call | flops 4128768 | bytes 8257536 | tf_op jit(solution)/shard_map/dots/pallas_call | solution.py:255
  68.1 20.5 %all_to_all.16.got_ref = f32[256,1,192]{2,1,0:T(1,128)S(1)} all-to-all(f32[256,1,192]{2,1,0:T(1,128)S(1)} %last_dots.1), channel_id=1, replica_groups=mesh['expert'=16,'width'=8] {'expert','width'}, dimensions={0} | all-to-all | bytes 393216 | tf_op jit(solution)/shard_map/all_to_all | solution.py:425
  88.7 1.9 %tail.1 = (bf16[256,384]{1,0:T(8,128)(2,1)S(1)}, bf16[256,896]{1,0:T(8,128)(2,1)}) custom-call(f32[256,1,192]{2,1,0:T(1,128)S(1)} %all_to_all.16.got_ref, f32[8,8,384]{2,1,0:T(8,128)S(1)} %all_to_all.15.parts_ref, s32[8,384]{1,0:T(8,128)S(1)} %bitcast.7, s32[8,384]{1,0:T(8,128)S(1)} %bitcast.10, bf16[384,896]{1,0:T(8,128)(2,1)S(1)} %copy-done), custom_call_target="tpu_custom_call" | custom-call | flops 176160768 | bytes 688128 | tf_op jit(solution)/shard_map/tail/pallas_call | solution.py:427
  90.6 3.6 %all-to-all-start.2 = ((bf16[16,16,896]{2,1,0:T(8,128)(2,1)}), bf16[16,16,896]{2,1,0:T(8,128)(2,1)S(1)}, u32[]{:S(2)}, u32[]{:S(2)}) async-start(bf16[16,16,896]{2,1,0:T(8,128)(2,1)} %bitcast.2), calls=%async_computation.2 | async-start | bytes 917504 | tf_op jit(solution)/shard_map/all_to_all | solution.py:439
  94.2 6.3 %scale.1 = (bf16[3072,896]{1,0:T(8,128)(2,1)}, bf16[384,896]{1,0:T(8,128)(2,1)}) custom-call(f32[256,1,192]{2,1,0:T(1,128)S(1)} %all_to_all.16.got_ref, bf16[256,384]{1,0:T(8,128)(2,1)S(1)} %get-tuple-element.31.lg_ref, bf16[896,256]{1,0:T(8,128)(2,1)S(1)} %copy-done.1, bf16[576,896]{1,0:T(8,128)(2,1)} %get-tuple-element.21.refs_0_.refs_2_, ...), custom_call_target="tpu_custom_call" | custom-call | flops 176160768 | bytes 11010048 | tf_op jit(solution)/shard_map/scale/pallas_call | solution.py:441
  100.4 4.5 %all-to-all-done.2 = bf16[16,16,896]{2,1,0:T(8,128)(2,1)S(1)} async-done(((bf16[16,16,896]{2,1,0:T(8,128)(2,1)}), bf16[16,16,896]{2,1,0:T(8,128)(2,1)S(1)}, u32[]{:S(2)}, u32[]{:S(2)}) %all-to-all-start.2) | async-done | bytes 458784 | tf_op jit(solution)/shard_map/all_to_all | solution.py:439
  (36 shorter events, 2.8 us)
Async XLA Ops:
  0.6 59.9 %copy-start.7 = (s32[384,8]{0,1:T(8,128)S(1)}, s32[384,8]{0,1:T(8,128)}, u32[]{:S(2)}) copy-start(s32[384,8]{0,1:T(8,128)} %param.11) | copy-start | bytes 36868
  0.6 59.9 %copy-start.6 = (s32[384,8]{0,1:T(8,128)S(1)}, s32[384,8]{0,1:T(8,128)}, u32[]{:S(2)}) copy-start(s32[384,8]{0,1:T(8,128)} %param.10) | copy-start | bytes 36868
  1.8 15.5 %collective-permute-start.3 = (bf16[200,896]{1,0:T(8,128)(2,1)S(1)}, bf16[200,896]{1,0:T(8,128)(2,1)S(1)}, u32[]{:S(2)}, u32[]{:S(2)}) collective-permute-start(bf16[200,896]{1,0:T(8,128)(2,1)S(1)} %get-tuple-element.20.refs_1_), channel_id=1, source_target_pairs={{0,96},{1,25},{2,98},{3,27},{4,100},{5,29},{6,102},{7,31},{8,104},... | collective-permute-start | bytes 1075208 | tf_op jit(solution)/shard_map/ppermute | solution.py:360
  5.0 12.3 %collective-permute-start.1 = (bf16[200,896]{1,0:T(8,128)(2,1)S(1)}, bf16[200,896]{1,0:T(8,128)(2,1)S(1)}, u32[]{:S(2)}, u32[]{:S(2)}) collective-permute-start(bf16[200,896]{1,0:T(8,128)(2,1)S(1)} %get-tuple-element.20.refs_1_), channel_id=1, source_target_pairs={{0,32},{1,9},{2,34},{3,11},{4,36},{5,13},{6,38},{7,15},{8,40},{9,1... | collective-permute-start | bytes 1075208 | tf_op jit(solution)/shard_map/ppermute | solution.py:360
  5.0 8.6 %collective-permute-start.2 = (bf16[192,896]{1,0:T(8,128)(2,1)S(1)}, bf16[192,896]{1,0:T(8,128)(2,1)S(1)}, u32[]{:S(2)}, u32[]{:S(2)}) collective-permute-start(bf16[192,896]{1,0:T(8,128)(2,1)S(1)} %get-tuple-element.19.refs_0_), channel_id=1, source_target_pairs={{0,96},{1,25},{2,98},{3,27},{4,100},{5,29},{6,102},{7,31},{8,104},... | collective-permute-start | bytes 1032200 | tf_op jit(solution)/shard_map/ppermute | solution.py:360
  8.3 9.1 %collective-permute-start = (bf16[192,896]{1,0:T(8,128)(2,1)S(1)}, bf16[192,896]{1,0:T(8,128)(2,1)S(1)}, u32[]{:S(2)}, u32[]{:S(2)}) collective-permute-start(bf16[192,896]{1,0:T(8,128)(2,1)S(1)} %get-tuple-element.19.refs_0_), channel_id=1, source_target_pairs={{0,32},{1,9},{2,34},{3,11},{4,36},{5,13},{6,38},{7,15},{8,40},{9,1... | collective-permute-start | bytes 1032200 | tf_op jit(solution)/shard_map/ppermute | solution.py:360
  21.1 26.0 %collective-permute-start.4 = (bf16[576,896]{1,0:T(8,128)(2,1)}, bf16[576,896]{1,0:T(8,128)(2,1)S(1)}, u32[]{:S(2)}, u32[]{:S(2)}) collective-permute-start(bf16[576,896]{1,0:T(8,128)(2,1)} %get-tuple-element.22), channel_id=1, source_target_pairs={{0,8},{1,33},{2,10},{3,35},{4,12},{5,37},{6,14},{7,39},{8,16},{9,4... | collective-permute-start | bytes 3096584 | tf_op jit(solution)/shard_map/ppermute | solution.py:360
  23.0 38.1 %collective-permute-start.5 = (bf16[576,896]{1,0:T(8,128)(2,1)}, bf16[576,896]{1,0:T(8,128)(2,1)S(1)}, u32[]{:S(2)}, u32[]{:S(2)}) collective-permute-start(bf16[576,896]{1,0:T(8,128)(2,1)} %get-tuple-element.23), channel_id=1, source_target_pairs={{0,16},{1,65},{2,18},{3,67},{4,20},{5,69},{6,22},{7,71},{8,24},{9,... | collective-permute-start | bytes 3096584 | tf_op jit(solution)/shard_map/ppermute | solution.py:360
  26.6 34.5 %collective-permute-start.6 = (bf16[576,896]{1,0:T(8,128)(2,1)}, bf16[576,896]{1,0:T(8,128)(2,1)S(1)}, u32[]{:S(2)}, u32[]{:S(2)}) collective-permute-start(bf16[576,896]{1,0:T(8,128)(2,1)} %get-tuple-element.24), channel_id=1, source_target_pairs={{0,24},{1,97},{2,26},{3,99},{4,28},{5,101},{6,30},{7,103},{8,0},{9... | collective-permute-start | bytes 3096584 | tf_op jit(solution)/shard_map/ppermute | solution.py:360
  27.6 15.6 %collective-permute-start.8 = (bf16[200,896]{1,0:T(8,128)(2,1)S(1)}, bf16[200,896]{1,0:T(8,128)(2,1)S(1)}, u32[]{:S(2)}, u32[]{:S(2)}) collective-permute-start(bf16[200,896]{1,0:T(8,128)(2,1)S(1)} %collective-permute-done.3.refs_5_), channel_id=1, source_target_pairs={{0,96},{1,25},{2,98},{3,27},{4,100},{5,29},{6,102},{7,31},{8,104},... | collective-permute-start | bytes 1075208 | tf_op jit(solution)/shard_map/ppermute | solution.py:360
  27.7 12.0 %collective-permute-start.7 = (bf16[192,896]{1,0:T(8,128)(2,1)S(1)}, bf16[192,896]{1,0:T(8,128)(2,1)S(1)}, u32[]{:S(2)}, u32[]{:S(2)}) collective-permute-start(bf16[192,896]{1,0:T(8,128)(2,1)S(1)} %collective-permute-done.refs_2_), channel_id=1, source_target_pairs={{0,32},{1,9},{2,34},{3,11},{4,36},{5,13},{6,38},{7,15},{8,40},{9,1... | collective-permute-start | bytes 1032200 | tf_op jit(solution)/shard_map/ppermute | solution.py:360
  45.1 22.5 %collective-permute-start.9 = (bf16[192,896]{1,0:T(8,128)(2,1)}, bf16[192,896]{1,0:T(8,128)(2,1)S(1)}, u32[]{:S(2)}, u32[]{:S(2)}) collective-permute-start(bf16[192,896]{1,0:T(8,128)(2,1)} %get-tuple-element.27), channel_id=1, source_target_pairs={{0,8},{1,33},{2,10},{3,35},{4,12},{5,37},{6,14},{7,39},{8,16},{9,4... | collective-permute-start | bytes 1032200 | tf_op jit(solution)/shard_map/ppermute | solution.py:360
  45.2 22.4 %collective-permute-start.10 = (bf16[192,896]{1,0:T(8,128)(2,1)}, bf16[192,896]{1,0:T(8,128)(2,1)S(1)}, u32[]{:S(2)}, u32[]{:S(2)}) collective-permute-start(bf16[192,896]{1,0:T(8,128)(2,1)} %get-tuple-element.28), channel_id=1, source_target_pairs={{0,16},{1,65},{2,18},{3,67},{4,20},{5,69},{6,22},{7,71},{8,24},{9,... | collective-permute-start | bytes 1032200 | tf_op jit(solution)/shard_map/ppermute | solution.py:360
  47.0 14.1 %copy-start.8 = (bf16[576,896]{1,0:T(8,128)(2,1)}, bf16[576,896]{1,0:T(8,128)(2,1)S(1)}, u32[]{:S(2)}) copy-start(bf16[576,896]{1,0:T(8,128)(2,1)S(1)} %collective-permute-done.4.refs_1_) | copy-start | bytes 3096580
  47.0 20.6 %copy-start.2 = (bf16[192,896]{1,0:T(8,128)(2,1)S(1)}, bf16[192,896]{1,0:T(8,128)(2,1)}, u32[]{:S(2)}) copy-start(bf16[192,896]{1,0:T(8,128)(2,1)} %get-tuple-element.26.refs_0_.refs_4_) | copy-start | bytes 1032196
  47.0 20.6 %collective-permute-start.11 = (bf16[192,896]{1,0:T(8,128)(2,1)}, bf16[192,896]{1,0:T(8,128)(2,1)S(1)}, u32[]{:S(2)}, u32[]{:S(2)}) collective-permute-start(bf16[192,896]{1,0:T(8,128)(2,1)} %get-tuple-element.29), channel_id=1, source_target_pairs={{0,24},{1,97},{2,26},{3,99},{4,28},{5,101},{6,30},{7,103},{8,0},{9... | collective-permute-start | bytes 1032200 | tf_op jit(solution)/shard_map/ppermute | solution.py:360
  61.1 27.6 %copy-start = (bf16[384,896]{1,0:T(8,128)(2,1)S(1)}, bf16[384,896]{1,0:T(8,128)(2,1)}, u32[]{:S(2)}) copy-start(bf16[384,896]{1,0:T(8,128)(2,1)} %tok_ref.3) | copy-start | bytes 2064388
  61.1 33.1 %copy-start.1 = (bf16[896,256]{1,0:T(8,128)(2,1)S(1)}, bf16[896,256]{1,0:T(8,128)(2,1)}, u32[]{:S(2)}) copy-start(bf16[896,256]{1,0:T(8,128)(2,1)} %w_ref.3) | copy-start | bytes 1376260
  61.1 1.0 copy-start.9
  62.1 1.0 copy-start.10
  67.6 26.6 %copy-start.3 = (bf16[192,896]{1,0:T(8,128)(2,1)}, bf16[192,896]{1,0:T(8,128)(2,1)S(1)}, u32[]{:S(2)}) copy-start(bf16[192,896]{1,0:T(8,128)(2,1)S(1)} %collective-permute-done.9.refs_1_.refs_5_) | copy-start | bytes 1032196
  67.6 26.5 %copy-start.4 = (bf16[192,896]{1,0:T(8,128)(2,1)}, bf16[192,896]{1,0:T(8,128)(2,1)S(1)}, u32[]{:S(2)}) copy-start(bf16[192,896]{1,0:T(8,128)(2,1)S(1)} %collective-permute-done.10.refs_2_.refs_6_) | copy-start | bytes 1032196
  67.6 26.5 %copy-start.5 = (bf16[192,896]{1,0:T(8,128)(2,1)}, bf16[192,896]{1,0:T(8,128)(2,1)S(1)}, u32[]{:S(2)}) copy-start(bf16[192,896]{1,0:T(8,128)(2,1)S(1)} %collective-permute-done.11.refs_3_.refs_7_) | copy-start | bytes 1032196
  90.6 14.4 %all-to-all-start.2 = ((bf16[16,16,896]{2,1,0:T(8,128)(2,1)}), bf16[16,16,896]{2,1,0:T(8,128)(2,1)S(1)}, u32[]{:S(2)}, u32[]{:S(2)}) async-start(bf16[16,16,896]{2,1,0:T(8,128)(2,1)} %bitcast.2), calls=%async_computation.2 | async-start | bytes 917504 | tf_op jit(solution)/shard_map/all_to_all | solution.py:439

commit v4 on v3

--- a/solution.py
+++ b/solution.py
@@ -11,6 +11,8 @@
 route_scale = 2.5
 AXES = ("expert", "width")
 f32, bf16, i32 = jnp.float32, jnp.bfloat16, jnp.int32
+PARTS = (((2,), (1, 3), (0,)), ((2, 1, 3, 0),))
+DOTS = ((0,), (2,), (1, 3))
 VMEM = pl.BlockSpec(memory_space=pltpu.VMEM)
 SMEM = pl.BlockSpec(memory_space=pltpu.SMEM)
 ANY = pl.BlockSpec(memory_space=pl.ANY)
@@ -79,8 +81,8 @@
     copies[3].wait()
 
 
-def compact_kernel(parts, tok, cap, n_dest, halves, *refs):
-    n_in, n_half = sum(parts), len(halves)
+def compact_kernel(parts, tok, cap, dests, halves, *refs):
+    n_in, n_half, n_dest = sum(parts), len(halves), len(dests)
     x_refs, (stage, sem) = refs[:n_in], refs[-2:]
     out_refs, half_refs = refs[-2 - n_half - n_dest : -2 - n_half], refs[-2 - n_half : -2]
     place = here()
@@ -89,7 +91,7 @@
         part = x_refs[j].at[pl.ds(first, rows), :]
         copies.append(pltpu.make_async_copy(part, half_refs[at], sem.at[n_dest + at]))
         copies[-1].start()
-    for d in list(range(1, n_dest)) + [0]:
+    for out, d in enumerate(dests):
         at = 0
         for j, count in enumerate(parts):
             mine_refs = x_refs[at : at + count]
@@ -108,20 +110,20 @@
                 term = jnp.dot(table, ref[:rows, :], preferred_element_type=f32)
                 got = term if got is None else got + term
                 first += rows
-            stage[d, j * cap : (j + 1) * cap, :] = got.astype(bf16)
-        copies.append(pltpu.make_async_copy(stage.at[d], out_refs[d], sem.at[d]))
+            stage[out, j * cap : (j + 1) * cap, :] = got.astype(bf16)
+        copies.append(pltpu.make_async_copy(stage.at[out], out_refs[out], sem.at[out]))
         copies[-1].start()
     for copy in copies:
         copy.wait()
 
 
-def compact(sources, after, tok, cap, n_dest, halves=()):
-    n_src, width = len(sources), sources[0][0].shape[1]
+def compact(sources, after, tok, cap, dests, halves=()):
+    n_src, width, n_dest = len(sources), sources[0][0].shape[1], len(dests)
     xs = sum(sources, [])
     outs = [pltpu.HBM((n_src * cap, width), bf16)] * n_dest
     outs += [pltpu.HBM((rows, width), bf16) for _, rows, _ in halves]
     return pl.pallas_call(
-        functools.partial(compact_kernel, [len(x) for x in sources], tok, cap, n_dest, halves),
+        functools.partial(compact_kernel, [len(x) for x in sources], tok, cap, dests, halves),
         out_shape=outs,
         in_specs=[VMEM] * len(xs) + [HBM] * len(after),
         out_specs=[HBM] * len(outs),
@@ -227,17 +229,17 @@
     return copies
 
 
-def cells_of(batch, side, place):
-    return [cell(place, -s, -d) for d in range(side) for s in batch]
-
-
-def dots_kernel(batch, side, cap, next_batch, eo_ref, *refs):
-    chunk_refs = refs[:side]
-    out_refs, (held, stage, sem, next_sem) = refs[side:-4], refs[-4:]
+def cells_of(batch, dests, place):
+    return [cell(place, -s, -d) for d in dests for s in batch]
+
+
+def dots_kernel(batch, dests, cap, ahead_cells, eo_ref, *refs):
+    chunk_refs = refs[: len(dests)]
+    out_refs, (held, stage, sem, next_sem) = refs[len(dests) : -4], refs[-4:]
     place = here()
     rows = fetch_chunks(chunk_refs, held, sem.at[0], cap)
-    others = fetch(eo_ref, stage, sem.at[1], cells_of(batch, side, place), cap)
-    ahead = fetch(eo_ref, out_refs[1], next_sem, cells_of(next_batch, side, place), cap) if next_batch else []
+    others = fetch(eo_ref, stage, sem.at[1], cells_of(batch, dests, place), cap)
+    ahead = fetch(eo_ref, out_refs[1], next_sem, cells_of(*ahead_cells, place), cap) if ahead_cells else []
     for at in range(len(rows)):
         rows[at].wait()
         others[at].wait()
@@ -246,16 +248,16 @@
         copy.wait()
 
 
-def row_dots_call(batch, next_batch, eo, chunks, cap):
-    n, width, side = len(batch) * len(chunks), chunks[0].shape[1], len(chunks)
-    n_next = len(next_batch) * side
+def row_dots_call(batch, dests, ahead_cells, eo, chunks, cap):
+    n, width = len(batch) * len(dests), chunks[0].shape[1]
+    n_next = len(ahead_cells[0]) * len(ahead_cells[1]) if ahead_cells else 0
     outs = [jax.ShapeDtypeStruct((n, cap), f32)]
     if n_next:
         outs.append(pltpu.VMEM((n_next, cap, width), bf16))
     return pl.pallas_call(
-        functools.partial(dots_kernel, batch, side, cap, next_batch),
+        functools.partial(dots_kernel, batch, dests, cap, ahead_cells),
         out_shape=outs,
-        in_specs=[HBM] * (1 + side),
+        in_specs=[HBM] * (1 + len(dests)),
         out_specs=[VMEM] * len(outs),
         scratch_shapes=[
             pltpu.VMEM((n, cap, width), bf16),
@@ -263,13 +265,13 @@
             pltpu.SemaphoreType.DMA((2, n)),
             pltpu.SemaphoreType.DMA((max(n_next, 1),)),
         ],
-        compiler_params=params(12),
+        compiler_params=params(8),
         cost_estimate=cost(2 * n * cap * width, 4 * n * cap * width),
         name="dots",
     )(in_hbm(eo), *map(in_hbm, chunks))
 
 
-def last_dots_kernel(n_width, batches, side, gate_ref, eo_ref, *refs):
+def last_dots_kernel(n_width, groups, last, side, gate_ref, eo_ref, *refs):
     chunk_refs, early_refs, out_ref = refs[:side], refs[side:-1], refs[-1]
     n_expert = gate_ref.shape[0]
     place = here()
@@ -282,10 +284,10 @@
         for w in range(n_width):
             out_ref[base + 2 * w] = row
 
-    for batch, early in zip(batches[:-1], early_refs):
-        for at, src in enumerate(cells_of(batch, side, place)):
+    for (batch, dests), early in zip(groups, early_refs):
+        for at, src in enumerate(cells_of(batch, dests, place)):
             put(src, early[at : at + 1, :])
-    for at, src in enumerate(cells_of(batches[-1], side, place)):
+    for at, src in enumerate(cells_of(last, range(side), place)):
         put(src, row_dots(chunk_refs[at], eo_ref.at[at]))
 
 
@@ -330,7 +332,7 @@
     place = here()
     rows = fetch_chunks(chunk_refs, held, in_sem, cap)
     copies = []
-    cells = sum([cells_of(batch, side, place) for batch in batches], [])
+    cells = sum([cells_of(batch, range(side), place) for batch in batches], [])
     for at, src in enumerate(cells):
         gate = jnp.broadcast_to(got_ref[src * (2 * n_width) + 1], (128, cap)).T
         rows[at].wait()
@@ -390,12 +392,13 @@
     parts = lax.all_to_all(sent_parts, "width", 0, 0, tiled=True)
 
     landed, after = [], []
-    for batch in batches:
-        chunks = compact([sources[s] for s in batch], after, tok, cap, side)
-        after = [chunks[0]]
-        group = [chunks[0]]
-        for d in range(1, side):
-            group.append(send(chunks[d], d, True))
+    for b, batch in enumerate(batches):
+        group = [None] * side
+        for dests in PARTS[b]:
+            chunks = compact([sources[s] for s in batch], after, tok, cap, dests)
+            after = [chunks[0]]
+            for d, chunk in zip(dests, chunks):
+                group[d] = chunk if d == 0 else send(chunk, d, True)
         landed.append(group)
 
     gates = pl.pallas_call(
@@ -408,20 +411,23 @@
         name="gates",
     )(parts, ids, slots)
 
-    early = []
+    early, groups, ahead = [], [], None
     for b, batch in enumerate(batches[:-1]):
-        next_batch = batches[-1] if b == len(batches) - 2 else []
-        outs = row_dots_call(batch, next_batch, expert_out, landed[b], cap)
-        early.append(outs[0])
+        for dests in DOTS:
+            ahead_cells = (batches[-1], range(side)) if ahead is None else ()
+            outs = row_dots_call(batch, dests, ahead_cells, expert_out, [landed[b][d] for d in dests], cap)
+            ahead = outs[1] if ahead is None else ahead
+            early.append(outs[0])
+            groups.append((batch, dests))
     sent = pl.pallas_call(
-        functools.partial(last_dots_kernel, n_width, batches, side),
+        functools.partial(last_dots_kernel, n_width, groups, batches[-1], side),
         out_shape=jax.ShapeDtypeStruct((2 * n_expert * n_width, 1, cap), f32),
         in_specs=[VMEM] * (2 + side + len(early)),
         out_specs=VMEM,
         compiler_params=params(6),
         cost_estimate=cost(2 * side * cap * width, 4 * side * cap * width),
         name="last_dots",
-    )(gates, outs[1], *landed[-1], *early)
+    )(gates, ahead, *landed[-1], *early)
     got = lax.all_to_all(sent, AXES, 0, 0, tiled=True)
 
     logit_grads, router_part = pl.pallas_call(

time: 106 us -> 106 us (level)
  Pallas kernels: 22.6 us -> 27.2 us
  waiting for transfers between devices: 27.2 us -> 24.7 us
  blocking collectives: 30.4 us -> 28.5 us
    ppermute x12, waiting for transfers between devices: 22.7 us -> 20.1 us  [send(): return lax.ppermute(x, AXES, line_shift(n_expert, n_width, shift, second))]
    pallas_call x2 -> x4, Pallas kernels: 5.54 us -> 7.94 us  [compact(): pl.pallas_call(functools.partial(compact_kernel, [len(x) for x in sources...]
    pallas_call x2 -> x4, Pallas kernels: 5.01 us -> 7.22 us  [the longest x3 6.73 us: row_dots_call(): pl.pallas_call(functools.partial(dots_kernel, batch, dests, cap, ahead_ce...]
    all_to_all x1, blocking collectives: 20.5 us -> 18.6 us  [body(): got = lax.all_to_all(sent, AXES, 0, 0, tiled=True)]
  transfers between devices with their start and end apart: 13 -> 13, of which waited for: 5 -> 4; matrix products, arithmetic and copies ran while one was open for 0% -> 0% of each run, Pallas kernels for 14% -> 21%
where the time goes in v4:
time: 106 us; the launch traced here: 105 us
  blocking collectives  28.5 us (27%)
  Pallas kernels  27.2 us (26%)
  waiting for transfers between devices  24.7 us (23%)
  starting transfers between devices  21.4 us (20%)
  local copies, waits for them, and re-layouts  1.97 us (2%)
    ppermute x12, waiting for transfers between devices, send(): return lax.ppermute(x, AXES, line_shift(n_expert, n_width, shift, second))  20.1 us
    all_to_all x1, blocking collectives, body(): got = lax.all_to_all(sent, AXES, 0, 0, tiled=True)  18.6 us
    ppermute x12, starting transfers between devices, send(): return lax.ppermute(x, AXES, line_shift(n_expert, n_width, shift, second))  17.9 us
    all_to_all x1, blocking collectives, body(): parts = lax.all_to_all(sent_parts, 'width', 0, 0, tiled=True)  9.92 us
    pallas_call x4, Pallas kernels, compact(): pl.pallas_call(functools.partial(compact_kernel, [len(x) for x in sources...  7.94 us
    pallas_call x3, Pallas kernels, row_dots_call(): pl.pallas_call(functools.partial(dots_kernel, batch, dests, cap, ahead_ce...  6.73 us
    pallas_call x1, Pallas kernels, body(): pl.pallas_call(functools.partial(scale_kernel, n_width, batches, cap, sid...  6.25 us
    all_to_all x1, waiting for transfers between devices, body(): lax.all_to_all(router_part.reshape(n_expert, per_device, width), 'expert'...  4.53 us
  transfers between devices with their start and end apart: 13, of which 4 were waited for; matrix products, arithmetic and copies ran while one was open for 0% of the time, Pallas kernels for 21%

profile of v4, /device:TPU:0, one launch (start us, length us, event | category | flops | bytes accessed | tf_op | source)
XLA Modules:
  0.0 105.4 jit_solution(13729320633131973391)
XLA Ops:
  1.8 3.2 %collective-permute-start.3 = (bf16[200,896]{1,0:T(8,128)(2,1)S(1)}, bf16[200,896]{1,0:T(8,128)(2,1)S(1)}, u32[]{:S(2)}, u32[]{:S(2)}) collective-permute-start(bf16[200,896]{1,0:T(8,128)(2,1)S(1)} %get-tuple-element.18.refs_1_), channel_id=1, source_target_pairs={{0,96},{1,25},{2,98},{3,27},{4,100},{5,29},{6,102},{7,31},{8,104},... | collective-permute-start | bytes 1075208 | tf_op jit(solution)/shard_map/ppermute | solution.py:362
  5.0 3.2 %collective-permute-start.2 = (bf16[192,896]{1,0:T(8,128)(2,1)S(1)}, bf16[192,896]{1,0:T(8,128)(2,1)S(1)}, u32[]{:S(2)}, u32[]{:S(2)}) collective-permute-start(bf16[192,896]{1,0:T(8,128)(2,1)S(1)} %get-tuple-element.17.refs_0_), channel_id=1, source_target_pairs={{0,96},{1,25},{2,98},{3,27},{4,100},{5,29},{6,102},{7,31},{8,104},... | collective-permute-start | bytes 1032200 | tf_op jit(solution)/shard_map/ppermute | solution.py:362
  8.2 5.4 %collective-permute-done.2.refs_4_ = bf16[192,896]{1,0:T(8,128)(2,1)S(1)} collective-permute-done((bf16[192,896]{1,0:T(8,128)(2,1)S(1)}, bf16[192,896]{1,0:T(8,128)(2,1)S(1)}, u32[]{:S(2)}, u32[]{:S(2)}) %collective-permute-start.2) | collective-permute-done | bytes 344096 | tf_op jit(solution)/shard_map/ppermute | solution.py:362
  13.6 3.7 %collective-permute-done.refs_2_ = bf16[192,896]{1,0:T(8,128)(2,1)S(1)} collective-permute-done((bf16[192,896]{1,0:T(8,128)(2,1)S(1)}, bf16[192,896]{1,0:T(8,128)(2,1)S(1)}, u32[]{:S(2)}, u32[]{:S(2)}) %collective-permute-start) | collective-permute-done | bytes 344096 | tf_op jit(solution)/shard_map/ppermute | solution.py:362
  17.3 1.8 %compact.4.refs_6_ = bf16[576,896]{1,0:T(8,128)(2,1)} custom-call(bf16[192,896]{1,0:T(8,128)(2,1)S(1)} %get-tuple-element.17.refs_0_, bf16[200,896]{1,0:T(8,128)(2,1)S(1)} %get-tuple-element.18.refs_1_, bf16[192,896]{1,0:T(8,128)(2,1)S(1)} %collective-permute-done.refs_2_, bf16[200,896]{1,0:T(8,128)(2,1)S(1)} %collective-permute-done.1.refs_3_, ...), custom_call_target="tpu_custom_call" | custom-call | flops 396361728 | bytes 6193152 | tf_op jit(solution)/shard_map/compact/pallas_call | solution.py:125
  19.2 3.9 %collective-permute-start.9 = (bf16[576,896]{1,0:T(8,128)(2,1)}, bf16[576,896]{1,0:T(8,128)(2,1)S(1)}, u32[]{:S(2)}, u32[]{:S(2)}) collective-permute-start(bf16[576,896]{1,0:T(8,128)(2,1)} %compact.4.refs_6_), channel_id=1, source_target_pairs={{0,16},{1,65},{2,18},{3,67},{4,20},{5,69},{6,22},{7,71},{8,24},{9,... | collective-permute-start | bytes 3096584 | tf_op jit(solution)/shard_map/ppermute | solution.py:362
  23.1 2.5 %compact.5 = (bf16[576,896]{1,0:T(8,128)(2,1)}, bf16[576,896]{1,0:T(8,128)(2,1)}) custom-call(bf16[192,896]{1,0:T(8,128)(2,1)S(1)} %get-tuple-element.17.refs_0_, bf16[200,896]{1,0:T(8,128)(2,1)S(1)} %get-tuple-element.18.refs_1_, bf16[192,896]{1,0:T(8,128)(2,1)S(1)} %collective-permute-done.refs_2_, bf16[200,896]{1,0:T(8,128)(2,1)S(1)} %collective-permute-done.1.refs_3_, ...), custom_call_target="tpu_custom_call" | custom-call | flops 792723456 | bytes 6193152 | tf_op jit(solution)/shard_map/compact/pallas_call | solution.py:125
  26.3 1.3 %collective-permute-start.10 = (bf16[576,896]{1,0:T(8,128)(2,1)}, bf16[576,896]{1,0:T(8,128)(2,1)S(1)}, u32[]{:S(2)}, u32[]{:S(2)}) collective-permute-start(bf16[576,896]{1,0:T(8,128)(2,1)} %get-tuple-element.19.refs_6_), channel_id=1, source_target_pairs={{0,8},{1,33},{2,10},{3,35},{4,12},{5,37},{6,14},{7,39},{8,16},{9,4... | collective-permute-start | bytes 3096584 | tf_op jit(solution)/shard_map/ppermute | solution.py:362
  27.7 2.0 %collective-permute-start.4 = (bf16[192,896]{1,0:T(8,128)(2,1)S(1)}, bf16[192,896]{1,0:T(8,128)(2,1)S(1)}, u32[]{:S(2)}, u32[]{:S(2)}) collective-permute-start(bf16[192,896]{1,0:T(8,128)(2,1)S(1)} %collective-permute-done.refs_2_), channel_id=1, source_target_pairs={{0,32},{1,9},{2,34},{3,11},{4,36},{5,13},{6,38},{7,15},{8,40},{9,1... | collective-permute-start | bytes 1032200 | tf_op jit(solution)/shard_map/ppermute | solution.py:362
  29.7 1.9 %compact.6.refs_0_.refs_2_ = bf16[576,896]{1,0:T(8,128)(2,1)} custom-call(bf16[192,896]{1,0:T(8,128)(2,1)S(1)} %get-tuple-element.17.refs_0_, bf16[200,896]{1,0:T(8,128)(2,1)S(1)} %get-tuple-element.18.refs_1_, bf16[192,896]{1,0:T(8,128)(2,1)S(1)} %collective-permute-done.refs_2_, bf16[200,896]{1,0:T(8,128)(2,1)S(1)} %collective-permute-done.1.refs_3_, ...), custom_call_target="tpu_custom_call" | custom-call | flops 396361728 | bytes 6193152 | tf_op jit(solution)/shard_map/compact/pallas_call | solution.py:125
  31.5 11.1 %collective-permute-done.4.refs_0_ = bf16[192,896]{1,0:T(8,128)(2,1)S(1)} collective-permute-done((bf16[192,896]{1,0:T(8,128)(2,1)S(1)}, bf16[192,896]{1,0:T(8,128)(2,1)S(1)}, u32[]{:S(2)}, u32[]{:S(2)}) %collective-permute-start.4) | collective-permute-done | bytes 344096 | tf_op jit(solution)/shard_map/ppermute | solution.py:362
  42.6 1.8 %compact.7 = (bf16[192,896]{1,0:T(8,128)(2,1)}, bf16[192,896]{1,0:T(8,128)(2,1)}, bf16[192,896]{1,0:T(8,128)(2,1)}, bf16[192,896]{1,0:T(8,128)(2,1)}) custom-call(bf16[192,896]{1,0:T(8,128)(2,1)S(1)} %collective-permute-done.4.refs_0_, bf16[200,896]{1,0:T(8,128)(2,1)S(1)} %collective-permute-done.5.refs_1_, bf16[576,896]{1,0:T(8,128)(2,1)} %compact.6.refs_0_.refs_2_), custom_call_target="tpu_custom_call" | custom-call | flops 528482304 | bytes 2064384 | tf_op jit(solution)/shard_map/compact/pallas_call | solution.py:125
  44.5 1.8 %collective-permute-start.7 = (bf16[192,896]{1,0:T(8,128)(2,1)}, bf16[192,896]{1,0:T(8,128)(2,1)S(1)}, u32[]{:S(2)}, u32[]{:S(2)}) collective-permute-start(bf16[192,896]{1,0:T(8,128)(2,1)} %get-tuple-element.23), channel_id=1, source_target_pairs={{0,16},{1,65},{2,18},{3,67},{4,20},{5,69},{6,22},{7,71},{8,24},{9,... | collective-permute-start | bytes 1032200 | tf_op jit(solution)/shard_map/ppermute | solution.py:362
  46.3 1.5 %collective-permute-start.8 = (bf16[192,896]{1,0:T(8,128)(2,1)}, bf16[192,896]{1,0:T(8,128)(2,1)S(1)}, u32[]{:S(2)}, u32[]{:S(2)}) collective-permute-start(bf16[192,896]{1,0:T(8,128)(2,1)} %get-tuple-element.24), channel_id=1, source_target_pairs={{0,24},{1,97},{2,26},{3,99},{4,28},{5,101},{6,30},{7,103},{8,0},{9... | collective-permute-start | bytes 1032200 | tf_op jit(solution)/shard_map/ppermute | solution.py:362
  47.8 2.2 %picked.1 = f32[8,8,384]{2,1,0:T(8,128)S(1)} custom-call(s32[8,384]{1,0:T(8,128)} %bitcast.5, bf16[384,896]{1,0:T(8,128)(2,1)} %tok_ref.3, bf16[896,256]{1,0:T(8,128)(2,1)} %w_ref.3), custom_call_target="tpu_custom_call" | custom-call | flops 176160768 | bytes 688128 | tf_op jit(solution)/shard_map/picked/pallas_call | solution.py:165
  50.0 9.9 %all_to_all.15.parts_ref = f32[8,8,384]{2,1,0:T(8,128)S(1)} all-to-all(f32[8,8,384]{2,1,0:T(8,128)S(1)} %picked.1), channel_id=1, replica_groups=mesh['expert'=16,'width'=8] {'width'}, dimensions={0} | all-to-all | bytes 196608 | tf_op jit(solution)/shard_map/all_to_all | solution.py:392
  60.4 2.1 %dots.3 = (f32[3,192]{1,0:T(4,128)S(1)}, bf16[4,192,896]{2,1,0:T(8,128)(2,1)S(1)}) custom-call(bf16[3072,896]{1,0:T(8,128)(2,1)} %eo_ref.5, bf16[576,896]{1,0:T(8,128)(2,1)} %compact.6.refs_0_.refs_2_), custom_call_target="tpu_custom_call" | custom-call | flops 1032192 | bytes 2064384 | tf_op jit(solution)/shard_map/dots/pallas_call | solution.py:257
  62.5 1.9 %dots.4.refs_5_ = f32[3,192]{1,0:T(4,128)S(1)} custom-call(bf16[3072,896]{1,0:T(8,128)(2,1)} %eo_ref.5, bf16[576,896]{1,0:T(8,128)(2,1)} %copy-done.8), custom_call_target="tpu_custom_call" | custom-call | flops 1032192 | bytes 2064384 | tf_op jit(solution)/shard_map/dots/pallas_call | solution.py:257
  66.4 2.7 %dots.5.refs_6_ = f32[6,192]{1,0:T(8,128)S(1)} custom-call(bf16[3072,896]{1,0:T(8,128)(2,1)} %eo_ref.5, bf16[576,896]{1,0:T(8,128)(2,1)} %copy-done.10, bf16[576,896]{1,0:T(8,128)(2,1)} %copy-done.9), custom_call_target="tpu_custom_call" | custom-call | flops 2064384 | bytes 4128768 | tf_op jit(solution)/shard_map/dots/pallas_call | solution.py:257
  69.7 18.6 %all_to_all.16.got_ref = f32[256,1,192]{2,1,0:T(1,128)S(1)} all-to-all(f32[256,1,192]{2,1,0:T(1,128)S(1)} %last_dots.1), channel_id=1, replica_groups=mesh['expert'=16,'width'=8] {'expert','width'}, dimensions={0} | all-to-all | bytes 393216 | tf_op jit(solution)/shard_map/all_to_all | solution.py:431
  88.4 1.9 %tail.1 = (bf16[256,384]{1,0:T(8,128)(2,1)S(1)}, bf16[256,896]{1,0:T(8,128)(2,1)}) custom-call(f32[256,1,192]{2,1,0:T(1,128)S(1)} %all_to_all.16.got_ref, f32[8,8,384]{2,1,0:T(8,128)S(1)} %all_to_all.15.parts_ref, s32[8,384]{1,0:T(8,128)S(1)} %bitcast.7, s32[8,384]{1,0:T(8,128)S(1)} %bitcast.10, bf16[384,896]{1,0:T(8,128)(2,1)S(1)} %copy-done), custom_call_target="tpu_custom_call" | custom-call | flops 176160768 | bytes 688128 | tf_op jit(solution)/shard_map/tail/pallas_call | solution.py:433
  90.3 3.6 %all-to-all-start.2 = ((bf16[16,16,896]{2,1,0:T(8,128)(2,1)}), bf16[16,16,896]{2,1,0:T(8,128)(2,1)S(1)}, u32[]{:S(2)}, u32[]{:S(2)}) async-start(bf16[16,16,896]{2,1,0:T(8,128)(2,1)} %bitcast.2), calls=%async_computation.2 | async-start | bytes 917504 | tf_op jit(solution)/shard_map/all_to_all | solution.py:445
  93.9 6.3 %scale.1 = (bf16[3072,896]{1,0:T(8,128)(2,1)}, bf16[384,896]{1,0:T(8,128)(2,1)}) custom-call(f32[256,1,192]{2,1,0:T(1,128)S(1)} %all_to_all.16.got_ref, bf16[256,384]{1,0:T(8,128)(2,1)S(1)} %get-tuple-element.27.lg_ref, bf16[896,256]{1,0:T(8,128)(2,1)S(1)} %copy-done.1, bf16[576,896]{1,0:T(8,128)(2,1)} %compact.6.refs_0_.refs_2_, ...), custom_call_target="tpu_custom_call" | custom-call | flops 176160768 | bytes 11010048 | tf_op jit(solution)/shard_map/scale/pallas_call | solution.py:447
  100.2 4.5 %all-to-all-done.2 = bf16[16,16,896]{2,1,0:T(8,128)(2,1)S(1)} async-done(((bf16[16,16,896]{2,1,0:T(8,128)(2,1)}), bf16[16,16,896]{2,1,0:T(8,128)(2,1)S(1)}, u32[]{:S(2)}, u32[]{:S(2)}) %all-to-all-start.2) | async-done | bytes 458784 | tf_op jit(solution)/shard_map/all_to_all | solution.py:445
  (40 shorter events, 5.7 us)
Async XLA Ops:
  1.8 15.5 %collective-permute-start.3 = (bf16[200,896]{1,0:T(8,128)(2,1)S(1)}, bf16[200,896]{1,0:T(8,128)(2,1)S(1)}, u32[]{:S(2)}, u32[]{:S(2)}) collective-permute-start(bf16[200,896]{1,0:T(8,128)(2,1)S(1)} %get-tuple-element.18.refs_1_), channel_id=1, source_target_pairs={{0,96},{1,25},{2,98},{3,27},{4,100},{5,29},{6,102},{7,31},{8,104},... | collective-permute-start | bytes 1075208 | tf_op jit(solution)/shard_map/ppermute | solution.py:362
  5.0 12.3 %collective-permute-start.1 = (bf16[200,896]{1,0:T(8,128)(2,1)S(1)}, bf16[200,896]{1,0:T(8,128)(2,1)S(1)}, u32[]{:S(2)}, u32[]{:S(2)}) collective-permute-start(bf16[200,896]{1,0:T(8,128)(2,1)S(1)} %get-tuple-element.18.refs_1_), channel_id=1, source_target_pairs={{0,32},{1,9},{2,34},{3,11},{4,36},{5,13},{6,38},{7,15},{8,40},{9,1... | collective-permute-start | bytes 1075208 | tf_op jit(solution)/shard_map/ppermute | solution.py:362
  5.0 8.6 %collective-permute-start.2 = (bf16[192,896]{1,0:T(8,128)(2,1)S(1)}, bf16[192,896]{1,0:T(8,128)(2,1)S(1)}, u32[]{:S(2)}, u32[]{:S(2)}) collective-permute-start(bf16[192,896]{1,0:T(8,128)(2,1)S(1)} %get-tuple-element.17.refs_0_), channel_id=1, source_target_pairs={{0,96},{1,25},{2,98},{3,27},{4,100},{5,29},{6,102},{7,31},{8,104},... | collective-permute-start | bytes 1032200 | tf_op jit(solution)/shard_map/ppermute | solution.py:362
  8.2 9.1 %collective-permute-start = (bf16[192,896]{1,0:T(8,128)(2,1)S(1)}, bf16[192,896]{1,0:T(8,128)(2,1)S(1)}, u32[]{:S(2)}, u32[]{:S(2)}) collective-permute-start(bf16[192,896]{1,0:T(8,128)(2,1)S(1)} %get-tuple-element.17.refs_0_), channel_id=1, source_target_pairs={{0,32},{1,9},{2,34},{3,11},{4,36},{5,13},{6,38},{7,15},{8,40},{9,1... | collective-permute-start | bytes 1032200 | tf_op jit(solution)/shard_map/ppermute | solution.py:362
  19.1 40.8 %copy-start.6 = (s32[384,8]{0,1:T(8,128)S(1)}, s32[384,8]{0,1:T(8,128)}, u32[]{:S(2)}) copy-start(s32[384,8]{0,1:T(8,128)} %param.10) | copy-start | bytes 36868
  19.1 40.8 %copy-start.7 = (s32[384,8]{0,1:T(8,128)S(1)}, s32[384,8]{0,1:T(8,128)}, u32[]{:S(2)}) copy-start(s32[384,8]{0,1:T(8,128)} %param.11) | copy-start | bytes 36868
  19.2 27.1 %collective-permute-start.9 = (bf16[576,896]{1,0:T(8,128)(2,1)}, bf16[576,896]{1,0:T(8,128)(2,1)S(1)}, u32[]{:S(2)}, u32[]{:S(2)}) collective-permute-start(bf16[576,896]{1,0:T(8,128)(2,1)} %compact.4.refs_6_), channel_id=1, source_target_pairs={{0,16},{1,65},{2,18},{3,67},{4,20},{5,69},{6,22},{7,71},{8,24},{9,... | collective-permute-start | bytes 3096584 | tf_op jit(solution)/shard_map/ppermute | solution.py:362
  25.6 38.9 %collective-permute-start.11 = (bf16[576,896]{1,0:T(8,128)(2,1)}, bf16[576,896]{1,0:T(8,128)(2,1)S(1)}, u32[]{:S(2)}, u32[]{:S(2)}) collective-permute-start(bf16[576,896]{1,0:T(8,128)(2,1)} %get-tuple-element.26), channel_id=1, source_target_pairs={{0,24},{1,97},{2,26},{3,99},{4,28},{5,101},{6,30},{7,103},{8,0},{9... | collective-permute-start | bytes 3096584 | tf_op jit(solution)/shard_map/ppermute | solution.py:362
  26.3 38.2 %collective-permute-start.10 = (bf16[576,896]{1,0:T(8,128)(2,1)}, bf16[576,896]{1,0:T(8,128)(2,1)S(1)}, u32[]{:S(2)}, u32[]{:S(2)}) collective-permute-start(bf16[576,896]{1,0:T(8,128)(2,1)} %get-tuple-element.19.refs_6_), channel_id=1, source_target_pairs={{0,8},{1,33},{2,10},{3,35},{4,12},{5,37},{6,14},{7,39},{8,16},{9,4... | collective-permute-start | bytes 3096584 | tf_op jit(solution)/shard_map/ppermute | solution.py:362
  27.6 14.9 %collective-permute-start.5 = (bf16[200,896]{1,0:T(8,128)(2,1)S(1)}, bf16[200,896]{1,0:T(8,128)(2,1)S(1)}, u32[]{:S(2)}, u32[]{:S(2)}) collective-permute-start(bf16[200,896]{1,0:T(8,128)(2,1)S(1)} %collective-permute-done.3.refs_5_), channel_id=1, source_target_pairs={{0,96},{1,25},{2,98},{3,27},{4,100},{5,29},{6,102},{7,31},{8,104},... | collective-permute-start | bytes 1075208 | tf_op jit(solution)/shard_map/ppermute | solution.py:362
  27.7 14.9 %collective-permute-start.4 = (bf16[192,896]{1,0:T(8,128)(2,1)S(1)}, bf16[192,896]{1,0:T(8,128)(2,1)S(1)}, u32[]{:S(2)}, u32[]{:S(2)}) collective-permute-start(bf16[192,896]{1,0:T(8,128)(2,1)S(1)} %collective-permute-done.refs_2_), channel_id=1, source_target_pairs={{0,32},{1,9},{2,34},{3,11},{4,36},{5,13},{6,38},{7,15},{8,40},{9,1... | collective-permute-start | bytes 1032200 | tf_op jit(solution)/shard_map/ppermute | solution.py:362
  44.4 24.8 %collective-permute-start.6 = (bf16[192,896]{1,0:T(8,128)(2,1)}, bf16[192,896]{1,0:T(8,128)(2,1)S(1)}, u32[]{:S(2)}, u32[]{:S(2)}) collective-permute-start(bf16[192,896]{1,0:T(8,128)(2,1)} %get-tuple-element.22), channel_id=1, source_target_pairs={{0,8},{1,33},{2,10},{3,35},{4,12},{5,37},{6,14},{7,39},{8,16},{9,4... | collective-permute-start | bytes 1032200 | tf_op jit(solution)/shard_map/ppermute | solution.py:362
  44.5 24.7 %collective-permute-start.7 = (bf16[192,896]{1,0:T(8,128)(2,1)}, bf16[192,896]{1,0:T(8,128)(2,1)S(1)}, u32[]{:S(2)}, u32[]{:S(2)}) collective-permute-start(bf16[192,896]{1,0:T(8,128)(2,1)} %get-tuple-element.23), channel_id=1, source_target_pairs={{0,16},{1,65},{2,18},{3,67},{4,20},{5,69},{6,22},{7,71},{8,24},{9,... | collective-permute-start | bytes 1032200 | tf_op jit(solution)/shard_map/ppermute | solution.py:362
  46.3 16.3 %copy-start.8 = (bf16[576,896]{1,0:T(8,128)(2,1)}, bf16[576,896]{1,0:T(8,128)(2,1)S(1)}, u32[]{:S(2)}) copy-start(bf16[576,896]{1,0:T(8,128)(2,1)S(1)} %collective-permute-done.9.refs_0_.refs_2_) | copy-start | bytes 3096580
  46.3 23.0 %collective-permute-start.8 = (bf16[192,896]{1,0:T(8,128)(2,1)}, bf16[192,896]{1,0:T(8,128)(2,1)S(1)}, u32[]{:S(2)}, u32[]{:S(2)}) collective-permute-start(bf16[192,896]{1,0:T(8,128)(2,1)} %get-tuple-element.24), channel_id=1, source_target_pairs={{0,24},{1,97},{2,26},{3,99},{4,28},{5,101},{6,30},{7,103},{8,0},{9... | collective-permute-start | bytes 1032200 | tf_op jit(solution)/shard_map/ppermute | solution.py:362
  62.5 6.7 %copy-start.2 = (bf16[192,896]{1,0:T(8,128)(2,1)S(1)}, bf16[192,896]{1,0:T(8,128)(2,1)}, u32[]{:S(2)}) copy-start(bf16[192,896]{1,0:T(8,128)(2,1)} %get-tuple-element.21.refs_0_.refs_4_) | copy-start | bytes 1032196
  64.5 23.9 %copy-start = (bf16[384,896]{1,0:T(8,128)(2,1)S(1)}, bf16[384,896]{1,0:T(8,128)(2,1)}, u32[]{:S(2)}) copy-start(bf16[384,896]{1,0:T(8,128)(2,1)} %tok_ref.3) | copy-start | bytes 2064388
  64.5 29.4 %copy-start.1 = (bf16[896,256]{1,0:T(8,128)(2,1)S(1)}, bf16[896,256]{1,0:T(8,128)(2,1)}, u32[]{:S(2)}) copy-start(bf16[896,256]{1,0:T(8,128)(2,1)} %w_ref.3) | copy-start | bytes 1376260
  64.5 1.0 copy-start.9
  65.5 1.0 copy-start.10
  69.2 24.7 %copy-start.3 = (bf16[192,896]{1,0:T(8,128)(2,1)}, bf16[192,896]{1,0:T(8,128)(2,1)S(1)}, u32[]{:S(2)}) copy-start(bf16[192,896]{1,0:T(8,128)(2,1)S(1)} %collective-permute-done.6.refs_1_.refs_5_) | copy-start | bytes 1032196
  69.2 24.6 %copy-start.4 = (bf16[192,896]{1,0:T(8,128)(2,1)}, bf16[192,896]{1,0:T(8,128)(2,1)S(1)}, u32[]{:S(2)}) copy-start(bf16[192,896]{1,0:T(8,128)(2,1)S(1)} %collective-permute-done.7.refs_2_.refs_6_) | copy-start | bytes 1032196
  69.2 24.6 %copy-start.5 = (bf16[192,896]{1,0:T(8,128)(2,1)}, bf16[192,896]{1,0:T(8,128)(2,1)S(1)}, u32[]{:S(2)}) copy-start(bf16[192,896]{1,0:T(8,128)(2,1)S(1)} %collective-permute-done.8.refs_3_.refs_7_) | copy-start | bytes 1032196
  90.3 14.4 %all-to-all-start.2 = ((bf16[16,16,896]{2,1,0:T(8,128)(2,1)}), bf16[16,16,896]{2,1,0:T(8,128)(2,1)S(1)}, u32[]{:S(2)}, u32[]{:S(2)}) async-start(bf16[16,16,896]{2,1,0:T(8,128)(2,1)} %bitcast.2), calls=%async_computation.2 | async-start | bytes 917504 | tf_op jit(solution)/shard_map/all_to_all | solution.py:445

commit v5 on v4

--- a/solution.py
+++ b/solution.py
@@ -11,7 +11,8 @@
 route_scale = 2.5
 AXES = ("expert", "width")
 f32, bf16, i32 = jnp.float32, jnp.bfloat16, jnp.int32
-PARTS = (((2,), (1, 3), (0,)), ((2, 1, 3, 0),))
+DIRECT = False
+PARTS = (((2,), (1,), (3,), (0,)), ((2,), (1, 3, 0)))
 DOTS = ((0,), (2,), (1, 3))
 VMEM = pl.BlockSpec(memory_space=pltpu.VMEM)
 SMEM = pl.BlockSpec(memory_space=pltpu.SMEM)
@@ -81,16 +82,12 @@
     copies[3].wait()
 
 
-def compact_kernel(parts, tok, cap, dests, halves, *refs):
-    n_in, n_half, n_dest = sum(parts), len(halves), len(dests)
-    x_refs, (stage, sem) = refs[:n_in], refs[-2:]
-    out_refs, half_refs = refs[-2 - n_half - n_dest : -2 - n_half], refs[-2 - n_half : -2]
+def compact_kernel(parts, tok, cap, dests, direct, *refs):
+    n_in, n_dest = sum(parts), len(dests)
+    x_refs = refs[:n_in]
+    out_refs = refs[n_in : n_in + n_dest]
     place = here()
     copies = []
-    for at, (j, rows, first) in enumerate(halves):
-        part = x_refs[j].at[pl.ds(first, rows), :]
-        copies.append(pltpu.make_async_copy(part, half_refs[at], sem.at[n_dest + at]))
-        copies[-1].start()
     for out, d in enumerate(dests):
         at = 0
         for j, count in enumerate(parts):
@@ -110,31 +107,34 @@
                 term = jnp.dot(table, ref[:rows, :], preferred_element_type=f32)
                 got = term if got is None else got + term
                 first += rows
-            stage[out, j * cap : (j + 1) * cap, :] = got.astype(bf16)
-        copies.append(pltpu.make_async_copy(stage.at[out], out_refs[out], sem.at[out]))
-        copies[-1].start()
+            if direct:
+                out_refs[out][j * cap : (j + 1) * cap, :] = got.astype(bf16)
+            else:
+                stage, sem = refs[-2:]
+                stage[out, j] = got.astype(bf16)
+                to = out_refs[out].at[pl.ds(j * cap, cap), :]
+                copies.append(pltpu.make_async_copy(stage.at[out, j], to, sem.at[out, j]))
+                copies[-1].start()
     for copy in copies:
         copy.wait()
 
 
-def compact(sources, after, tok, cap, dests, halves=()):
+def compact(sources, tok, cap, dests):
     n_src, width, n_dest = len(sources), sources[0][0].shape[1], len(dests)
     xs = sum(sources, [])
-    outs = [pltpu.HBM((n_src * cap, width), bf16)] * n_dest
-    outs += [pltpu.HBM((rows, width), bf16) for _, rows, _ in halves]
+    direct = DIRECT and 0 not in dests
+    shape = (n_src * cap, width)
+    scratch = [pltpu.VMEM((n_dest, n_src, cap, width), bf16), pltpu.SemaphoreType.DMA((n_dest, n_src))]
     return pl.pallas_call(
-        functools.partial(compact_kernel, [len(x) for x in sources], tok, cap, dests, halves),
-        out_shape=outs,
-        in_specs=[VMEM] * len(xs) + [HBM] * len(after),
-        out_specs=[HBM] * len(outs),
-        scratch_shapes=[
-            pltpu.VMEM((n_dest, n_src * cap, width), bf16),
-            pltpu.SemaphoreType.DMA((n_dest + len(halves),)),
-        ],
-        compiler_params=params(12),
+        functools.partial(compact_kernel, [len(x) for x in sources], tok, cap, dests, direct),
+        out_shape=[jax.ShapeDtypeStruct(shape, bf16) if direct else pltpu.HBM(shape, bf16)] * n_dest,
+        in_specs=[VMEM] * len(xs),
+        out_specs=[VMEM if direct else HBM] * n_dest,
+        scratch_shapes=[] if direct else scratch,
+        compiler_params=params(8),
         cost_estimate=cost(2 * n_src * n_dest * cap * tok * width, n_src * tok * width * 6),
         name="compact",
-    )(*xs, *map(in_hbm, after))
+    )(*xs)
 
 
 def picked_kernel(ids_ref, tok_ref, w_ref, out_ref, ids, toks, weights, sem):
@@ -273,16 +273,12 @@
 
 def last_dots_kernel(n_width, groups, last, side, gate_ref, eo_ref, *refs):
     chunk_refs, early_refs, out_ref = refs[:side], refs[side:-1], refs[-1]
-    n_expert = gate_ref.shape[0]
     place = here()
-    for e in range(n_expert):
+
+    def put(src, row):
+        both = jnp.concatenate([row, gate_ref[pl.ds(src, 1), :]], axis=1)
         for w in range(n_width):
-            out_ref[2 * (e * n_width + w) + 1] = gate_ref[e : e + 1, :]
-
-    def put(src, row):
-        base = src * (2 * n_width)
-        for w in range(n_width):
-            out_ref[base + 2 * w] = row
+            out_ref[src * n_width + w] = both
 
     for (batch, dests), early in zip(groups, early_refs):
         for at, src in enumerate(cells_of(batch, dests, place)):
@@ -295,12 +291,12 @@
     top, tok = ids_ref.shape
     rows = []
     for e in range(n_expert):
-        row = got_ref[2 * e * n_width]
+        row = got_ref[e * n_width]
         for w in range(1, n_width):
-            row = row + got_ref[2 * (e * n_width + w)]
+            row = row + got_ref[e * n_width + w]
         rows.append(row)
-    dots = jnp.concatenate(rows, axis=0)
-    cap = dots.shape[1]
+    cap = got_ref.shape[2] // 2
+    dots = jnp.concatenate(rows, axis=0)[:, :cap]
     high = dots.astype(bf16)
     low = (dots - high.astype(f32)).astype(bf16)
     both = jnp.concatenate([high, low], axis=0)
@@ -334,7 +330,7 @@
     copies = []
     cells = sum([cells_of(batch, range(side), place) for batch in batches], [])
     for at, src in enumerate(cells):
-        gate = jnp.broadcast_to(got_ref[src * (2 * n_width) + 1], (128, cap)).T
+        gate = jnp.broadcast_to(got_ref[src * n_width][:, cap:], (128, cap)).T
         rows[at].wait()
         for lane in range(0, held.shape[2], 128):
             part = held[at, :, lane : lane + 128].astype(f32)
@@ -391,12 +387,11 @@
     sent_parts = front(ids, tokens_in, router_weight, n_width)
     parts = lax.all_to_all(sent_parts, "width", 0, 0, tiled=True)
 
-    landed, after = [], []
+    landed = []
     for b, batch in enumerate(batches):
         group = [None] * side
         for dests in PARTS[b]:
-            chunks = compact([sources[s] for s in batch], after, tok, cap, dests)
-            after = [chunks[0]]
+            chunks = compact([sources[s] for s in batch], tok, cap, dests)
             for d, chunk in zip(dests, chunks):
                 group[d] = chunk if d == 0 else send(chunk, d, True)
         landed.append(group)
@@ -421,7 +416,7 @@
             groups.append((batch, dests))
     sent = pl.pallas_call(
         functools.partial(last_dots_kernel, n_width, groups, batches[-1], side),
-        out_shape=jax.ShapeDtypeStruct((2 * n_expert * n_width, 1, cap), f32),
+        out_shape=jax.ShapeDtypeStruct((n_expert * n_width, 1, 2 * cap), f32),
         in_specs=[VMEM] * (2 + side + len(early)),
         out_specs=VMEM,
         compiler_params=params(6),

time: 106 us -> 108 us (1.019)
  Pallas kernels: 27.2 us -> 28.5 us
  starting transfers between devices: 21.4 us -> 22.7 us
    pallas_call x4 -> x6, Pallas kernels: 7.94 us -> 9.23 us  [compact(): pl.pallas_call(functools.partial(compact_kernel, [len(x) for x in sources...]
    ppermute x12, starting transfers between devices: 17.9 us -> 19.2 us  [send(): return lax.ppermute(x, AXES, line_shift(n_expert, n_width, shift, second))]
  transfers between devices with their start and end apart: 13 -> 13, of which waited for: 4 -> 4; matrix products, arithmetic and copies ran while one was open for 0% -> 0% of each run, Pallas kernels for 21% -> 22%
where the time goes in v5:
time: 108 us
  Pallas kernels  28.5 us (26%)
  blocking collectives  28.1 us (26%)
  waiting for transfers between devices  24.9 us (23%)
  starting transfers between devices  22.7 us (21%)
  local copies, waits for them, and re-layouts  1.98 us (2%)
    ppermute x12, waiting for transfers between devices, send(): return lax.ppermute(x, AXES, line_shift(n_expert, n_width, shift, second))  20 us
    ppermute x12, starting transfers between devices, send(): return lax.ppermute(x, AXES, line_shift(n_expert, n_width, shift, second))  19.2 us
    all_to_all x1, blocking collectives, body(): got = lax.all_to_all(sent, AXES, 0, 0, tiled=True)  17.6 us
    all_to_all x1, blocking collectives, body(): parts = lax.all_to_all(sent_parts, 'width', 0, 0, tiled=True)  10.5 us
    pallas_call x6, Pallas kernels, compact(): pl.pallas_call(functools.partial(compact_kernel, [len(x) for x in sources...  9.23 us
    pallas_call x3, Pallas kernels, row_dots_call(): pl.pallas_call(functools.partial(dots_kernel, batch, dests, cap, ahead_ce...  6.72 us
    pallas_call x1, Pallas kernels, body(): pl.pallas_call(functools.partial(scale_kernel, n_width, batches, cap, sid...  6.02 us
    all_to_all x1, waiting for transfers between devices, body(): lax.all_to_all(router_part.reshape(n_expert, per_device, width), 'expert'...  4.95 us
  transfers between devices with their start and end apart: 13, of which 4 were waited for; matrix products, arithmetic and copies ran while one was open for 0% of the time, Pallas kernels for 22%

profile of v5, /device:TPU:0, one launch (start us, length us, event | category | flops | bytes accessed | tf_op | source)
XLA Modules:
  0.0 107.9 jit_solution(17714214236622472267)
XLA Ops:
  1.8 3.2 %collective-permute-start.3 = (bf16[200,896]{1,0:T(8,128)(2,1)S(1)}, bf16[200,896]{1,0:T(8,128)(2,1)S(1)}, u32[]{:S(2)}, u32[]{:S(2)}) collective-permute-start(bf16[200,896]{1,0:T(8,128)(2,1)S(1)} %get-tuple-element.15.refs_1_), channel_id=1, source_target_pairs={{0,96},{1,25},{2,98},{3,27},{4,100},{5,29},{6,102},{7,31},{8,104},... | collective-permute-start | bytes 1075208 | tf_op jit(solution)/shard_map/ppermute | solution.py:358
  5.0 3.2 %collective-permute-start.2 = (bf16[192,896]{1,0:T(8,128)(2,1)S(1)}, bf16[192,896]{1,0:T(8,128)(2,1)S(1)}, u32[]{:S(2)}, u32[]{:S(2)}) collective-permute-start(bf16[192,896]{1,0:T(8,128)(2,1)S(1)} %get-tuple-element.14.refs_0_), channel_id=1, source_target_pairs={{0,96},{1,25},{2,98},{3,27},{4,100},{5,29},{6,102},{7,31},{8,104},... | collective-permute-start | bytes 1032200 | tf_op jit(solution)/shard_map/ppermute | solution.py:358
  8.2 5.4 %collective-permute-done.2.refs_4_ = bf16[192,896]{1,0:T(8,128)(2,1)S(1)} collective-permute-done((bf16[192,896]{1,0:T(8,128)(2,1)S(1)}, bf16[192,896]{1,0:T(8,128)(2,1)S(1)}, u32[]{:S(2)}, u32[]{:S(2)}) %collective-permute-start.2) | collective-permute-done | bytes 344096 | tf_op jit(solution)/shard_map/ppermute | solution.py:358
  13.6 3.7 %collective-permute-done.refs_2_ = bf16[192,896]{1,0:T(8,128)(2,1)S(1)} collective-permute-done((bf16[192,896]{1,0:T(8,128)(2,1)S(1)}, bf16[192,896]{1,0:T(8,128)(2,1)S(1)}, u32[]{:S(2)}, u32[]{:S(2)}) %collective-permute-start) | collective-permute-done | bytes 344096 | tf_op jit(solution)/shard_map/ppermute | solution.py:358
  17.3 1.6 %compact.9 = bf16[576,896]{1,0:T(8,128)(2,1)} custom-call(bf16[192,896]{1,0:T(8,128)(2,1)S(1)} %get-tuple-element.14.refs_0_, bf16[200,896]{1,0:T(8,128)(2,1)S(1)} %get-tuple-element.15.refs_1_, bf16[192,896]{1,0:T(8,128)(2,1)S(1)} %collective-permute-done.refs_2_, bf16[200,896]{1,0:T(8,128)(2,1)S(1)} %collective-permute-done.1.refs_3_, ...), custom_call_target="tpu_custom_call" | custom-call | flops 396361728 | bytes 6193152 | tf_op jit(solution)/shard_map/compact/pallas_call | solution.py:128
  18.9 3.9 %collective-permute-start.9 = (bf16[576,896]{1,0:T(8,128)(2,1)}, bf16[576,896]{1,0:T(8,128)(2,1)S(1)}, u32[]{:S(2)}, u32[]{:S(2)}) collective-permute-start(bf16[576,896]{1,0:T(8,128)(2,1)} %compact.9), channel_id=1, source_target_pairs={{0,16},{1,65},{2,18},{3,67},{4,20},{5,69},{6,22},{7,71},{8,24},{9,... | collective-permute-start | bytes 3096584 | tf_op jit(solution)/shard_map/ppermute | solution.py:358
  22.9 1.6 %compact.10 = bf16[576,896]{1,0:T(8,128)(2,1)} custom-call(bf16[192,896]{1,0:T(8,128)(2,1)S(1)} %get-tuple-element.14.refs_0_, bf16[200,896]{1,0:T(8,128)(2,1)S(1)} %get-tuple-element.15.refs_1_, bf16[192,896]{1,0:T(8,128)(2,1)S(1)} %collective-permute-done.refs_2_, bf16[200,896]{1,0:T(8,128)(2,1)S(1)} %collective-permute-done.1.refs_3_, ...), custom_call_target="tpu_custom_call" | custom-call | flops 396361728 | bytes 6193152 | tf_op jit(solution)/shard_map/compact/pallas_call | solution.py:128
  25.6 1.6 %compact.11 = bf16[576,896]{1,0:T(8,128)(2,1)} custom-call(bf16[192,896]{1,0:T(8,128)(2,1)S(1)} %get-tuple-element.14.refs_0_, bf16[200,896]{1,0:T(8,128)(2,1)S(1)} %get-tuple-element.15.refs_1_, bf16[192,896]{1,0:T(8,128)(2,1)S(1)} %collective-permute-done.refs_2_, bf16[200,896]{1,0:T(8,128)(2,1)S(1)} %collective-permute-done.1.refs_3_, ...), custom_call_target="tpu_custom_call" | custom-call | flops 396361728 | bytes 6193152 | tf_op jit(solution)/shard_map/compact/pallas_call | solution.py:128
  27.2 2.3 %collective-permute-start.11 = (bf16[576,896]{1,0:T(8,128)(2,1)}, bf16[576,896]{1,0:T(8,128)(2,1)S(1)}, u32[]{:S(2)}, u32[]{:S(2)}) collective-permute-start(bf16[576,896]{1,0:T(8,128)(2,1)} %compact.11), channel_id=1, source_target_pairs={{0,24},{1,97},{2,26},{3,99},{4,28},{5,101},{6,30},{7,103},{8,0},{9... | collective-permute-start | bytes 3096584 | tf_op jit(solution)/shard_map/ppermute | solution.py:358
  29.5 2.0 %collective-permute-start.4 = (bf16[192,896]{1,0:T(8,128)(2,1)S(1)}, bf16[192,896]{1,0:T(8,128)(2,1)S(1)}, u32[]{:S(2)}, u32[]{:S(2)}) collective-permute-start(bf16[192,896]{1,0:T(8,128)(2,1)S(1)} %collective-permute-done.refs_2_), channel_id=1, source_target_pairs={{0,32},{1,9},{2,34},{3,11},{4,36},{5,13},{6,38},{7,15},{8,40},{9,1... | collective-permute-start | bytes 1032200 | tf_op jit(solution)/shard_map/ppermute | solution.py:358
  31.5 10.9 %collective-permute-done.4.refs_0_ = bf16[192,896]{1,0:T(8,128)(2,1)S(1)} collective-permute-done((bf16[192,896]{1,0:T(8,128)(2,1)S(1)}, bf16[192,896]{1,0:T(8,128)(2,1)S(1)}, u32[]{:S(2)}, u32[]{:S(2)}) %collective-permute-start.4) | collective-permute-done | bytes 344096 | tf_op jit(solution)/shard_map/ppermute | solution.py:358
  42.4 1.6 %compact.7 = (bf16[192,896]{1,0:T(8,128)(2,1)}, bf16[192,896]{1,0:T(8,128)(2,1)}, bf16[192,896]{1,0:T(8,128)(2,1)}) custom-call(bf16[192,896]{1,0:T(8,128)(2,1)S(1)} %collective-permute-done.4.refs_0_, bf16[200,896]{1,0:T(8,128)(2,1)S(1)} %collective-permute-done.5.refs_1_), custom_call_target="tpu_custom_call" | custom-call | flops 396361728 | bytes 2064384 | tf_op jit(solution)/shard_map/compact/pallas_call | solution.py:128
  44.1 3.2 %collective-permute-start.8 = (bf16[192,896]{1,0:T(8,128)(2,1)}, bf16[192,896]{1,0:T(8,128)(2,1)S(1)}, u32[]{:S(2)}, u32[]{:S(2)}) collective-permute-start(bf16[192,896]{1,0:T(8,128)(2,1)} %get-tuple-element.19), channel_id=1, source_target_pairs={{0,24},{1,97},{2,26},{3,99},{4,28},{5,101},{6,30},{7,103},{8,0},{9... | collective-permute-start | bytes 1032200 | tf_op jit(solution)/shard_map/ppermute | solution.py:358
  48.6 2.5 %picked.1 = f32[8,8,384]{2,1,0:T(8,128)S(1)} custom-call(s32[8,384]{1,0:T(8,128)} %bitcast.5, bf16[384,896]{1,0:T(8,128)(2,1)} %tok_ref.3, bf16[896,256]{1,0:T(8,128)(2,1)} %w_ref.3), custom_call_target="tpu_custom_call" | custom-call | flops 176160768 | bytes 688128 | tf_op jit(solution)/shard_map/picked/pallas_call | solution.py:165
  51.1 10.5 %all_to_all.15.parts_ref = f32[8,8,384]{2,1,0:T(8,128)S(1)} all-to-all(f32[8,8,384]{2,1,0:T(8,128)S(1)} %picked.1), channel_id=1, replica_groups=mesh['expert'=16,'width'=8] {'width'}, dimensions={0} | all-to-all | bytes 196608 | tf_op jit(solution)/shard_map/all_to_all | solution.py:388
  62.1 1.6 %compact.6.refs_0_ = bf16[576,896]{1,0:T(8,128)(2,1)} custom-call(bf16[192,896]{1,0:T(8,128)(2,1)S(1)} %get-tuple-element.14.refs_0_, bf16[200,896]{1,0:T(8,128)(2,1)S(1)} %get-tuple-element.15.refs_1_, bf16[192,896]{1,0:T(8,128)(2,1)S(1)} %collective-permute-done.refs_2_, bf16[200,896]{1,0:T(8,128)(2,1)S(1)} %collective-permute-done.1.refs_3_, ...), custom_call_target="tpu_custom_call" | custom-call | flops 396361728 | bytes 6193152 | tf_op jit(solution)/shard_map/compact/pallas_call | solution.py:128
  63.7 2.1 %dots.3 = (f32[3,192]{1,0:T(4,128)S(1)}, bf16[4,192,896]{2,1,0:T(8,128)(2,1)S(1)}) custom-call(bf16[3072,896]{1,0:T(8,128)(2,1)} %eo_ref.5, bf16[576,896]{1,0:T(8,128)(2,1)} %compact.6.refs_0_), custom_call_target="tpu_custom_call" | custom-call | flops 1032192 | bytes 2064384 | tf_op jit(solution)/shard_map/dots/pallas_call | solution.py:257
  65.8 1.9 %dots.4.refs_5_ = f32[3,192]{1,0:T(4,128)S(1)} custom-call(bf16[3072,896]{1,0:T(8,128)(2,1)} %eo_ref.5, bf16[576,896]{1,0:T(8,128)(2,1)} %copy-done.8), custom_call_target="tpu_custom_call" | custom-call | flops 1032192 | bytes 2064384 | tf_op jit(solution)/shard_map/dots/pallas_call | solution.py:257
  69.7 2.7 %dots.5.refs_6_ = f32[6,192]{1,0:T(8,128)S(1)} custom-call(bf16[3072,896]{1,0:T(8,128)(2,1)} %eo_ref.5, bf16[576,896]{1,0:T(8,128)(2,1)} %copy-done.9, bf16[576,896]{1,0:T(8,128)(2,1)} %copy-done.10), custom_call_target="tpu_custom_call" | custom-call | flops 2064384 | bytes 4128768 | tf_op jit(solution)/shard_map/dots/pallas_call | solution.py:257
  73.0 17.6 %all_to_all.16.got_ref = f32[128,1,384]{2,1,0:T(1,128)S(1)} all-to-all(f32[128,1,384]{2,1,0:T(1,128)S(1)} %last_dots.1), channel_id=1, replica_groups=mesh['expert'=16,'width'=8] {'expert','width'}, dimensions={0} | all-to-all | bytes 393216 | tf_op jit(solution)/shard_map/all_to_all | solution.py:426
  90.7 1.9 %tail.1 = (bf16[256,384]{1,0:T(8,128)(2,1)S(1)}, bf16[256,896]{1,0:T(8,128)(2,1)}) custom-call(f32[128,1,384]{2,1,0:T(1,128)S(1)} %all_to_all.16.got_ref, f32[8,8,384]{2,1,0:T(8,128)S(1)} %all_to_all.15.parts_ref, s32[8,384]{1,0:T(8,128)S(1)} %bitcast.7, s32[8,384]{1,0:T(8,128)S(1)} %bitcast.10, bf16[384,896]{1,0:T(8,128)(2,1)S(1)} %copy-done), custom_call_target="tpu_custom_call" | custom-call | flops 176160768 | bytes 688128 | tf_op jit(solution)/shard_map/tail/pallas_call | solution.py:428
  92.6 3.6 %all-to-all-start.2 = ((bf16[16,16,896]{2,1,0:T(8,128)(2,1)}), bf16[16,16,896]{2,1,0:T(8,128)(2,1)S(1)}, u32[]{:S(2)}, u32[]{:S(2)}) async-start(bf16[16,16,896]{2,1,0:T(8,128)(2,1)} %bitcast.2), calls=%async_computation.2 | async-start | bytes 917504 | tf_op jit(solution)/shard_map/all_to_all | solution.py:440
  96.2 6.0 %scale.1 = (bf16[3072,896]{1,0:T(8,128)(2,1)}, bf16[384,896]{1,0:T(8,128)(2,1)}) custom-call(f32[128,1,384]{2,1,0:T(1,128)S(1)} %all_to_all.16.got_ref, bf16[256,384]{1,0:T(8,128)(2,1)S(1)} %get-tuple-element.21.lg_ref, bf16[896,256]{1,0:T(8,128)(2,1)S(1)} %copy-done.1, bf16[576,896]{1,0:T(8,128)(2,1)} %compact.6.refs_0_, bf16[576,896]{1,0:T(8,128)(2,1)} %copy-done.9, ...), custom_call_target="tpu_custom_call" | custom-call | flops 176160768 | bytes 11010048 | tf_op jit(solution)/shard_map/scale/pallas_call | solution.py:442
  102.2 5.0 %all-to-all-done.2 = bf16[16,16,896]{2,1,0:T(8,128)(2,1)S(1)} async-done(((bf16[16,16,896]{2,1,0:T(8,128)(2,1)}), bf16[16,16,896]{2,1,0:T(8,128)(2,1)S(1)}, u32[]{:S(2)}, u32[]{:S(2)}) %all-to-all-start.2) | async-done | bytes 458784 | tf_op jit(solution)/shard_map/all_to_all | solution.py:440
  (42 shorter events, 7.3 us)
Async XLA Ops:
  1.8 15.5 %collective-permute-start.3 = (bf16[200,896]{1,0:T(8,128)(2,1)S(1)}, bf16[200,896]{1,0:T(8,128)(2,1)S(1)}, u32[]{:S(2)}, u32[]{:S(2)}) collective-permute-start(bf16[200,896]{1,0:T(8,128)(2,1)S(1)} %get-tuple-element.15.refs_1_), channel_id=1, source_target_pairs={{0,96},{1,25},{2,98},{3,27},{4,100},{5,29},{6,102},{7,31},{8,104},... | collective-permute-start | bytes 1075208 | tf_op jit(solution)/shard_map/ppermute | solution.py:358
  5.0 12.3 %collective-permute-start.1 = (bf16[200,896]{1,0:T(8,128)(2,1)S(1)}, bf16[200,896]{1,0:T(8,128)(2,1)S(1)}, u32[]{:S(2)}, u32[]{:S(2)}) collective-permute-start(bf16[200,896]{1,0:T(8,128)(2,1)S(1)} %get-tuple-element.15.refs_1_), channel_id=1, source_target_pairs={{0,32},{1,9},{2,34},{3,11},{4,36},{5,13},{6,38},{7,15},{8,40},{9,1... | collective-permute-start | bytes 1075208 | tf_op jit(solution)/shard_map/ppermute | solution.py:358
  5.0 8.6 %collective-permute-start.2 = (bf16[192,896]{1,0:T(8,128)(2,1)S(1)}, bf16[192,896]{1,0:T(8,128)(2,1)S(1)}, u32[]{:S(2)}, u32[]{:S(2)}) collective-permute-start(bf16[192,896]{1,0:T(8,128)(2,1)S(1)} %get-tuple-element.14.refs_0_), channel_id=1, source_target_pairs={{0,96},{1,25},{2,98},{3,27},{4,100},{5,29},{6,102},{7,31},{8,104},... | collective-permute-start | bytes 1032200 | tf_op jit(solution)/shard_map/ppermute | solution.py:358
  8.2 9.1 %collective-permute-start = (bf16[192,896]{1,0:T(8,128)(2,1)S(1)}, bf16[192,896]{1,0:T(8,128)(2,1)S(1)}, u32[]{:S(2)}, u32[]{:S(2)}) collective-permute-start(bf16[192,896]{1,0:T(8,128)(2,1)S(1)} %get-tuple-element.14.refs_0_), channel_id=1, source_target_pairs={{0,32},{1,9},{2,34},{3,11},{4,36},{5,13},{6,38},{7,15},{8,40},{9,1... | collective-permute-start | bytes 1032200 | tf_op jit(solution)/shard_map/ppermute | solution.py:358
  18.9 42.7 %copy-start.6 = (s32[384,8]{0,1:T(8,128)S(1)}, s32[384,8]{0,1:T(8,128)}, u32[]{:S(2)}) copy-start(s32[384,8]{0,1:T(8,128)} %param.10) | copy-start | bytes 36868
  18.9 42.7 %copy-start.7 = (s32[384,8]{0,1:T(8,128)S(1)}, s32[384,8]{0,1:T(8,128)}, u32[]{:S(2)}) copy-start(s32[384,8]{0,1:T(8,128)} %param.11) | copy-start | bytes 36868
  18.9 29.6 %collective-permute-start.9 = (bf16[576,896]{1,0:T(8,128)(2,1)}, bf16[576,896]{1,0:T(8,128)(2,1)S(1)}, u32[]{:S(2)}, u32[]{:S(2)}) collective-permute-start(bf16[576,896]{1,0:T(8,128)(2,1)} %compact.9), channel_id=1, source_target_pairs={{0,16},{1,65},{2,18},{3,67},{4,20},{5,69},{6,22},{7,71},{8,24},{9,... | collective-permute-start | bytes 3096584 | tf_op jit(solution)/shard_map/ppermute | solution.py:358
  24.5 43.3 %collective-permute-start.10 = (bf16[576,896]{1,0:T(8,128)(2,1)}, bf16[576,896]{1,0:T(8,128)(2,1)S(1)}, u32[]{:S(2)}, u32[]{:S(2)}) collective-permute-start(bf16[576,896]{1,0:T(8,128)(2,1)} %compact.10), channel_id=1, source_target_pairs={{0,8},{1,33},{2,10},{3,35},{4,12},{5,37},{6,14},{7,39},{8,16},{9,4... | collective-permute-start | bytes 3096584 | tf_op jit(solution)/shard_map/ppermute | solution.py:358
  27.2 40.6 %collective-permute-start.11 = (bf16[576,896]{1,0:T(8,128)(2,1)}, bf16[576,896]{1,0:T(8,128)(2,1)S(1)}, u32[]{:S(2)}, u32[]{:S(2)}) collective-permute-start(bf16[576,896]{1,0:T(8,128)(2,1)} %compact.11), channel_id=1, source_target_pairs={{0,24},{1,97},{2,26},{3,99},{4,28},{5,101},{6,30},{7,103},{8,0},{9... | collective-permute-start | bytes 3096584 | tf_op jit(solution)/shard_map/ppermute | solution.py:358
  29.5 12.9 %collective-permute-start.5 = (bf16[200,896]{1,0:T(8,128)(2,1)S(1)}, bf16[200,896]{1,0:T(8,128)(2,1)S(1)}, u32[]{:S(2)}, u32[]{:S(2)}) collective-permute-start(bf16[200,896]{1,0:T(8,128)(2,1)S(1)} %collective-permute-done.3.refs_5_), channel_id=1, source_target_pairs={{0,96},{1,25},{2,98},{3,27},{4,100},{5,29},{6,102},{7,31},{8,104},... | collective-permute-start | bytes 1075208 | tf_op jit(solution)/shard_map/ppermute | solution.py:358
  29.5 12.9 %collective-permute-start.4 = (bf16[192,896]{1,0:T(8,128)(2,1)S(1)}, bf16[192,896]{1,0:T(8,128)(2,1)S(1)}, u32[]{:S(2)}, u32[]{:S(2)}) collective-permute-start(bf16[192,896]{1,0:T(8,128)(2,1)S(1)} %collective-permute-done.refs_2_), channel_id=1, source_target_pairs={{0,32},{1,9},{2,34},{3,11},{4,36},{5,13},{6,38},{7,15},{8,40},{9,1... | collective-permute-start | bytes 1032200 | tf_op jit(solution)/shard_map/ppermute | solution.py:358
  44.0 28.5 %collective-permute-start.6 = (bf16[192,896]{1,0:T(8,128)(2,1)}, bf16[192,896]{1,0:T(8,128)(2,1)S(1)}, u32[]{:S(2)}, u32[]{:S(2)}) collective-permute-start(bf16[192,896]{1,0:T(8,128)(2,1)} %get-tuple-element.18), channel_id=1, source_target_pairs={{0,8},{1,33},{2,10},{3,35},{4,12},{5,37},{6,14},{7,39},{8,16},{9,4... | collective-permute-start | bytes 1032200 | tf_op jit(solution)/shard_map/ppermute | solution.py:358
  44.1 28.4 %collective-permute-start.8 = (bf16[192,896]{1,0:T(8,128)(2,1)}, bf16[192,896]{1,0:T(8,128)(2,1)S(1)}, u32[]{:S(2)}, u32[]{:S(2)}) collective-permute-start(bf16[192,896]{1,0:T(8,128)(2,1)} %get-tuple-element.19), channel_id=1, source_target_pairs={{0,24},{1,97},{2,26},{3,99},{4,28},{5,101},{6,30},{7,103},{8,0},{9... | collective-permute-start | bytes 1032200 | tf_op jit(solution)/shard_map/ppermute | solution.py:358
  48.5 17.3 %copy-start.8 = (bf16[576,896]{1,0:T(8,128)(2,1)}, bf16[576,896]{1,0:T(8,128)(2,1)S(1)}, u32[]{:S(2)}) copy-start(bf16[576,896]{1,0:T(8,128)(2,1)S(1)} %collective-permute-done.9.refs_0_.refs_2_) | copy-start | bytes 3096580
  48.5 24.0 %collective-permute-start.7 = (bf16[192,896]{1,0:T(8,128)(2,1)}, bf16[192,896]{1,0:T(8,128)(2,1)S(1)}, u32[]{:S(2)}, u32[]{:S(2)}) collective-permute-start(bf16[192,896]{1,0:T(8,128)(2,1)} %compact.8), channel_id=1, source_target_pairs={{0,16},{1,65},{2,18},{3,67},{4,20},{5,69},{6,22},{7,71},{8,24},{9,... | collective-permute-start | bytes 1032200 | tf_op jit(solution)/shard_map/ppermute | solution.py:358
  65.8 6.7 %copy-start.2 = (bf16[192,896]{1,0:T(8,128)(2,1)S(1)}, bf16[192,896]{1,0:T(8,128)(2,1)}, u32[]{:S(2)}) copy-start(bf16[192,896]{1,0:T(8,128)(2,1)} %get-tuple-element.17.refs_0_.refs_4_) | copy-start | bytes 1032196
  67.7 22.9 %copy-start = (bf16[384,896]{1,0:T(8,128)(2,1)S(1)}, bf16[384,896]{1,0:T(8,128)(2,1)}, u32[]{:S(2)}) copy-start(bf16[384,896]{1,0:T(8,128)(2,1)} %tok_ref.3) | copy-start | bytes 2064388
  67.8 28.4 %copy-start.1 = (bf16[896,256]{1,0:T(8,128)(2,1)S(1)}, bf16[896,256]{1,0:T(8,128)(2,1)}, u32[]{:S(2)}) copy-start(bf16[896,256]{1,0:T(8,128)(2,1)} %w_ref.3) | copy-start | bytes 1376260
  67.8 1.0 copy-start.9
  68.8 1.0 copy-start.10
  72.5 23.7 %copy-start.3 = (bf16[192,896]{1,0:T(8,128)(2,1)}, bf16[192,896]{1,0:T(8,128)(2,1)S(1)}, u32[]{:S(2)}) copy-start(bf16[192,896]{1,0:T(8,128)(2,1)S(1)} %collective-permute-done.6.refs_1_.refs_5_) | copy-start | bytes 1032196
  72.5 23.7 %copy-start.4 = (bf16[192,896]{1,0:T(8,128)(2,1)}, bf16[192,896]{1,0:T(8,128)(2,1)S(1)}, u32[]{:S(2)}) copy-start(bf16[192,896]{1,0:T(8,128)(2,1)S(1)} %collective-permute-done.8.refs_3_.refs_7_) | copy-start | bytes 1032196
  72.5 23.6 %copy-start.5 = (bf16[192,896]{1,0:T(8,128)(2,1)}, bf16[192,896]{1,0:T(8,128)(2,1)S(1)}, u32[]{:S(2)}) copy-start(bf16[192,896]{1,0:T(8,128)(2,1)S(1)} %collective-permute-done.7.refs_2_.refs_6_) | copy-start | bytes 1032196
  92.6 14.6 %all-to-all-start.2 = ((bf16[16,16,896]{2,1,0:T(8,128)(2,1)}), bf16[16,16,896]{2,1,0:T(8,128)(2,1)S(1)}, u32[]{:S(2)}, u32[]{:S(2)}) async-start(bf16[16,16,896]{2,1,0:T(8,128)(2,1)} %bitcast.2), calls=%async_computation.2 | async-start | bytes 917504 | tf_op jit(solution)/shard_map/all_to_all | solution.py:440

commit v6 on v5

--- a/solution.py
+++ b/solution.py
@@ -12,7 +12,7 @@
 AXES = ("expert", "width")
 f32, bf16, i32 = jnp.float32, jnp.bfloat16, jnp.int32
 DIRECT = False
-PARTS = (((2,), (1,), (3,), (0,)), ((2,), (1, 3, 0)))
+PARTS = (((2,), (1,), (3,), (0,)), ((2,), (1, 3), (0,)))
 DOTS = ((0,), (2,), (1, 3))
 VMEM = pl.BlockSpec(memory_space=pltpu.VMEM)
 SMEM = pl.BlockSpec(memory_space=pltpu.SMEM)
@@ -287,7 +287,8 @@
         put(src, row_dots(chunk_refs[at], eo_ref.at[at]))
 
 
-def tail_kernel(n_expert, n_width, per_device, got_ref, parts_ref, ids_ref, slots_ref, tok_ref, lg_ref, router_ref):
+def tail_kernel(n_expert, n_width, per_device, got_ref, parts_ref, ids_ref, slots_ref, tok_ref, *refs):
+    lg_ref, router_ref, stage, sem = refs
     top, tok = ids_ref.shape
     rows = []
     for e in range(n_expert):
@@ -304,12 +305,13 @@
     dev = ids // per_device
     slot_rows = lax.broadcasted_iota(i32, (cap, tok), 0)
     dev_rows = lax.broadcasted_iota(i32, (n_expert, tok), 0)
+    tables = [jnp.where(slot_rows == slots[k : k + 1], 1.0, 0.0).astype(bf16) for k in range(top)]
+    found = jnp.dot(both, jnp.concatenate(tables, axis=1), preferred_element_type=f32)
+    found = found[:n_expert] + found[n_expert:]
     out = []
     for k in range(top):
-        table = jnp.where(slot_rows == slots[k : k + 1], 1.0, 0.0).astype(bf16)
-        found = jnp.dot(both, table, preferred_element_type=f32)
-        found = found[:n_expert] + found[n_expert:]
-        out.append(jnp.sum(jnp.where(dev_rows == dev[k : k + 1], found, 0.0), axis=0, keepdims=True))
+        mine = jnp.where(dev_rows == dev[k : k + 1], found[:, k * tok : (k + 1) * tok], 0.0)
+        out.append(jnp.sum(mine, axis=0, keepdims=True))
     gate_grads = jnp.concatenate(out, axis=0)
     picked, totals = gates_of(parts_ref[...])
     weighted = jnp.sum(gate_grads * picked, axis=0, keepdims=True) / totals
@@ -320,7 +322,15 @@
         grads = grads + jnp.where(experts == ids[k : k + 1], local[k : k + 1], 0.0)
     grads = grads.astype(bf16)
     lg_ref[...] = grads
-    router_ref[...] = jnp.dot(grads, tok_ref[...], preferred_element_type=f32).astype(bf16)
+    copies = []
+    rows = grads.shape[0] // 2
+    for at in range(2):
+        part = grads[at * rows : (at + 1) * rows]
+        stage[at] = jnp.dot(part, tok_ref[...], preferred_element_type=f32).astype(bf16)
+        copies.append(pltpu.make_async_copy(stage.at[at], router_ref.at[pl.ds(at * rows, rows), :], sem.at[at]))
+        copies[-1].start()
+    for copy in copies:
+        copy.wait()
 
 
 def scale_kernel(n_width, batches, cap, side, got_ref, lg_ref, w_ref, *refs):
@@ -429,10 +439,14 @@
         functools.partial(tail_kernel, n_expert, n_width, per_device),
         out_shape=[
             jax.ShapeDtypeStruct((experts, tok), bf16),
-            jax.ShapeDtypeStruct((experts, width), bf16),
+            pltpu.HBM((experts, width), bf16),
         ],
         in_specs=[VMEM] * 5,
-        out_specs=[VMEM] * 2,
+        out_specs=[VMEM, HBM],
+        scratch_shapes=[
+            pltpu.VMEM((2, experts // 2, width), bf16),
+            pltpu.SemaphoreType.DMA((2,)),
+        ],
         compiler_params=params(8),
         cost_estimate=cost(2 * tok * width * experts, 2 * tok * width),
         name="tail",

time: 108 us -> 109 us (level)
    pallas_call x6 -> x7, Pallas kernels: 9.23 us -> 10.2 us  [compact(): pl.pallas_call(functools.partial(compact_kernel, [len(x) for x in sources...]
where the time goes in v6:
time: 109 us
  Pallas kernels  29.3 us (27%)
  blocking collectives  28.1 us (26%)
  waiting for transfers between devices  24.9 us (23%)
  starting transfers between devices  22.7 us (21%)
  local copies, waits for them, and re-layouts  1.98 us (2%)
    ppermute x12, waiting for transfers between devices, send(): return lax.ppermute(x, AXES, line_shift(n_expert, n_width, shift, second))  20 us
    ppermute x12, starting transfers between devices, send(): return lax.ppermute(x, AXES, line_shift(n_expert, n_width, shift, second))  19.2 us
    all_to_all x1, blocking collectives, body(): got = lax.all_to_all(sent, AXES, 0, 0, tiled=True)  17.6 us
    all_to_all x1, blocking collectives, body(): parts = lax.all_to_all(sent_parts, 'width', 0, 0, tiled=True)  10.5 us
    pallas_call x7, Pallas kernels, compact(): pl.pallas_call(functools.partial(compact_kernel, [len(x) for x in sources...  10.2 us
    pallas_call x3, Pallas kernels, row_dots_call(): pl.pallas_call(functools.partial(dots_kernel, batch, dests, cap, ahead_ce...  6.72 us
    pallas_call x1, Pallas kernels, body(): pl.pallas_call(functools.partial(scale_kernel, n_width, batches, cap, sid...  6.02 us
    all_to_all x1, waiting for transfers between devices, body(): lax.all_to_all(router_part.reshape(n_expert, per_device, width), 'expert'...  4.95 us
  transfers between devices with their start and end apart: 13, of which 4 were waited for; matrix products, arithmetic and copies ran while one was open for 0% of the time, Pallas kernels for 22%

profile of v6, /device:TPU:0, one launch (start us, length us, event | category | flops | bytes accessed | tf_op | source)
XLA Modules:
  0.0 108.7 jit_solution(586850252864623710)
XLA Ops:
  1.8 3.2 %collective-permute-start.3 = (bf16[200,896]{1,0:T(8,128)(2,1)S(1)}, bf16[200,896]{1,0:T(8,128)(2,1)S(1)}, u32[]{:S(2)}, u32[]{:S(2)}) collective-permute-start(bf16[200,896]{1,0:T(8,128)(2,1)S(1)} %get-tuple-element.14.refs_1_), channel_id=1, source_target_pairs={{0,96},{1,25},{2,98},{3,27},{4,100},{5,29},{6,102},{7,31},{8,104},... | collective-permute-start | bytes 1075208 | tf_op jit(solution)/shard_map/ppermute | solution.py:368
  5.0 3.2 %collective-permute-start.2 = (bf16[192,896]{1,0:T(8,128)(2,1)S(1)}, bf16[192,896]{1,0:T(8,128)(2,1)S(1)}, u32[]{:S(2)}, u32[]{:S(2)}) collective-permute-start(bf16[192,896]{1,0:T(8,128)(2,1)S(1)} %get-tuple-element.13.refs_0_), channel_id=1, source_target_pairs={{0,96},{1,25},{2,98},{3,27},{4,100},{5,29},{6,102},{7,31},{8,104},... | collective-permute-start | bytes 1032200 | tf_op jit(solution)/shard_map/ppermute | solution.py:368
  8.2 5.4 %collective-permute-done.2.refs_4_ = bf16[192,896]{1,0:T(8,128)(2,1)S(1)} collective-permute-done((bf16[192,896]{1,0:T(8,128)(2,1)S(1)}, bf16[192,896]{1,0:T(8,128)(2,1)S(1)}, u32[]{:S(2)}, u32[]{:S(2)}) %collective-permute-start.2) | collective-permute-done | bytes 344096 | tf_op jit(solution)/shard_map/ppermute | solution.py:368
  13.6 3.7 %collective-permute-done.refs_2_ = bf16[192,896]{1,0:T(8,128)(2,1)S(1)} collective-permute-done((bf16[192,896]{1,0:T(8,128)(2,1)S(1)}, bf16[192,896]{1,0:T(8,128)(2,1)S(1)}, u32[]{:S(2)}, u32[]{:S(2)}) %collective-permute-start) | collective-permute-done | bytes 344096 | tf_op jit(solution)/shard_map/ppermute | solution.py:368
  17.3 1.6 %compact.11 = bf16[576,896]{1,0:T(8,128)(2,1)} custom-call(bf16[192,896]{1,0:T(8,128)(2,1)S(1)} %get-tuple-element.13.refs_0_, bf16[200,896]{1,0:T(8,128)(2,1)S(1)} %get-tuple-element.14.refs_1_, bf16[192,896]{1,0:T(8,128)(2,1)S(1)} %collective-permute-done.refs_2_, bf16[200,896]{1,0:T(8,128)(2,1)S(1)} %collective-permute-done.1.refs_3_, ...), custom_call_target="tpu_custom_call" | custom-call | flops 396361728 | bytes 6193152 | tf_op jit(solution)/shard_map/compact/pallas_call | solution.py:128
  18.9 3.9 %collective-permute-start.9 = (bf16[576,896]{1,0:T(8,128)(2,1)}, bf16[576,896]{1,0:T(8,128)(2,1)S(1)}, u32[]{:S(2)}, u32[]{:S(2)}) collective-permute-start(bf16[576,896]{1,0:T(8,128)(2,1)} %compact.11), channel_id=1, source_target_pairs={{0,16},{1,65},{2,18},{3,67},{4,20},{5,69},{6,22},{7,71},{8,24},{9,... | collective-permute-start | bytes 3096584 | tf_op jit(solution)/shard_map/ppermute | solution.py:368
  22.9 1.6 %compact.12 = bf16[576,896]{1,0:T(8,128)(2,1)} custom-call(bf16[192,896]{1,0:T(8,128)(2,1)S(1)} %get-tuple-element.13.refs_0_, bf16[200,896]{1,0:T(8,128)(2,1)S(1)} %get-tuple-element.14.refs_1_, bf16[192,896]{1,0:T(8,128)(2,1)S(1)} %collective-permute-done.refs_2_, bf16[200,896]{1,0:T(8,128)(2,1)S(1)} %collective-permute-done.1.refs_3_, ...), custom_call_target="tpu_custom_call" | custom-call | flops 396361728 | bytes 6193152 | tf_op jit(solution)/shard_map/compact/pallas_call | solution.py:128
  25.6 1.6 %compact.13 = bf16[576,896]{1,0:T(8,128)(2,1)} custom-call(bf16[192,896]{1,0:T(8,128)(2,1)S(1)} %get-tuple-element.13.refs_0_, bf16[200,896]{1,0:T(8,128)(2,1)S(1)} %get-tuple-element.14.refs_1_, bf16[192,896]{1,0:T(8,128)(2,1)S(1)} %collective-permute-done.refs_2_, bf16[200,896]{1,0:T(8,128)(2,1)S(1)} %collective-permute-done.1.refs_3_, ...), custom_call_target="tpu_custom_call" | custom-call | flops 396361728 | bytes 6193152 | tf_op jit(solution)/shard_map/compact/pallas_call | solution.py:128
  27.2 2.3 %collective-permute-start.11 = (bf16[576,896]{1,0:T(8,128)(2,1)}, bf16[576,896]{1,0:T(8,128)(2,1)S(1)}, u32[]{:S(2)}, u32[]{:S(2)}) collective-permute-start(bf16[576,896]{1,0:T(8,128)(2,1)} %compact.13), channel_id=1, source_target_pairs={{0,24},{1,97},{2,26},{3,99},{4,28},{5,101},{6,30},{7,103},{8,0},{9... | collective-permute-start | bytes 3096584 | tf_op jit(solution)/shard_map/ppermute | solution.py:368
  29.5 2.0 %collective-permute-start.4 = (bf16[192,896]{1,0:T(8,128)(2,1)S(1)}, bf16[192,896]{1,0:T(8,128)(2,1)S(1)}, u32[]{:S(2)}, u32[]{:S(2)}) collective-permute-start(bf16[192,896]{1,0:T(8,128)(2,1)S(1)} %collective-permute-done.refs_2_), channel_id=1, source_target_pairs={{0,32},{1,9},{2,34},{3,11},{4,36},{5,13},{6,38},{7,15},{8,40},{9,1... | collective-permute-start | bytes 1032200 | tf_op jit(solution)/shard_map/ppermute | solution.py:368
  31.5 10.9 %collective-permute-done.4.refs_0_ = bf16[192,896]{1,0:T(8,128)(2,1)S(1)} collective-permute-done((bf16[192,896]{1,0:T(8,128)(2,1)S(1)}, bf16[192,896]{1,0:T(8,128)(2,1)S(1)}, u32[]{:S(2)}, u32[]{:S(2)}) %collective-permute-start.4) | collective-permute-done | bytes 344096 | tf_op jit(solution)/shard_map/ppermute | solution.py:368
  42.4 1.4 %compact.9 = (bf16[192,896]{1,0:T(8,128)(2,1)}, bf16[192,896]{1,0:T(8,128)(2,1)}) custom-call(bf16[192,896]{1,0:T(8,128)(2,1)S(1)} %collective-permute-done.4.refs_0_, bf16[200,896]{1,0:T(8,128)(2,1)S(1)} %collective-permute-done.5.refs_1_), custom_call_target="tpu_custom_call" | custom-call | flops 264241152 | bytes 2064384 | tf_op jit(solution)/shard_map/compact/pallas_call | solution.py:128
  43.9 3.2 %collective-permute-start.8 = (bf16[192,896]{1,0:T(8,128)(2,1)}, bf16[192,896]{1,0:T(8,128)(2,1)S(1)}, u32[]{:S(2)}, u32[]{:S(2)}) collective-permute-start(bf16[192,896]{1,0:T(8,128)(2,1)} %get-tuple-element.17), channel_id=1, source_target_pairs={{0,24},{1,97},{2,26},{3,99},{4,28},{5,101},{6,30},{7,103},{8,0},{9... | collective-permute-start | bytes 1032200 | tf_op jit(solution)/shard_map/ppermute | solution.py:368
  48.4 2.5 %picked.1 = f32[8,8,384]{2,1,0:T(8,128)S(1)} custom-call(s32[8,384]{1,0:T(8,128)} %bitcast.5, bf16[384,896]{1,0:T(8,128)(2,1)} %tok_ref.3, bf16[896,256]{1,0:T(8,128)(2,1)} %w_ref.3), custom_call_target="tpu_custom_call" | custom-call | flops 176160768 | bytes 688128 | tf_op jit(solution)/shard_map/picked/pallas_call | solution.py:165
  50.9 10.5 %all_to_all.15.parts_ref = f32[8,8,384]{2,1,0:T(8,128)S(1)} all-to-all(f32[8,8,384]{2,1,0:T(8,128)S(1)} %picked.1), channel_id=1, replica_groups=mesh['expert'=16,'width'=8] {'width'}, dimensions={0} | all-to-all | bytes 196608 | tf_op jit(solution)/shard_map/all_to_all | solution.py:398
  61.9 1.6 %compact.7.refs_0_ = bf16[576,896]{1,0:T(8,128)(2,1)} custom-call(bf16[192,896]{1,0:T(8,128)(2,1)S(1)} %get-tuple-element.13.refs_0_, bf16[200,896]{1,0:T(8,128)(2,1)S(1)} %get-tuple-element.14.refs_1_, bf16[192,896]{1,0:T(8,128)(2,1)S(1)} %collective-permute-done.refs_2_, bf16[200,896]{1,0:T(8,128)(2,1)S(1)} %collective-permute-done.1.refs_3_, ...), custom_call_target="tpu_custom_call" | custom-call | flops 396361728 | bytes 6193152 | tf_op jit(solution)/shard_map/compact/pallas_call | solution.py:128
  63.5 2.1 %dots.3 = (f32[3,192]{1,0:T(4,128)S(1)}, bf16[4,192,896]{2,1,0:T(8,128)(2,1)S(1)}) custom-call(bf16[3072,896]{1,0:T(8,128)(2,1)} %eo_ref.5, bf16[576,896]{1,0:T(8,128)(2,1)} %compact.7.refs_0_), custom_call_target="tpu_custom_call" | custom-call | flops 1032192 | bytes 2064384 | tf_op jit(solution)/shard_map/dots/pallas_call | solution.py:257
  66.8 1.9 %dots.4.refs_5_ = f32[3,192]{1,0:T(4,128)S(1)} custom-call(bf16[3072,896]{1,0:T(8,128)(2,1)} %eo_ref.5, bf16[576,896]{1,0:T(8,128)(2,1)} %copy-done.8), custom_call_target="tpu_custom_call" | custom-call | flops 1032192 | bytes 2064384 | tf_op jit(solution)/shard_map/dots/pallas_call | solution.py:257
  70.7 2.7 %dots.5.refs_6_ = f32[6,192]{1,0:T(8,128)S(1)} custom-call(bf16[3072,896]{1,0:T(8,128)(2,1)} %eo_ref.5, bf16[576,896]{1,0:T(8,128)(2,1)} %copy-done.9, bf16[576,896]{1,0:T(8,128)(2,1)} %copy-done.10), custom_call_target="tpu_custom_call" | custom-call | flops 2064384 | bytes 4128768 | tf_op jit(solution)/shard_map/dots/pallas_call | solution.py:257
  74.0 17.6 %all_to_all.16.got_ref = f32[128,1,384]{2,1,0:T(1,128)S(1)} all-to-all(f32[128,1,384]{2,1,0:T(1,128)S(1)} %last_dots.1), channel_id=1, replica_groups=mesh['expert'=16,'width'=8] {'expert','width'}, dimensions={0} | all-to-all | bytes 393216 | tf_op jit(solution)/shard_map/all_to_all | solution.py:436
  91.6 1.8 %tail.1 = (bf16[256,384]{1,0:T(8,128)(2,1)S(1)}, bf16[256,896]{1,0:T(8,128)(2,1)}) custom-call(f32[128,1,384]{2,1,0:T(1,128)S(1)} %all_to_all.16.got_ref, f32[8,8,384]{2,1,0:T(8,128)S(1)} %all_to_all.15.parts_ref, s32[8,384]{1,0:T(8,128)S(1)} %bitcast.7, s32[8,384]{1,0:T(8,128)S(1)} %bitcast.10, bf16[384,896]{1,0:T(8,128)(2,1)S(1)} %copy-done.1), custom_call_target="tpu_custom_call" | custom-call | flops 176160768 | bytes 688128 | tf_op jit(solution)/shard_map/tail/pallas_call | solution.py:438
  93.4 3.6 %all-to-all-start.2 = ((bf16[16,16,896]{2,1,0:T(8,128)(2,1)}), bf16[16,16,896]{2,1,0:T(8,128)(2,1)S(1)}, u32[]{:S(2)}, u32[]{:S(2)}) async-start(bf16[16,16,896]{2,1,0:T(8,128)(2,1)} %bitcast.11), calls=%async_computation.2 | async-start | bytes 917504 | tf_op jit(solution)/shard_map/all_to_all | solution.py:454
  97.0 6.0 %scale.1 = (bf16[3072,896]{1,0:T(8,128)(2,1)}, bf16[384,896]{1,0:T(8,128)(2,1)}) custom-call(f32[128,1,384]{2,1,0:T(1,128)S(1)} %all_to_all.16.got_ref, bf16[256,384]{1,0:T(8,128)(2,1)S(1)} %get-tuple-element.19.lg_ref, bf16[896,256]{1,0:T(8,128)(2,1)S(1)} %copy-done.2, bf16[576,896]{1,0:T(8,128)(2,1)} %compact.7.refs_0_, bf16[576,896]{1,0:T(8,128)(2,1)} %copy-done.9, ...), custom_call_target="tpu_custom_call" | custom-call | flops 176160768 | bytes 11010048 | tf_op jit(solution)/shard_map/scale/pallas_call | solution.py:456
  103.0 4.9 %all-to-all-done.2 = bf16[16,16,896]{2,1,0:T(8,128)(2,1)S(1)} async-done(((bf16[16,16,896]{2,1,0:T(8,128)(2,1)}), bf16[16,16,896]{2,1,0:T(8,128)(2,1)S(1)}, u32[]{:S(2)}, u32[]{:S(2)}) %all-to-all-start.2) | async-done | bytes 458784 | tf_op jit(solution)/shard_map/all_to_all | solution.py:454
  (43 shorter events, 8.4 us)
Async XLA Ops:
  1.8 15.5 %collective-permute-start.3 = (bf16[200,896]{1,0:T(8,128)(2,1)S(1)}, bf16[200,896]{1,0:T(8,128)(2,1)S(1)}, u32[]{:S(2)}, u32[]{:S(2)}) collective-permute-start(bf16[200,896]{1,0:T(8,128)(2,1)S(1)} %get-tuple-element.14.refs_1_), channel_id=1, source_target_pairs={{0,96},{1,25},{2,98},{3,27},{4,100},{5,29},{6,102},{7,31},{8,104},... | collective-permute-start | bytes 1075208 | tf_op jit(solution)/shard_map/ppermute | solution.py:368
  5.0 12.3 %collective-permute-start.1 = (bf16[200,896]{1,0:T(8,128)(2,1)S(1)}, bf16[200,896]{1,0:T(8,128)(2,1)S(1)}, u32[]{:S(2)}, u32[]{:S(2)}) collective-permute-start(bf16[200,896]{1,0:T(8,128)(2,1)S(1)} %get-tuple-element.14.refs_1_), channel_id=1, source_target_pairs={{0,32},{1,9},{2,34},{3,11},{4,36},{5,13},{6,38},{7,15},{8,40},{9,1... | collective-permute-start | bytes 1075208 | tf_op jit(solution)/shard_map/ppermute | solution.py:368
  5.0 8.6 %collective-permute-start.2 = (bf16[192,896]{1,0:T(8,128)(2,1)S(1)}, bf16[192,896]{1,0:T(8,128)(2,1)S(1)}, u32[]{:S(2)}, u32[]{:S(2)}) collective-permute-start(bf16[192,896]{1,0:T(8,128)(2,1)S(1)} %get-tuple-element.13.refs_0_), channel_id=1, source_target_pairs={{0,96},{1,25},{2,98},{3,27},{4,100},{5,29},{6,102},{7,31},{8,104},... | collective-permute-start | bytes 1032200 | tf_op jit(solution)/shard_map/ppermute | solution.py:368
  8.2 9.1 %collective-permute-start = (bf16[192,896]{1,0:T(8,128)(2,1)S(1)}, bf16[192,896]{1,0:T(8,128)(2,1)S(1)}, u32[]{:S(2)}, u32[]{:S(2)}) collective-permute-start(bf16[192,896]{1,0:T(8,128)(2,1)S(1)} %get-tuple-element.13.refs_0_), channel_id=1, source_target_pairs={{0,32},{1,9},{2,34},{3,11},{4,36},{5,13},{6,38},{7,15},{8,40},{9,1... | collective-permute-start | bytes 1032200 | tf_op jit(solution)/shard_map/ppermute | solution.py:368
  18.9 42.5 %copy-start.6 = (s32[384,8]{0,1:T(8,128)S(1)}, s32[384,8]{0,1:T(8,128)}, u32[]{:S(2)}) copy-start(s32[384,8]{0,1:T(8,128)} %param.10) | copy-start | bytes 36868
  18.9 42.4 %copy-start.7 = (s32[384,8]{0,1:T(8,128)S(1)}, s32[384,8]{0,1:T(8,128)}, u32[]{:S(2)}) copy-start(s32[384,8]{0,1:T(8,128)} %param.11) | copy-start | bytes 36868
  18.9 29.4 %collective-permute-start.9 = (bf16[576,896]{1,0:T(8,128)(2,1)}, bf16[576,896]{1,0:T(8,128)(2,1)S(1)}, u32[]{:S(2)}, u32[]{:S(2)}) collective-permute-start(bf16[576,896]{1,0:T(8,128)(2,1)} %compact.11), channel_id=1, source_target_pairs={{0,16},{1,65},{2,18},{3,67},{4,20},{5,69},{6,22},{7,71},{8,24},{9,... | collective-permute-start | bytes 3096584 | tf_op jit(solution)/shard_map/ppermute | solution.py:368
  24.5 44.3 %collective-permute-start.10 = (bf16[576,896]{1,0:T(8,128)(2,1)}, bf16[576,896]{1,0:T(8,128)(2,1)S(1)}, u32[]{:S(2)}, u32[]{:S(2)}) collective-permute-start(bf16[576,896]{1,0:T(8,128)(2,1)} %compact.12), channel_id=1, source_target_pairs={{0,8},{1,33},{2,10},{3,35},{4,12},{5,37},{6,14},{7,39},{8,16},{9,4... | collective-permute-start | bytes 3096584 | tf_op jit(solution)/shard_map/ppermute | solution.py:368
  27.2 41.6 %collective-permute-start.11 = (bf16[576,896]{1,0:T(8,128)(2,1)}, bf16[576,896]{1,0:T(8,128)(2,1)S(1)}, u32[]{:S(2)}, u32[]{:S(2)}) collective-permute-start(bf16[576,896]{1,0:T(8,128)(2,1)} %compact.13), channel_id=1, source_target_pairs={{0,24},{1,97},{2,26},{3,99},{4,28},{5,101},{6,30},{7,103},{8,0},{9... | collective-permute-start | bytes 3096584 | tf_op jit(solution)/shard_map/ppermute | solution.py:368
  29.5 12.9 %collective-permute-start.5 = (bf16[200,896]{1,0:T(8,128)(2,1)S(1)}, bf16[200,896]{1,0:T(8,128)(2,1)S(1)}, u32[]{:S(2)}, u32[]{:S(2)}) collective-permute-start(bf16[200,896]{1,0:T(8,128)(2,1)S(1)} %collective-permute-done.3.refs_5_), channel_id=1, source_target_pairs={{0,96},{1,25},{2,98},{3,27},{4,100},{5,29},{6,102},{7,31},{8,104},... | collective-permute-start | bytes 1075208 | tf_op jit(solution)/shard_map/ppermute | solution.py:368
  29.5 12.9 %collective-permute-start.4 = (bf16[192,896]{1,0:T(8,128)(2,1)S(1)}, bf16[192,896]{1,0:T(8,128)(2,1)S(1)}, u32[]{:S(2)}, u32[]{:S(2)}) collective-permute-start(bf16[192,896]{1,0:T(8,128)(2,1)S(1)} %collective-permute-done.refs_2_), channel_id=1, source_target_pairs={{0,32},{1,9},{2,34},{3,11},{4,36},{5,13},{6,38},{7,15},{8,40},{9,1... | collective-permute-start | bytes 1032200 | tf_op jit(solution)/shard_map/ppermute | solution.py:368
  43.8 29.6 %collective-permute-start.6 = (bf16[192,896]{1,0:T(8,128)(2,1)}, bf16[192,896]{1,0:T(8,128)(2,1)S(1)}, u32[]{:S(2)}, u32[]{:S(2)}) collective-permute-start(bf16[192,896]{1,0:T(8,128)(2,1)} %get-tuple-element.16), channel_id=1, source_target_pairs={{0,8},{1,33},{2,10},{3,35},{4,12},{5,37},{6,14},{7,39},{8,16},{9,4... | collective-permute-start | bytes 1032200 | tf_op jit(solution)/shard_map/ppermute | solution.py:368
  43.9 29.6 %collective-permute-start.8 = (bf16[192,896]{1,0:T(8,128)(2,1)}, bf16[192,896]{1,0:T(8,128)(2,1)S(1)}, u32[]{:S(2)}, u32[]{:S(2)}) collective-permute-start(bf16[192,896]{1,0:T(8,128)(2,1)} %get-tuple-element.17), channel_id=1, source_target_pairs={{0,24},{1,97},{2,26},{3,99},{4,28},{5,101},{6,30},{7,103},{8,0},{9... | collective-permute-start | bytes 1032200 | tf_op jit(solution)/shard_map/ppermute | solution.py:368
  48.3 17.3 %copy-start.8 = (bf16[576,896]{1,0:T(8,128)(2,1)}, bf16[576,896]{1,0:T(8,128)(2,1)S(1)}, u32[]{:S(2)}) copy-start(bf16[576,896]{1,0:T(8,128)(2,1)S(1)} %collective-permute-done.9.refs_0_.refs_2_) | copy-start | bytes 3096580
  48.3 25.2 %collective-permute-start.7 = (bf16[192,896]{1,0:T(8,128)(2,1)}, bf16[192,896]{1,0:T(8,128)(2,1)S(1)}, u32[]{:S(2)}, u32[]{:S(2)}) collective-permute-start(bf16[192,896]{1,0:T(8,128)(2,1)} %compact.10), channel_id=1, source_target_pairs={{0,16},{1,65},{2,18},{3,67},{4,20},{5,69},{6,22},{7,71},{8,24},{9,... | collective-permute-start | bytes 1032200 | tf_op jit(solution)/shard_map/ppermute | solution.py:368
  66.8 6.7 %copy-start = (bf16[192,896]{1,0:T(8,128)(2,1)S(1)}, bf16[192,896]{1,0:T(8,128)(2,1)}, u32[]{:S(2)}) copy-start(bf16[192,896]{1,0:T(8,128)(2,1)} %compact.8.refs_0_.refs_4_) | copy-start | bytes 1032196
  68.7 22.9 %copy-start.1 = (bf16[384,896]{1,0:T(8,128)(2,1)S(1)}, bf16[384,896]{1,0:T(8,128)(2,1)}, u32[]{:S(2)}) copy-start(bf16[384,896]{1,0:T(8,128)(2,1)} %tok_ref.3) | copy-start | bytes 2064388
  68.7 28.3 %copy-start.2 = (bf16[896,256]{1,0:T(8,128)(2,1)S(1)}, bf16[896,256]{1,0:T(8,128)(2,1)}, u32[]{:S(2)}) copy-start(bf16[896,256]{1,0:T(8,128)(2,1)} %w_ref.3) | copy-start | bytes 1376260
  68.8 1.0 copy-start.9
  69.7 1.0 copy-start.10
  73.5 23.5 %copy-start.3 = (bf16[192,896]{1,0:T(8,128)(2,1)}, bf16[192,896]{1,0:T(8,128)(2,1)S(1)}, u32[]{:S(2)}) copy-start(bf16[192,896]{1,0:T(8,128)(2,1)S(1)} %collective-permute-done.6.refs_1_.refs_5_) | copy-start | bytes 1032196
  73.5 23.5 %copy-start.4 = (bf16[192,896]{1,0:T(8,128)(2,1)}, bf16[192,896]{1,0:T(8,128)(2,1)S(1)}, u32[]{:S(2)}) copy-start(bf16[192,896]{1,0:T(8,128)(2,1)S(1)} %collective-permute-done.8.refs_3_.refs_7_) | copy-start | bytes 1032196
  73.5 23.5 %copy-start.5 = (bf16[192,896]{1,0:T(8,128)(2,1)}, bf16[192,896]{1,0:T(8,128)(2,1)S(1)}, u32[]{:S(2)}) copy-start(bf16[192,896]{1,0:T(8,128)(2,1)S(1)} %collective-permute-done.7.refs_2_.refs_6_) | copy-start | bytes 1032196
  93.4 14.6 %all-to-all-start.2 = ((bf16[16,16,896]{2,1,0:T(8,128)(2,1)}), bf16[16,16,896]{2,1,0:T(8,128)(2,1)S(1)}, u32[]{:S(2)}, u32[]{:S(2)}) async-start(bf16[16,16,896]{2,1,0:T(8,128)(2,1)} %bitcast.11), calls=%async_computation.2 | async-start | bytes 917504 | tf_op jit(solution)/shard_map/all_to_all | solution.py:454
